TPU v7x, 128 devices: a whole 4x4x4 slice. The times are simulated.
128 devices in a mesh: dp: 32 (over z, x, core), rep: 4 (over y).
Axes of the slice: x: 4, y: 4, z: 4, core: 2. Of those that a mesh axis runs over, the one named last changes fastest.
Arguments:
- token_inputs: bfloat16 [65536, 2048], P(('dp', 'rep')), may hold values from -12 to 12
- cotangent: bfloat16 [65536, 2048], P(('dp', 'rep')), may hold values from -24 to 24
- gate_preact: bfloat16 [65536, 768], P(('dp', 'rep')), may hold values from -6 to 6
- up_preact: bfloat16 [65536, 768], P(('dp', 'rep')), may hold values from -6 to 6
- down_weight: bfloat16 [2, 768, 2048], P(None, None, 'dp'), may hold values from -0.21875 to 0.21875
- block_expert: int32 [512], P(('dp', 'rep')), may hold values from 0 to 1
- block_count: int32 [512], P(('dp', 'rep')), may hold values from 1 to 128, as said below
Outputs:
- update: bfloat16 [2, 3, 768, 2048], P(None, None, None, 'dp')
Inputs may be any that keep to these rules, and one draw needn't show every extreme that they name: `block_count`: live rows of a block, at most 128; in every draw some block is full.
All inputs are finite; a program needn't handle non-finite values.
Results may differ from a plain program's by a relative error of at most 0.02.
Values may be sent and summed in bfloat16 or wider, within the bound.
No kernel may reach another device: no remote copies, remote signals or barrier semaphores. Data moves between devices by JAX's collectives and lax.ppermute only.
A program may use at most 128 MiB of HBM per device.

v0:
```python
import functools

import jax
import jax.numpy as jnp
from jax import lax
from jax.experimental import pallas as pl
from jax.experimental.pallas import tpu as pltpu
from jax.sharding import Mesh
from jax.sharding import PartitionSpec as P


DP = ("dp_0", "dp_1", "dp_2")
DP_REP = ("dp_0", "dp_1", "dp_2", "rep")

ns_first = 3.4445
ns_second = -4.775
ns_third = 2.0315
norm_eps = 1e-07

F = 768
D = 2048
BLOCK = 128
BLK = 4
HALF = D // 2
TILE = 512
RING = 4
CHUNK = F // RING
PIECE = CHUNK // RING
COLS = D // 16
SHIFTS = (1, 3, 2)
f32 = jnp.float32
bf16 = jnp.bfloat16


def shift(value, axis, by, sources=RING, targets=RING):
    pairs = [(i, (i + by) % RING) for i in range(sources)]
    return lax.ppermute(value, axis, [p for p in pairs if p[1] < targets])


def swap(value):
    return lax.ppermute(value, "dp_2", [(0, 1), (1, 0)])


def turn_kernel(info, own, other, first, second, rows):
    width = COLS // 2
    here = info[2]
    rows[pl.ds(pl.multiple_of(here * width, width), width), :] = own[here].astype(f32)
    rows[pl.ds(pl.multiple_of((1 - here) * width, width), width), :] = other[here].astype(f32)
    value = rows[...].T.astype(bf16)
    first[...] = value[: F // 2]
    second[...] = value[F // 2 :]


def finish_kernel(info, *rest):
    terms, outs = rest[:8], rest[8:]
    for s in range(RING):
        matrix = (info[3] + s) % RING
        at = jnp.minimum(matrix, 2)
        for half in range(2):
            value = terms[half * RING][at].astype(f32)
            for j in range(1, RING):
                value = value + terms[half * RING + j][at].astype(f32)
            outs[s][half] = jnp.where(matrix < 3, value, 0.0).astype(bf16)


def products(half, place, left, right_a, right_b, acc, outs):
    rows = BLK * BLOCK
    mats = left.shape[0] // F

    def tile(n, carry):
        to = pl.ds(pl.multiple_of(n * TILE, TILE), TILE)
        at = pl.ds(pl.multiple_of(half * HALF + n * TILE, TILE), TILE)
        for m in range(mats):
            one = pl.ds(m * F, F)
            acc[...] = jnp.dot(
                left[one, :rows], right_a[:, at], preferred_element_type=f32
            ) + jnp.dot(left[one, rows:], right_b[:, at], preferred_element_type=f32)
            for s in range(RING):
                chunk = (place + s) % RING
                value = acc[pl.ds(pl.multiple_of(chunk * CHUNK, CHUNK), CHUNK), :]
                outs[half * RING + s][m, :, to] = value.astype(bf16)
        return carry

    lax.fori_loop(0, HALF // TILE, tile, 0)


def hidden_kernel(info, count_a, expert_a, count_b, expert_b, gate_h, up_h, cot_h, *rest):
    gate_b, up_b, cot_b = rest[:3]
    outs, for_gate, for_up = rest[3:11], rest[11], rest[12]
    gate_a, up_a, cot_a, left, acc, sems = rest[13:]
    copies = [
        pltpu.make_async_copy(source, target, sems.at[i])
        for i, (source, target) in enumerate(((gate_h, gate_a), (up_h, up_a), (cot_h, cot_a)))
    ]
    for copy in copies:
        copy.start()

    def factors(gate_ref, up_ref, count, expert, base):
        def block(i, carry):
            rows = pl.ds(pl.multiple_of(i * BLOCK, BLOCK), BLOCK)
            gate = gate_ref[rows, :].astype(f32).T
            up = up_ref[rows, :].astype(f32).T
            limit = jnp.where(expert[i] == info[2], count[i], 0)
            live = lax.broadcasted_iota(jnp.int32, (F, BLOCK), 1) < limit
            sig = jax.nn.sigmoid(gate)
            to = pl.ds(pl.multiple_of(base + i * BLOCK, BLOCK), BLOCK)
            common = jnp.where(live, sig, 0.0)
            factor = common * gate
            left[:, to] = (factor * up).astype(bf16)
            for_up[:, to] = factor.astype(bf16)
            for_gate[:, to] = (common * up * (1.0 + gate * (1.0 - sig))).astype(bf16)
            return carry

        lax.fori_loop(0, BLK, block, 0)

    factors(gate_b, up_b, count_b, expert_b, BLK * BLOCK)
    copies[0].wait()
    copies[1].wait()
    factors(gate_a, up_a, count_a, expert_a, 0)
    copies[2].wait()
    for half in range(2):
        products(half, info[half], left, cot_a, cot_b, acc, outs)


def grads_kernel(info, cot_h, tok_h, for_gate, for_up, cot_b, tok_b, *rest):
    weights, outs, (cot_a, tok_a, whole, left, acc, sems) = rest[:8], rest[8:16], rest[16:]
    rows = BLK * BLOCK
    part = rows // 2
    halves = F // 2
    copies = [
        pltpu.make_async_copy(source, target, sems.at[i])
        for i, (source, target) in enumerate(((cot_h, cot_a), (tok_h, tok_a)))
    ]
    for copy in copies:
        copy.start()
    for half in range(2):
        for t in range(RING):
            for s in range(RING):
                near = (info[half] - s) % RING
                far = (info[1 - half] - t) % RING
                z, x = (near, far) if half == 0 else (far, near)
                at = pl.multiple_of((z * RING + x) * COLS, COLS)
                whole[half * halves : (half + 1) * halves, pl.ds(at, COLS)] = weights[
                    half * RING + t
                ][s]

    def backward(cot, base):
        def step(i, carry):
            here = pl.ds(pl.multiple_of(i * part, part), part)
            to = pl.ds(pl.multiple_of(base + i * part, part), part)
            back = lax.dot_general(
                whole[...], cot[here, :], (((1,), (1,)), ((), ())), preferred_element_type=f32
            )
            left[:F, to] = (back * for_gate[:, to].astype(f32)).astype(bf16)
            left[F:, to] = (back * for_up[:, to].astype(f32)).astype(bf16)
            return carry

        lax.fori_loop(0, rows // part, step, 0)

    backward(cot_b, rows)
    copies[0].wait()
    backward(cot_a, 0)
    copies[1].wait()
    for half in range(2):
        products(half, info[half], left, tok_a, tok_b, acc, outs)


def fold_kernel(half, info, *rest):
    grads, hidden, outs = rest[:4], rest[4:8], rest[8:]
    place = info[1 - half]

    def total(terms, at):
        value = terms[0][:, at, :].astype(f32)
        for term in terms[1:]:
            value = value + term[:, at, :].astype(f32)
        return value.astype(bf16)

    for s in range(RING):
        at = pl.ds(pl.multiple_of(((place + s) % RING) * PIECE, PIECE), PIECE)
        outs[s][:2] = total(grads, at)
        outs[s][2:] = total(hidden, at)


def settle_kernel(info, *rest):
    terms, outs = rest[:RING], rest[RING:]
    for half in range(2):
        value = terms[0][half].astype(f32)
        for term in terms[1:]:
            value = value + term[half].astype(f32)
        outs[half][...] = value.astype(bf16)


def pair_kernel(info, kept, arrived, out):
    out[info[2]] = kept[...]
    out[1 - info[2]] = arrived[...]


def spread_kernel(info, *rest):
    pieces, out = rest[:RING], rest[RING]
    for s in range(RING):
        matrix = (info[3] - s) % RING

        @pl.when(matrix < 3)
        def _(s=s, matrix=matrix):
            for expert in range(2):
                out[expert, matrix] = pieces[s][expert]


def sweep_kernel(info, *rest):
    parts, kept, sent, (whole, half_gram, half_poly, turned) = rest[:8], rest[8], rest[9], rest[10:]
    for half in range(2):
        for t in range(RING):
            for s in range(RING):
                near = (info[1 - half] - s) % RING
                far = (info[half] - t) % RING
                at = pl.multiple_of(far * CHUNK + near * PIECE, PIECE)
                whole[pl.ds(at, PIECE), half * HALF : (half + 1) * HALF] = parts[half * RING + t][s]
    both = (((1,), (1,)), ((), ()))
    raw = lax.dot_general(whole[...], whole[...], both, preferred_element_type=f32)
    diagonal = lax.broadcasted_iota(jnp.int32, (F, F), 0) == lax.broadcasted_iota(jnp.int32, (F, F), 1)
    norm = jnp.sqrt(jnp.sum(jnp.where(diagonal, raw, 0.0)))
    inverse = 1.0 / (norm + norm_eps)
    gram = raw * inverse * inverse

    def poly_of(gram):
        half_gram[...] = gram.astype(bf16)
        squared = jnp.dot(half_gram[...], half_gram[...], preferred_element_type=f32)
        return (ns_second * gram + ns_third * squared).astype(bf16)

    half_poly[...] = poly_of(gram)
    mixed = ns_first * gram + jnp.dot(half_poly[...], half_gram[...], preferred_element_type=f32)
    gram = ns_first * mixed + jnp.dot(mixed.astype(bf16), half_poly[...], preferred_element_type=f32)
    column = pl.multiple_of((info[0] * RING + info[1]) * COLS, COLS)
    mine = whole[:, pl.ds(column, COLS)]
    first = inverse * (
        ns_first * mine.astype(f32) + jnp.dot(half_poly[...], mine, preferred_element_type=f32)
    )
    first = first.astype(bf16)
    last = poly_of(gram)
    newer = ns_first * first.astype(f32) + jnp.dot(last, first, preferred_element_type=f32)
    turned[...] = (jnp.sqrt(jnp.float32(D)) * newer).T
    width = COLS // 2
    for ref, core in ((kept, info[2]), (sent, 1 - info[2])):
        ref[...] = turned[pl.ds(pl.multiple_of(core * width, width), width), :].astype(bf16)


def out_shapes(count):
    return [jax.ShapeDtypeStruct((count, CHUNK, HALF), bf16)] * 8


def call(kernel, flops, room, out_shape, scratch, scalars, operands, far=0):
    several = isinstance(out_shape, list)
    operands = [
        pltpu.with_memory_space_constraint(v, pltpu.HBM) if i < far else v
        for i, v in enumerate(operands)
    ]
    specs = [pl.BlockSpec(memory_space=pltpu.HBM)] * far
    specs += [pl.BlockSpec(memory_space=pltpu.VMEM)] * (len(operands) - far)
    out_spec = pl.BlockSpec(memory_space=pltpu.VMEM)
    return pl.pallas_call(
        kernel,
        in_specs=[pl.BlockSpec(memory_space=pltpu.SMEM)] * len(scalars) + specs,
        out_specs=[out_spec] * len(out_shape) if several else out_spec,
        out_shape=out_shape,
        scratch_shapes=scratch,
        compiler_params=pltpu.CompilerParams(vmem_limit_bytes=room * 1024 * 1024),
        cost_estimate=pl.CostEstimate(flops=flops, bytes_accessed=flops // 500, transcendentals=0),
    )(*scalars, *operands)


AXES = ("dp_0", "dp_1")


def gather_stage(values, flip):
    found = [[values[0]], [values[1]]]
    received = {}
    for s in SHIFTS:
        for half in range(2):
            axis = AXES[1 - half] if flip else AXES[half]
            received[half, s] = shift(values[half], axis, s)
    for half in range(2):
        found[half] += [received[half, s] for s in range(1, RING)]
    return found


def per_device(token_inputs, cotangent, gate, up, down_weight, block_expert, block_count):
    z, x, c, y = (lax.axis_index(a) for a in DP_REP)
    rows = BLK * BLOCK
    turned = jnp.swapaxes(down_weight, 1, 2)
    other = swap(turned)
    info = jnp.stack([z, x, c, y]).astype(jnp.int32)
    columns = call(
        turn_kernel,
        F * D,
        4,
        [jax.ShapeDtypeStruct((F // 2, COLS), bf16)] * 2,
        [pltpu.VMEM((COLS, F), f32)],
        [info],
        [turned, other],
    )
    count_b, expert_b = swap(block_count), swap(block_expert)
    columns, gate, up, cotangent, token_inputs, count_b, expert_b = lax.optimization_barrier(
        (columns, gate, up, cotangent, token_inputs, count_b, expert_b)
    )
    stage = gather_stage(columns, False)
    stacked = [jnp.stack(v) for v in stage]
    stage = gather_stage(stacked, True)
    weights = stage[0] + stage[1]

    gate_b, up_b = swap(gate), swap(up)
    cot_b, tok_b = swap(cotangent), swap(token_inputs)

    factor_shape = jax.ShapeDtypeStruct((F, 2 * rows), bf16)
    *hidden_out, for_gate, for_up = call(
        hidden_kernel,
        2 * F * 2 * rows * D,
        12,
        out_shapes(1) + [factor_shape] * 2,
        [
            pltpu.VMEM((rows, F), bf16),
            pltpu.VMEM((rows, F), bf16),
            pltpu.VMEM((rows, D), bf16),
            pltpu.VMEM((F, 2 * rows), bf16),
            pltpu.VMEM((F, TILE), f32),
            pltpu.SemaphoreType.DMA((3,)),
        ],
        [info, block_count, block_expert, count_b, expert_b],
        [gate, up, cotangent, gate_b, up_b, cot_b],
        3,
    )
    grads_out = call(
        grads_kernel,
        6 * F * 2 * rows * D,
        18,
        out_shapes(2),
        [
            pltpu.VMEM((rows, D), bf16),
            pltpu.VMEM((rows, D), bf16),
            pltpu.VMEM((F, D), bf16),
            pltpu.VMEM((2 * F, 2 * rows), bf16),
            pltpu.VMEM((F, TILE), f32),
            pltpu.SemaphoreType.DMA((2,)),
        ],
        [info],
        [cotangent, token_inputs, for_gate, for_up, cot_b, tok_b, *weights],
        2,
    )

    def exchanged(parts, axes):
        got = {}
        for s in SHIFTS:
            for half in range(2):
                got[half, s] = shift(parts[half][s], axes[half], s)
        return [[parts[half][0]] + [got[half, s] for s in SHIFTS] for half in range(2)]

    hidden_terms = exchanged([hidden_out[:RING], hidden_out[RING:]], AXES)
    grads_terms = exchanged([grads_out[:RING], grads_out[RING:]], AXES)

    def fold(half):
        return call(
            functools.partial(fold_kernel, half),
            F * HALF * RING,
            4,
            [jax.ShapeDtypeStruct((3, PIECE, HALF), bf16)] * 4,
            [],
            [info],
            [*grads_terms[half], *hidden_terms[half]],
        )

    second = [fold(half) for half in range(2)]
    final_terms = exchanged(second, AXES[::-1])
    blocks = (2, PIECE, HALF)
    parts = call(
        finish_kernel,
        F * D,
        4,
        [jax.ShapeDtypeStruct(blocks, bf16)] * RING,
        [],
        [info],
        [*final_terms[0], *final_terms[1]],
    )
    arrived = [shift(parts[s], "rep", s, targets=3) for s in SHIFTS]
    block = call(
        settle_kernel,
        F * D,
        4,
        [jax.ShapeDtypeStruct((PIECE, HALF), bf16)] * 2,
        [],
        [info],
        [parts[0], *arrived],
    )
    stage = gather_stage([block[0], block[1]], True)
    stage = gather_stage([jnp.stack(v) for v in stage], False)
    kept, sent = call(
        sweep_kernel,
        8 * F * F * F,
        26,
        [jax.ShapeDtypeStruct((COLS // 2, F), bf16)] * 2,
        [
            pltpu.VMEM((F, D), bf16),
            pltpu.VMEM((F, F), bf16),
            pltpu.VMEM((F, F), bf16),
            pltpu.VMEM((COLS, F), f32),
        ],
        [info],
        [*stage[0], *stage[1]],
    )
    narrow = (2, COLS // 2, F)
    pair = call(
        pair_kernel, F * COLS, 2, jax.ShapeDtypeStruct(narrow, bf16), [], [info], [kept, swap(sent)]
    )
    pieces = {0: pair, **{s: shift(pair, "rep", s, sources=3) for s in SHIFTS}}
    everyone = call(
        spread_kernel,
        F * COLS,
        4,
        jax.ShapeDtypeStruct((2, 3, COLS // 2, F), bf16),
        [],
        [info],
        [pieces[s] for s in range(RING)],
    )
    return jnp.swapaxes(everyone, 2, 3)


def solution(mesh):
    torus = Mesh(mesh.devices.reshape(4, 4, 2, mesh.shape["rep"]), DP_REP)

    return jax.shard_map(
        per_device,
        mesh=torus,
        in_specs=(
            P(DP_REP, None),
            P(DP_REP, None),
            P(DP_REP, None),
            P(DP_REP, None),
            P(None, None, DP),
            P(DP_REP),
            P(DP_REP),
        ),
        out_specs=P(None, None, None, DP),
        check_vma=False,
    )
```

profile of v0, /device:TPU:1, one launch (start us, length us, event | category | flops | bytes accessed | tf_op | source)
XLA Modules:
  0.0 280.7 jit_solution(1052084481926104245)
XLA Ops:
  0.0 1.4 collective-permute-start
  4.9 2.6 collective-permute-start.15
  9.1 3.8 %collective-permute-start.9 = (bf16[384,128]{1,0:T(8,128)(2,1)S(1)}, bf16[384,128]{1,0:T(8,128)(2,1)S(1)}, u32[]{:S(2)}, u32[]{:S(2)}) collective-permute-start(bf16[384,128]{1,0:T(8,128)(2,1)S(1)} %get-tuple-element.59), channel_id=1, source_target_pairs={{0,96},{32,0},{64,32},{96,64},{1,97},{33,1},{65,33},{97,65},{2,98}... | collective-permute-start | bytes 294920 | tf_op jit(solution)/shard_map/ppermute | solution.py:37
  12.9 2.7 collective-permute-done.13
  15.7 3.8 %collective-permute-start.18 = (bf16[4,384,128]{2,1,0:T(8,128)(2,1)S(1)}, bf16[4,384,128]{2,1,0:T(8,128)(2,1)S(1)}, u32[]{:S(2)}, u32[]{:S(2)}) collective-permute-start(bf16[4,384,128]{2,1,0:T(8,128)(2,1)S(1)} %pad_maximum_fusion.1.rest_4_), channel_id=1, source_target_pairs={{0,96},{32,0},{64,32},{96,64},{1,97},{33,1},{65,33},{97,65},{2,98}... | collective-permute-start | bytes 1179656 | tf_op jit(solution)/shard_map/ppermute | solution.py:37
  20.2 4.4 %collective-permute-done.8 = bf16[384,128]{1,0:T(8,128)(2,1)S(1)} collective-permute-done((bf16[384,128]{1,0:T(8,128)(2,1)S(1)}, bf16[384,128]{1,0:T(8,128)(2,1)S(1)}, u32[]{:S(2)}, u32[]{:S(2)}) %collective-permute-start.8) | collective-permute-done | bytes 98336 | tf_op jit(solution)/shard_map/ppermute | solution.py:37
  24.6 2.7 collective-permute-start.3
  28.0 1.2 collective-permute-done.18.rest_7_
  29.3 10.4 %collective-permute-done.17.rest_6_ = bf16[4,384,128]{2,1,0:T(8,128)(2,1)S(1)} collective-permute-done((bf16[4,384,128]{2,1,0:T(8,128)(2,1)S(1)}, bf16[4,384,128]{2,1,0:T(8,128)(2,1)S(1)}, u32[]{:S(2)}, u32[]{:S(2)}) %collective-permute-start.17) | collective-permute-done | bytes 393248 | tf_op jit(solution)/shard_map/ppermute | solution.py:37
  39.7 4.5 %collective-permute-start.16 = (bf16[4,384,128]{2,1,0:T(8,128)(2,1)S(1)}, bf16[4,384,128]{2,1,0:T(8,128)(2,1)S(1)}, u32[]{:S(2)}, u32[]{:S(2)}) collective-permute-start(bf16[4,384,128]{2,1,0:T(8,128)(2,1)S(1)} %pad_maximum_fusion.1.rest_4_), channel_id=1, source_target_pairs={{0,32},{32,64},{64,96},{96,0},{1,33},{33,65},{65,97},{97,1},{2,34}... | collective-permute-start | bytes 1179656 | tf_op jit(solution)/shard_map/ppermute | solution.py:37
  44.3 1.2 collective-permute-start.12
  47.5 7.4 %shard_map.74 = (bf16[1,192,1024]{2,1,0:T(8,128)(2,1)S(1)}, bf16[1,192,1024]{2,1,0:T(8,128)(2,1)S(1)}, bf16[1,192,1024]{2,1,0:T(8,128)(2,1)S(1)}, bf16[1,192,102...) custom-call(s32[4]{0:T(128)S(1)} %pad_add_fusion.info, ...), custom_call_target="tpu_custom_call" | custom-call | flops 3221225472 | bytes 6442450 | tf_op jit(solution)/shard_map/pallas_call | solution.py:260
  55.0 2.7 collective-permute-start.23
  57.7 8.4 %collective-permute-done.10.rest_1_ = bf16[4,384,128]{2,1,0:T(8,128)(2,1)S(1)} collective-permute-done((bf16[4,384,128]{2,1,0:T(8,128)(2,1)S(1)}, bf16[4,384,128]{2,1,0:T(8,128)(2,1)S(1)}, u32[]{:S(2)}, u32[]{:S(2)}) %collective-permute-start.10) | collective-permute-done | bytes 393248 | tf_op jit(solution)/shard_map/ppermute | solution.py:37
  66.1 13.5 %shard_map.75 = (bf16[2,192,1024]{2,1,0:T(8,128)(2,1)S(1)}, bf16[2,192,1024]{2,1,0:T(8,128)(2,1)S(1)}, bf16[2,192,1024]{2,1,0:T(8,128)(2,1)S(1)}, bf16[2,192,102...) custom-call(s32[4]{0:T(128)S(1)} %pad_add_fusion.info, ...), custom_call_target="tpu_custom_call" | custom-call | flops 9663676416 | bytes 19327352 | tf_op jit(solution)/shard_map/pallas_call | solution.py:260
  79.6 2.7 collective-permute-start.20
  83.4 1.9 collective-permute-start.24
  85.3 38.9 %collective-permute-done.24.rest_7_ = bf16[1,192,1024]{2,1,0:T(8,128)(2,1)S(1)} collective-permute-done((bf16[1,192,1024]{2,1,0:T(8,128)(2,1)S(1)}, bf16[1,192,1024]{2,1,0:T(8,128)(2,1)S(1)}, u32[]{:S(2)}, u32[]{:S(2)}) %collective-permute-start.24) | collective-permute-done | bytes 393248 | tf_op jit(solution)/shard_map/ppermute | solution.py:37
  124.2 2.7 collective-permute-start.29
  128.0 1.9 collective-permute-start.33
  131.0 36.7 %collective-permute-done.32.rest_6_ = bf16[1,192,1024]{2,1,0:T(8,128)(2,1)S(1)} collective-permute-done((bf16[1,192,1024]{2,1,0:T(8,128)(2,1)S(1)}, bf16[1,192,1024]{2,1,0:T(8,128)(2,1)S(1)}, u32[]{:S(2)}, u32[]{:S(2)}) %collective-permute-start.32) | collective-permute-done | bytes 393248 | tf_op jit(solution)/shard_map/ppermute | solution.py:37
  167.8 10.0 %collective-permute-start.26 = (bf16[3,48,1024]{2,1,0:T(8,128)(2,1)S(1)}, bf16[3,48,1024]{2,1,0:T(8,128)(2,1)S(1)}, u32[]{:S(2)}, u32[]{:S(2)}) collective-permute-start(bf16[3,48,1024]{2,1,0:T(8,128)(2,1)S(1)} %get-tuple-element.71), channel_id=1, source_target_pairs={{0,24},{8,0},{16,8},{24,16},{1,25},{9,1},{17,9},{25,17},{2,26},{10... | collective-permute-start | bytes 884744 | tf_op jit(solution)/shard_map/ppermute | solution.py:37
  180.7 2.1 collective-permute-start.35
  183.4 2.3 collective-permute-done.27.rest_3_
  185.8 1.5 collective-permute-done.34.rest_5_
  187.2 2.8 collective-permute-done.35.rest_6_
  190.0 1.9 collective-permute-done.36.rest_7_
  193.0 3.2 %collective-permute-start.37 = (bf16[2,48,1024]{2,1,0:T(8,128)(2,1)S(1)}, bf16[2,48,1024]{2,1,0:T(8,128)(2,1)S(1)}, u32[]{:S(2)}, u32[]{:S(2)}) collective-permute-start(bf16[2,48,1024]{2,1,0:T(8,128)(2,1)S(1)} %get-tuple-element.86), channel_id=1, source_target_pairs={{0,1},{1,2},{3,0},{4,5},{5,6},{7,4},{8,9},{9,10},{11,8},{12,13},{1... | collective-permute-start | bytes 589832 | tf_op jit(solution)/shard_map/ppermute | solution.py:37
  196.2 1.5 collective-permute-start.38
  197.7 5.6 %collective-permute-start.39 = (bf16[2,48,1024]{2,1,0:T(8,128)(2,1)S(1)}, bf16[2,48,1024]{2,1,0:T(8,128)(2,1)S(1)}, u32[]{:S(2)}, u32[]{:S(2)}) collective-permute-start(bf16[2,48,1024]{2,1,0:T(8,128)(2,1)S(1)} %get-tuple-element.88), channel_id=1, source_target_pairs={{0,2},{2,0},{3,1},{4,6},{6,4},{7,5},{8,10},{10,8},{11,9},{12,14},{... | collective-permute-start | bytes 589832 | tf_op jit(solution)/shard_map/ppermute | solution.py:37
  203.3 3.7 %collective-permute-done.39.rest_3_ = bf16[2,48,1024]{2,1,0:T(8,128)(2,1)S(1)} collective-permute-done((bf16[2,48,1024]{2,1,0:T(8,128)(2,1)S(1)}, bf16[2,48,1024]{2,1,0:T(8,128)(2,1)S(1)}, u32[]{:S(2)}, u32[]{:S(2)}) %collective-permute-start.39) | collective-permute-done | bytes 196640 | tf_op jit(solution)/shard_map/ppermute | solution.py:37
  207.7 2.2 collective-permute-start.48
  210.5 1.9 collective-permute-done.48
  212.5 2.4 collective-permute-done.47
  216.6 1.5 collective-permute-start.42
  219.3 2.4 collective-permute-start.50
  221.7 2.0 collective-permute-done.42
  225.8 2.6 collective-permute-done.50.rest_6_
  228.4 6.6 %collective-permute-done.49.rest_5_ = bf16[4,48,1024]{2,1,0:T(8,128)(2,1)S(1)} collective-permute-done((bf16[4,48,1024]{2,1,0:T(8,128)(2,1)S(1)}, bf16[4,48,1024]{2,1,0:T(8,128)(2,1)S(1)}, u32[]{:S(2)}, u32[]{:S(2)}) %collective-permute-start.49) | collective-permute-done | bytes 393248 | tf_op jit(solution)/shard_map/ppermute | solution.py:37
  235.0 2.2 collective-permute-done.43.rest_1_
  237.2 9.8 %shard_map.80 = (bf16[64,768]{1,0:T(8,128)(2,1)S(1)}, bf16[64,768]{1,0:T(8,128)(2,1)S(1)}) custom-call(s32[4]{0:T(128)S(1)} %pad_add_fusion.info, bf16[4,48,1024]{2,1,0:T(8,128)(2,1)S(1)} %pad_maximum_fusion.2.rest_0_, bf16[4,48,1024]{2,1,0:T(8,128)(2,1)S(1)} %collective-permute-done.43.rest_1_, bf16[4,48,1024]{2,1,0:T(8,128)(2,1)S(1)} %collective-permute-done.44.rest_2_, ...), custom_call_target="tpu_custom_call" | custom-call | flops 3623878656 | bytes 7247757 | tf_op jit(solution)/shard_map/pallas_call | solution.py:260
  247.0 13.5 %collective-permute-start.52 = (bf16[64,768]{1,0:T(8,128)(2,1)S(1)}, bf16[64,768]{1,0:T(8,128)(2,1)S(1)}, u32[]{:S(2)}, u32[]{:S(2)}) collective-permute-start(bf16[64,768]{1,0:T(8,128)(2,1)S(1)} %get-tuple-element.92), channel_id=1, source_target_pairs={{0,4},{4,0},{1,5},{5,1},{2,6},{6,2},{3,7},{7,3},{8,12},{12,8},{9,1... | collective-permute-start | bytes 294920 | tf_op jit(solution)/shard_map/ppermute | solution.py:41
  262.0 4.7 %collective-permute-start.55 = (bf16[2,64,768]{2,1,0:T(8,128)(2,1)S(1)}, bf16[2,64,768]{2,1,0:T(8,128)(2,1)S(1)}, u32[]{:S(2)}, u32[]{:S(2)}) collective-permute-start(bf16[2,64,768]{2,1,0:T(8,128)(2,1)S(1)} %shard_map.81.rest_0_), channel_id=1, source_target_pairs={{0,3},{1,0},{2,1},{4,7},{5,4},{6,5},{8,11},{9,8},{10,9},{12,15},{1... | collective-permute-start | bytes 589832 | tf_op jit(solution)/shard_map/ppermute | solution.py:37
  266.6 4.7 %collective-permute-start.54 = (bf16[2,64,768]{2,1,0:T(8,128)(2,1)S(1)}, bf16[2,64,768]{2,1,0:T(8,128)(2,1)S(1)}, u32[]{:S(2)}, u32[]{:S(2)}) collective-permute-start(bf16[2,64,768]{2,1,0:T(8,128)(2,1)S(1)} %shard_map.81.rest_0_), channel_id=1, source_target_pairs={{0,2},{1,3},{2,0},{4,6},{5,7},{6,4},{8,10},{9,11},{10,8},{12,14},{... | collective-permute-start | bytes 589832 | tf_op jit(solution)/shard_map/ppermute | solution.py:37
  271.4 1.3 collective-permute-start.53
  272.7 3.2 %collective-permute-done.54.rest_2_ = bf16[2,64,768]{2,1,0:T(8,128)(2,1)S(1)} collective-permute-done((bf16[2,64,768]{2,1,0:T(8,128)(2,1)S(1)}, bf16[2,64,768]{2,1,0:T(8,128)(2,1)S(1)}, u32[]{:S(2)}, u32[]{:S(2)}) %collective-permute-start.54) | collective-permute-done | bytes 196640 | tf_op jit(solution)/shard_map/ppermute | solution.py:37
  275.9 3.4 %collective-permute-done.53.rest_1_ = bf16[2,64,768]{2,1,0:T(8,128)(2,1)S(1)} collective-permute-done((bf16[2,64,768]{2,1,0:T(8,128)(2,1)S(1)}, bf16[2,64,768]{2,1,0:T(8,128)(2,1)S(1)}, u32[]{:S(2)}, u32[]{:S(2)}) %collective-permute-start.53) | collective-permute-done | bytes 196640 | tf_op jit(solution)/shard_map/ppermute | solution.py:37
  279.2 1.4 shard_map.82
  (85 shorter events, 24.5 us)
Async XLA Ops:
  4.3 41.2 %collective-permute-start.5 = (bf16[512,2048]{1,0:T(8,128)(2,1)}, bf16[512,2048]{1,0:T(8,128)(2,1)S(1)}, u32[]{:S(2)}, u32[]{:S(2)}) collective-permute-start(bf16[512,2048]{1,0:T(8,128)(2,1)} %cot_h.1), channel_id=1, source_target_pairs={{0,4},{4,0},{1,5},{5,1},{2,6},{6,2},{3,7},{7,3},{8,12},{12,8},{9,1... | collective-permute-start | bytes 6291464 | tf_op jit(solution)/shard_map/ppermute | solution.py:41
  4.8 61.3 %collective-permute-start.6 = (bf16[512,2048]{1,0:T(8,128)(2,1)}, bf16[512,2048]{1,0:T(8,128)(2,1)S(1)}, u32[]{:S(2)}, u32[]{:S(2)}) collective-permute-start(bf16[512,2048]{1,0:T(8,128)(2,1)} %tok_h), channel_id=1, source_target_pairs={{0,4},{4,0},{1,5},{5,1},{2,6},{6,2},{3,7},{7,3},{8,12},{12,8},{9,1... | collective-permute-start | bytes 6291464 | tf_op jit(solution)/shard_map/ppermute | solution.py:41
  7.5 5.4 %collective-permute-start.14 = (bf16[384,128]{1,0:T(8,128)(2,1)S(1)}, bf16[384,128]{1,0:T(8,128)(2,1)S(1)}, u32[]{:S(2)}, u32[]{:S(2)}) collective-permute-start(bf16[384,128]{1,0:T(8,128)(2,1)S(1)} %get-tuple-element.60), channel_id=1, source_target_pairs={{0,16},{8,24},{16,0},{24,8},{1,17},{9,25},{17,1},{25,9},{2,18},{10... | collective-permute-start | bytes 294920 | tf_op jit(solution)/shard_map/ppermute | solution.py:37
  8.0 7.6 %collective-permute-start.13 = (bf16[384,128]{1,0:T(8,128)(2,1)S(1)}, bf16[384,128]{1,0:T(8,128)(2,1)S(1)}, u32[]{:S(2)}, u32[]{:S(2)}) collective-permute-start(bf16[384,128]{1,0:T(8,128)(2,1)S(1)} %get-tuple-element.60), channel_id=1, source_target_pairs={{0,8},{8,16},{16,24},{24,0},{1,9},{9,17},{17,25},{25,1},{2,10},{10... | collective-permute-start | bytes 294920 | tf_op jit(solution)/shard_map/ppermute | solution.py:37
  9.1 10.4 %collective-permute-start.9 = (bf16[384,128]{1,0:T(8,128)(2,1)S(1)}, bf16[384,128]{1,0:T(8,128)(2,1)S(1)}, u32[]{:S(2)}, u32[]{:S(2)}) collective-permute-start(bf16[384,128]{1,0:T(8,128)(2,1)S(1)} %get-tuple-element.59), channel_id=1, source_target_pairs={{0,96},{32,0},{64,32},{96,64},{1,97},{33,1},{65,33},{97,65},{2,98}... | collective-permute-start | bytes 294920 | tf_op jit(solution)/shard_map/ppermute | solution.py:37
  15.7 13.6 %collective-permute-start.18 = (bf16[4,384,128]{2,1,0:T(8,128)(2,1)S(1)}, bf16[4,384,128]{2,1,0:T(8,128)(2,1)S(1)}, u32[]{:S(2)}, u32[]{:S(2)}) collective-permute-start(bf16[4,384,128]{2,1,0:T(8,128)(2,1)S(1)} %pad_maximum_fusion.1.rest_4_), channel_id=1, source_target_pairs={{0,96},{32,0},{64,32},{96,64},{1,97},{33,1},{65,33},{97,65},{2,98}... | collective-permute-start | bytes 1179656 | tf_op jit(solution)/shard_map/ppermute | solution.py:37
  19.5 7.8 %collective-permute-start.7 = (bf16[384,128]{1,0:T(8,128)(2,1)S(1)}, bf16[384,128]{1,0:T(8,128)(2,1)S(1)}, u32[]{:S(2)}, u32[]{:S(2)}) collective-permute-start(bf16[384,128]{1,0:T(8,128)(2,1)S(1)} %get-tuple-element.59), channel_id=1, source_target_pairs={{0,32},{32,64},{64,96},{96,0},{1,33},{33,65},{65,97},{97,1},{2,34}... | collective-permute-start | bytes 294920 | tf_op jit(solution)/shard_map/ppermute | solution.py:37
  24.6 19.7 %collective-permute-start.3 = (bf16[512,768]{1,0:T(8,128)(2,1)}, bf16[512,768]{1,0:T(8,128)(2,1)S(1)}, u32[]{:S(2)}, u32[]{:S(2)}) collective-permute-start(bf16[512,768]{1,0:T(8,128)(2,1)} %gate_h), channel_id=1, source_target_pairs={{0,4},{4,0},{1,5},{5,1},{2,6},{6,2},{3,7},{7,3},{8,12},{12,8},{9,1... | collective-permute-start | bytes 2359304 | tf_op jit(solution)/shard_map/ppermute | solution.py:41
  27.3 18.2 %collective-permute-start.4 = (bf16[512,768]{1,0:T(8,128)(2,1)}, bf16[512,768]{1,0:T(8,128)(2,1)S(1)}, u32[]{:S(2)}, u32[]{:S(2)}) collective-permute-start(bf16[512,768]{1,0:T(8,128)(2,1)} %up_h), channel_id=1, source_target_pairs={{0,4},{4,0},{1,5},{5,1},{2,6},{6,2},{3,7},{7,3},{8,12},{12,8},{9,1... | collective-permute-start | bytes 2359304 | tf_op jit(solution)/shard_map/ppermute | solution.py:41
  29.2 10.5 %collective-permute-start.17 = (bf16[4,384,128]{2,1,0:T(8,128)(2,1)S(1)}, bf16[4,384,128]{2,1,0:T(8,128)(2,1)S(1)}, u32[]{:S(2)}, u32[]{:S(2)}) collective-permute-start(bf16[4,384,128]{2,1,0:T(8,128)(2,1)S(1)} %pad_maximum_fusion.1.rest_4_), channel_id=1, source_target_pairs={{0,64},{32,96},{64,0},{96,32},{1,65},{33,97},{65,1},{97,33},{2,66}... | collective-permute-start | bytes 1179656 | tf_op jit(solution)/shard_map/ppermute | solution.py:37
  39.7 15.2 %collective-permute-start.16 = (bf16[4,384,128]{2,1,0:T(8,128)(2,1)S(1)}, bf16[4,384,128]{2,1,0:T(8,128)(2,1)S(1)}, u32[]{:S(2)}, u32[]{:S(2)}) collective-permute-start(bf16[4,384,128]{2,1,0:T(8,128)(2,1)S(1)} %pad_maximum_fusion.1.rest_4_), channel_id=1, source_target_pairs={{0,32},{32,64},{64,96},{96,0},{1,33},{33,65},{65,97},{97,1},{2,34}... | collective-permute-start | bytes 1179656 | tf_op jit(solution)/shard_map/ppermute | solution.py:37
  44.3 10.7 %collective-permute-start.12 = (bf16[4,384,128]{2,1,0:T(8,128)(2,1)S(1)}, bf16[4,384,128]{2,1,0:T(8,128)(2,1)S(1)}, u32[]{:S(2)}, u32[]{:S(2)}) collective-permute-start(bf16[4,384,128]{2,1,0:T(8,128)(2,1)S(1)} %pad_maximum_fusion.rest_0_), channel_id=1, source_target_pairs={{0,24},{8,0},{16,8},{24,16},{1,25},{9,1},{17,9},{25,17},{2,26},{10... | collective-permute-start | bytes 1179656 | tf_op jit(solution)/shard_map/ppermute | solution.py:37
  45.5 12.2 %collective-permute-start.11 = (bf16[4,384,128]{2,1,0:T(8,128)(2,1)S(1)}, bf16[4,384,128]{2,1,0:T(8,128)(2,1)S(1)}, u32[]{:S(2)}, u32[]{:S(2)}) collective-permute-start(bf16[4,384,128]{2,1,0:T(8,128)(2,1)S(1)} %pad_maximum_fusion.rest_0_), channel_id=1, source_target_pairs={{0,16},{8,24},{16,0},{24,8},{1,17},{9,25},{17,1},{25,9},{2,18},{10... | collective-permute-start | bytes 1179656 | tf_op jit(solution)/shard_map/ppermute | solution.py:37
  45.5 20.5 %collective-permute-start.10 = (bf16[4,384,128]{2,1,0:T(8,128)(2,1)S(1)}, bf16[4,384,128]{2,1,0:T(8,128)(2,1)S(1)}, u32[]{:S(2)}, u32[]{:S(2)}) collective-permute-start(bf16[4,384,128]{2,1,0:T(8,128)(2,1)S(1)} %pad_maximum_fusion.rest_0_), channel_id=1, source_target_pairs={{0,8},{8,16},{16,24},{24,0},{1,9},{9,17},{17,25},{25,1},{2,10},{10... | collective-permute-start | bytes 1179656 | tf_op jit(solution)/shard_map/ppermute | solution.py:37
  54.9 28.4 %collective-permute-start.22 = (bf16[1,192,1024]{2,1,0:T(8,128)(2,1)S(1)}, bf16[1,192,1024]{2,1,0:T(8,128)(2,1)S(1)}, u32[]{:S(2)}, u32[]{:S(2)}) collective-permute-start(bf16[1,192,1024]{2,1,0:T(8,128)(2,1)S(1)} %get-tuple-element.66), channel_id=1, source_target_pairs={{0,32},{32,64},{64,96},{96,0},{1,33},{33,65},{65,97},{97,1},{2,34}... | collective-permute-start | bytes 1179656 | tf_op jit(solution)/shard_map/ppermute | solution.py:37
  55.0 30.2 %collective-permute-start.23 = (bf16[1,192,1024]{2,1,0:T(8,128)(2,1)S(1)}, bf16[1,192,1024]{2,1,0:T(8,128)(2,1)S(1)}, u32[]{:S(2)}, u32[]{:S(2)}) collective-permute-start(bf16[1,192,1024]{2,1,0:T(8,128)(2,1)S(1)} %get-tuple-element.67), channel_id=1, source_target_pairs={{0,96},{32,0},{64,32},{96,64},{1,97},{33,1},{65,33},{97,65},{2,98}... | collective-permute-start | bytes 1179656 | tf_op jit(solution)/shard_map/ppermute | solution.py:37
  79.5 47.3 %collective-permute-start.19 = (bf16[2,192,1024]{2,1,0:T(8,128)(2,1)S(1)}, bf16[2,192,1024]{2,1,0:T(8,128)(2,1)S(1)}, u32[]{:S(2)}, u32[]{:S(2)}) collective-permute-start(bf16[2,192,1024]{2,1,0:T(8,128)(2,1)S(1)} %get-tuple-element.62), channel_id=1, source_target_pairs={{0,32},{32,64},{64,96},{96,0},{1,33},{33,65},{65,97},{97,1},{2,34}... | collective-permute-start | bytes 2359304 | tf_op jit(solution)/shard_map/ppermute | solution.py:37
  79.6 47.2 %collective-permute-start.20 = (bf16[2,192,1024]{2,1,0:T(8,128)(2,1)S(1)}, bf16[2,192,1024]{2,1,0:T(8,128)(2,1)S(1)}, u32[]{:S(2)}, u32[]{:S(2)}) collective-permute-start(bf16[2,192,1024]{2,1,0:T(8,128)(2,1)S(1)} %get-tuple-element.63), channel_id=1, source_target_pairs={{0,96},{32,0},{64,32},{96,64},{1,97},{33,1},{65,33},{97,65},{2,98}... | collective-permute-start | bytes 2359304 | tf_op jit(solution)/shard_map/ppermute | solution.py:37
  82.3 45.7 %collective-permute-start.21 = (bf16[2,192,1024]{2,1,0:T(8,128)(2,1)S(1)}, bf16[2,192,1024]{2,1,0:T(8,128)(2,1)S(1)}, u32[]{:S(2)}, u32[]{:S(2)}) collective-permute-start(bf16[2,192,1024]{2,1,0:T(8,128)(2,1)S(1)} %get-tuple-element.64), channel_id=1, source_target_pairs={{0,64},{32,96},{64,0},{96,32},{1,65},{33,97},{65,1},{97,33},{2,66}... | collective-permute-start | bytes 2359304 | tf_op jit(solution)/shard_map/ppermute | solution.py:37
  83.4 40.8 %collective-permute-start.24 = (bf16[1,192,1024]{2,1,0:T(8,128)(2,1)S(1)}, bf16[1,192,1024]{2,1,0:T(8,128)(2,1)S(1)}, u32[]{:S(2)}, u32[]{:S(2)}) collective-permute-start(bf16[1,192,1024]{2,1,0:T(8,128)(2,1)S(1)} %get-tuple-element.68), channel_id=1, source_target_pairs={{0,64},{32,96},{64,0},{96,32},{1,65},{33,97},{65,1},{97,33},{2,66}... | collective-permute-start | bytes 1179656 | tf_op jit(solution)/shard_map/ppermute | solution.py:37
  85.3 38.9 %collective-permute-start.31 = (bf16[1,192,1024]{2,1,0:T(8,128)(2,1)S(1)}, bf16[1,192,1024]{2,1,0:T(8,128)(2,1)S(1)}, u32[]{:S(2)}, u32[]{:S(2)}) collective-permute-start(bf16[1,192,1024]{2,1,0:T(8,128)(2,1)S(1)} %get-tuple-element.78), channel_id=1, source_target_pairs={{0,8},{8,16},{16,24},{24,0},{1,9},{9,17},{17,25},{25,1},{2,10},{10... | collective-permute-start | bytes 1179656 | tf_op jit(solution)/shard_map/ppermute | solution.py:37
  124.1 53.7 %collective-permute-start.28 = (bf16[2,192,1024]{2,1,0:T(8,128)(2,1)S(1)}, bf16[2,192,1024]{2,1,0:T(8,128)(2,1)S(1)}, u32[]{:S(2)}, u32[]{:S(2)}) collective-permute-start(bf16[2,192,1024]{2,1,0:T(8,128)(2,1)S(1)} %get-tuple-element.74), channel_id=1, source_target_pairs={{0,8},{8,16},{16,24},{24,0},{1,9},{9,17},{17,25},{25,1},{2,10},{10... | collective-permute-start | bytes 2359304 | tf_op jit(solution)/shard_map/ppermute | solution.py:37
  124.2 54.8 %collective-permute-start.29 = (bf16[2,192,1024]{2,1,0:T(8,128)(2,1)S(1)}, bf16[2,192,1024]{2,1,0:T(8,128)(2,1)S(1)}, u32[]{:S(2)}, u32[]{:S(2)}) collective-permute-start(bf16[2,192,1024]{2,1,0:T(8,128)(2,1)S(1)} %get-tuple-element.75), channel_id=1, source_target_pairs={{0,24},{8,0},{16,8},{24,16},{1,25},{9,1},{17,9},{25,17},{2,26},{10... | collective-permute-start | bytes 2359304 | tf_op jit(solution)/shard_map/ppermute | solution.py:37
  126.8 52.1 %collective-permute-start.30 = (bf16[2,192,1024]{2,1,0:T(8,128)(2,1)S(1)}, bf16[2,192,1024]{2,1,0:T(8,128)(2,1)S(1)}, u32[]{:S(2)}, u32[]{:S(2)}) collective-permute-start(bf16[2,192,1024]{2,1,0:T(8,128)(2,1)S(1)} %get-tuple-element.76), channel_id=1, source_target_pairs={{0,16},{8,24},{16,0},{24,8},{1,17},{9,25},{17,1},{25,9},{2,18},{10... | collective-permute-start | bytes 2359304 | tf_op jit(solution)/shard_map/ppermute | solution.py:37
  126.8 40.9 %collective-permute-start.32 = (bf16[1,192,1024]{2,1,0:T(8,128)(2,1)S(1)}, bf16[1,192,1024]{2,1,0:T(8,128)(2,1)S(1)}, u32[]{:S(2)}, u32[]{:S(2)}) collective-permute-start(bf16[1,192,1024]{2,1,0:T(8,128)(2,1)S(1)} %get-tuple-element.79), channel_id=1, source_target_pairs={{0,24},{8,0},{16,8},{24,16},{1,25},{9,1},{17,9},{25,17},{2,26},{10... | collective-permute-start | bytes 1179656 | tf_op jit(solution)/shard_map/ppermute | solution.py:37
  128.0 39.7 %collective-permute-start.33 = (bf16[1,192,1024]{2,1,0:T(8,128)(2,1)S(1)}, bf16[1,192,1024]{2,1,0:T(8,128)(2,1)S(1)}, u32[]{:S(2)}, u32[]{:S(2)}) collective-permute-start(bf16[1,192,1024]{2,1,0:T(8,128)(2,1)S(1)} %get-tuple-element.80), channel_id=1, source_target_pairs={{0,16},{8,24},{16,0},{24,8},{1,17},{9,25},{17,1},{25,9},{2,18},{10... | collective-permute-start | bytes 1179656 | tf_op jit(solution)/shard_map/ppermute | solution.py:37
  167.8 15.1 %collective-permute-start.25 = (bf16[3,48,1024]{2,1,0:T(8,128)(2,1)S(1)}, bf16[3,48,1024]{2,1,0:T(8,128)(2,1)S(1)}, u32[]{:S(2)}, u32[]{:S(2)}) collective-permute-start(bf16[3,48,1024]{2,1,0:T(8,128)(2,1)S(1)} %get-tuple-element.70), channel_id=1, source_target_pairs={{0,8},{8,16},{16,24},{24,0},{1,9},{9,17},{17,25},{25,1},{2,10},{10... | collective-permute-start | bytes 884744 | tf_op jit(solution)/shard_map/ppermute | solution.py:37
  167.8 15.7 %collective-permute-start.26 = (bf16[3,48,1024]{2,1,0:T(8,128)(2,1)S(1)}, bf16[3,48,1024]{2,1,0:T(8,128)(2,1)S(1)}, u32[]{:S(2)}, u32[]{:S(2)}) collective-permute-start(bf16[3,48,1024]{2,1,0:T(8,128)(2,1)S(1)} %get-tuple-element.71), channel_id=1, source_target_pairs={{0,24},{8,0},{16,8},{24,16},{1,25},{9,1},{17,9},{25,17},{2,26},{10... | collective-permute-start | bytes 884744 | tf_op jit(solution)/shard_map/ppermute | solution.py:37
  177.8 8.0 %collective-permute-start.27 = (bf16[3,48,1024]{2,1,0:T(8,128)(2,1)S(1)}, bf16[3,48,1024]{2,1,0:T(8,128)(2,1)S(1)}, u32[]{:S(2)}, u32[]{:S(2)}) collective-permute-start(bf16[3,48,1024]{2,1,0:T(8,128)(2,1)S(1)} %get-tuple-element.72), channel_id=1, source_target_pairs={{0,16},{8,24},{16,0},{24,8},{1,17},{9,25},{17,1},{25,9},{2,18},{10... | collective-permute-start | bytes 884744 | tf_op jit(solution)/shard_map/ppermute | solution.py:37
  180.1 7.1 %collective-permute-start.34 = (bf16[3,48,1024]{2,1,0:T(8,128)(2,1)S(1)}, bf16[3,48,1024]{2,1,0:T(8,128)(2,1)S(1)}, u32[]{:S(2)}, u32[]{:S(2)}) collective-permute-start(bf16[3,48,1024]{2,1,0:T(8,128)(2,1)S(1)} %get-tuple-element.82), channel_id=1, source_target_pairs={{0,32},{32,64},{64,96},{96,0},{1,33},{33,65},{65,97},{97,1},{2,34}... | collective-permute-start | bytes 884744 | tf_op jit(solution)/shard_map/ppermute | solution.py:37
  180.7 9.3 %collective-permute-start.35 = (bf16[3,48,1024]{2,1,0:T(8,128)(2,1)S(1)}, bf16[3,48,1024]{2,1,0:T(8,128)(2,1)S(1)}, u32[]{:S(2)}, u32[]{:S(2)}) collective-permute-start(bf16[3,48,1024]{2,1,0:T(8,128)(2,1)S(1)} %get-tuple-element.83), channel_id=1, source_target_pairs={{0,96},{32,0},{64,32},{96,64},{1,97},{33,1},{65,33},{97,65},{2,98}... | collective-permute-start | bytes 884744 | tf_op jit(solution)/shard_map/ppermute | solution.py:37
  182.8 9.1 %collective-permute-start.36 = (bf16[3,48,1024]{2,1,0:T(8,128)(2,1)S(1)}, bf16[3,48,1024]{2,1,0:T(8,128)(2,1)S(1)}, u32[]{:S(2)}, u32[]{:S(2)}) collective-permute-start(bf16[3,48,1024]{2,1,0:T(8,128)(2,1)S(1)} %get-tuple-element.84), channel_id=1, source_target_pairs={{0,64},{32,96},{64,0},{96,32},{1,65},{33,97},{65,1},{97,33},{2,66}... | collective-permute-start | bytes 884744 | tf_op jit(solution)/shard_map/ppermute | solution.py:37
  193.0 10.3 %collective-permute-start.37 = (bf16[2,48,1024]{2,1,0:T(8,128)(2,1)S(1)}, bf16[2,48,1024]{2,1,0:T(8,128)(2,1)S(1)}, u32[]{:S(2)}, u32[]{:S(2)}) collective-permute-start(bf16[2,48,1024]{2,1,0:T(8,128)(2,1)S(1)} %get-tuple-element.86), channel_id=1, source_target_pairs={{0,1},{1,2},{3,0},{4,5},{5,6},{7,4},{8,9},{9,10},{11,8},{12,13},{1... | collective-permute-start | bytes 589832 | tf_op jit(solution)/shard_map/ppermute | solution.py:37
  196.2 7.2 %collective-permute-start.38 = (bf16[2,48,1024]{2,1,0:T(8,128)(2,1)S(1)}, bf16[2,48,1024]{2,1,0:T(8,128)(2,1)S(1)}, u32[]{:S(2)}, u32[]{:S(2)}) collective-permute-start(bf16[2,48,1024]{2,1,0:T(8,128)(2,1)S(1)} %get-tuple-element.87), channel_id=1, source_target_pairs={{1,0},{2,1},{3,2},{5,4},{6,5},{7,6},{9,8},{10,9},{11,10},{13,12},{... | collective-permute-start | bytes 589832 | tf_op jit(solution)/shard_map/ppermute | solution.py:37
  197.7 9.4 %collective-permute-start.39 = (bf16[2,48,1024]{2,1,0:T(8,128)(2,1)S(1)}, bf16[2,48,1024]{2,1,0:T(8,128)(2,1)S(1)}, u32[]{:S(2)}, u32[]{:S(2)}) collective-permute-start(bf16[2,48,1024]{2,1,0:T(8,128)(2,1)S(1)} %get-tuple-element.88), channel_id=1, source_target_pairs={{0,2},{2,0},{3,1},{4,6},{6,4},{7,5},{8,10},{10,8},{11,9},{12,14},{... | collective-permute-start | bytes 589832 | tf_op jit(solution)/shard_map/ppermute | solution.py:37
  210.4 5.5 %collective-permute-start.46 = (bf16[48,1024]{1,0:T(8,128)(2,1)S(1)}, bf16[48,1024]{1,0:T(8,128)(2,1)S(1)}, u32[]{:S(2)}, u32[]{:S(2)}) collective-permute-start(bf16[48,1024]{1,0:T(8,128)(2,1)S(1)} %get-tuple-element.90), channel_id=1, source_target_pairs={{0,32},{32,64},{64,96},{96,0},{1,33},{33,65},{65,97},{97,1},{2,34}... | collective-permute-start | bytes 294920 | tf_op jit(solution)/shard_map/ppermute | solution.py:37
  215.9 9.2 %collective-permute-start.51 = (bf16[4,48,1024]{2,1,0:T(8,128)(2,1)S(1)}, bf16[4,48,1024]{2,1,0:T(8,128)(2,1)S(1)}, u32[]{:S(2)}, u32[]{:S(2)}) collective-permute-start(bf16[4,48,1024]{2,1,0:T(8,128)(2,1)S(1)} %pad_maximum_fusion.3.rest_4_), channel_id=1, source_target_pairs={{0,24},{8,0},{16,8},{24,16},{1,25},{9,1},{17,9},{25,17},{2,26},{10... | collective-permute-start | bytes 1179656 | tf_op jit(solution)/shard_map/ppermute | solution.py:37
  216.6 7.1 %collective-permute-start.42 = (bf16[48,1024]{1,0:T(8,128)(2,1)S(1)}, bf16[48,1024]{1,0:T(8,128)(2,1)S(1)}, u32[]{:S(2)}, u32[]{:S(2)}) collective-permute-start(bf16[48,1024]{1,0:T(8,128)(2,1)S(1)} %get-tuple-element.89), channel_id=1, source_target_pairs={{0,24},{8,0},{16,8},{24,16},{1,25},{9,1},{17,9},{25,17},{2,26},{10... | collective-permute-start | bytes 294920 | tf_op jit(solution)/shard_map/ppermute | solution.py:37
  218.1 5.6 %collective-permute-start.41 = (bf16[48,1024]{1,0:T(8,128)(2,1)S(1)}, bf16[48,1024]{1,0:T(8,128)(2,1)S(1)}, u32[]{:S(2)}, u32[]{:S(2)}) collective-permute-start(bf16[48,1024]{1,0:T(8,128)(2,1)S(1)} %get-tuple-element.89), channel_id=1, source_target_pairs={{0,16},{8,24},{16,0},{24,8},{1,17},{9,25},{17,1},{25,9},{2,18},{10... | collective-permute-start | bytes 294920 | tf_op jit(solution)/shard_map/ppermute | solution.py:37
  219.3 9.1 %collective-permute-start.50 = (bf16[4,48,1024]{2,1,0:T(8,128)(2,1)S(1)}, bf16[4,48,1024]{2,1,0:T(8,128)(2,1)S(1)}, u32[]{:S(2)}, u32[]{:S(2)}) collective-permute-start(bf16[4,48,1024]{2,1,0:T(8,128)(2,1)S(1)} %pad_maximum_fusion.3.rest_4_), channel_id=1, source_target_pairs={{0,16},{8,24},{16,0},{24,8},{1,17},{9,25},{17,1},{25,9},{2,18},{10... | collective-permute-start | bytes 1179656 | tf_op jit(solution)/shard_map/ppermute | solution.py:37
  223.7 11.3 %collective-permute-start.49 = (bf16[4,48,1024]{2,1,0:T(8,128)(2,1)S(1)}, bf16[4,48,1024]{2,1,0:T(8,128)(2,1)S(1)}, u32[]{:S(2)}, u32[]{:S(2)}) collective-permute-start(bf16[4,48,1024]{2,1,0:T(8,128)(2,1)S(1)} %pad_maximum_fusion.3.rest_4_), channel_id=1, source_target_pairs={{0,8},{8,16},{16,24},{24,0},{1,9},{9,17},{17,25},{25,1},{2,10},{10... | collective-permute-start | bytes 1179656 | tf_op jit(solution)/shard_map/ppermute | solution.py:37
  224.2 10.7 %collective-permute-start.45 = (bf16[4,48,1024]{2,1,0:T(8,128)(2,1)S(1)}, bf16[4,48,1024]{2,1,0:T(8,128)(2,1)S(1)}, u32[]{:S(2)}, u32[]{:S(2)}) collective-permute-start(bf16[4,48,1024]{2,1,0:T(8,128)(2,1)S(1)} %pad_maximum_fusion.2.rest_0_), channel_id=1, source_target_pairs={{0,96},{32,0},{64,32},{96,64},{1,97},{33,1},{65,33},{97,65},{2,98}... | collective-permute-start | bytes 1179656 | tf_op jit(solution)/shard_map/ppermute | solution.py:37
  224.6 10.4 %collective-permute-start.44 = (bf16[4,48,1024]{2,1,0:T(8,128)(2,1)S(1)}, bf16[4,48,1024]{2,1,0:T(8,128)(2,1)S(1)}, u32[]{:S(2)}, u32[]{:S(2)}) collective-permute-start(bf16[4,48,1024]{2,1,0:T(8,128)(2,1)S(1)} %pad_maximum_fusion.2.rest_0_), channel_id=1, source_target_pairs={{0,64},{32,96},{64,0},{96,32},{1,65},{33,97},{65,1},{97,33},{2,66}... | collective-permute-start | bytes 1179656 | tf_op jit(solution)/shard_map/ppermute | solution.py:37
  225.1 12.1 %collective-permute-start.43 = (bf16[4,48,1024]{2,1,0:T(8,128)(2,1)S(1)}, bf16[4,48,1024]{2,1,0:T(8,128)(2,1)S(1)}, u32[]{:S(2)}, u32[]{:S(2)}) collective-permute-start(bf16[4,48,1024]{2,1,0:T(8,128)(2,1)S(1)} %pad_maximum_fusion.2.rest_0_), channel_id=1, source_target_pairs={{0,32},{32,64},{64,96},{96,0},{1,33},{33,65},{65,97},{97,1},{2,34}... | collective-permute-start | bytes 1179656 | tf_op jit(solution)/shard_map/ppermute | solution.py:37
  247.0 14.4 %collective-permute-start.52 = (bf16[64,768]{1,0:T(8,128)(2,1)S(1)}, bf16[64,768]{1,0:T(8,128)(2,1)S(1)}, u32[]{:S(2)}, u32[]{:S(2)}) collective-permute-start(bf16[64,768]{1,0:T(8,128)(2,1)S(1)} %get-tuple-element.92), channel_id=1, source_target_pairs={{0,4},{4,0},{1,5},{5,1},{2,6},{6,2},{3,7},{7,3},{8,12},{12,8},{9,1... | collective-permute-start | bytes 294920 | tf_op jit(solution)/shard_map/ppermute | solution.py:41
  262.0 10.7 %collective-permute-start.55 = (bf16[2,64,768]{2,1,0:T(8,128)(2,1)S(1)}, bf16[2,64,768]{2,1,0:T(8,128)(2,1)S(1)}, u32[]{:S(2)}, u32[]{:S(2)}) collective-permute-start(bf16[2,64,768]{2,1,0:T(8,128)(2,1)S(1)} %shard_map.81.rest_0_), channel_id=1, source_target_pairs={{0,3},{1,0},{2,1},{4,7},{5,4},{6,5},{8,11},{9,8},{10,9},{12,15},{1... | collective-permute-start | bytes 589832 | tf_op jit(solution)/shard_map/ppermute | solution.py:37
  266.6 9.2 %collective-permute-start.54 = (bf16[2,64,768]{2,1,0:T(8,128)(2,1)S(1)}, bf16[2,64,768]{2,1,0:T(8,128)(2,1)S(1)}, u32[]{:S(2)}, u32[]{:S(2)}) collective-permute-start(bf16[2,64,768]{2,1,0:T(8,128)(2,1)S(1)} %shard_map.81.rest_0_), channel_id=1, source_target_pairs={{0,2},{1,3},{2,0},{4,6},{5,7},{6,4},{8,10},{9,11},{10,8},{12,14},{... | collective-permute-start | bytes 589832 | tf_op jit(solution)/shard_map/ppermute | solution.py:37
  271.4 7.9 %collective-permute-start.53 = (bf16[2,64,768]{2,1,0:T(8,128)(2,1)S(1)}, bf16[2,64,768]{2,1,0:T(8,128)(2,1)S(1)}, u32[]{:S(2)}, u32[]{:S(2)}) collective-permute-start(bf16[2,64,768]{2,1,0:T(8,128)(2,1)S(1)} %shard_map.81.rest_0_), channel_id=1, source_target_pairs={{0,1},{1,2},{2,3},{4,5},{5,6},{6,7},{8,9},{9,10},{10,11},{12,13},{... | collective-permute-start | bytes 589832 | tf_op jit(solution)/shard_map/ppermute | solution.py:37
  (11 other events, 34.8 us)
where the time goes:
time: 284 us; the launch traced here: 281 us
  waiting for transfers between devices  143 us (50%)
  starting transfers between devices  97.8 us (34%)
  Pallas kernels  37.2 us (13%)
    ppermute x48, waiting for transfers between devices, shift(): return lax.ppermute(value, axis, [p for p in pairs if p[1] < targets])  141 us
    ppermute x48, starting transfers between devices, shift(): return lax.ppermute(value, axis, [p for p in pairs if p[1] < targets])  78.3 us
    pallas_call x10, Pallas kernels, call(): pl.pallas_call(kernel, in_specs=[pl.BlockSpec(memory_space=pltpu.SMEM)] *...  37.2 us
    ppermute x8, starting transfers between devices, swap(): return lax.ppermute(value, 'dp_2', [(0, 1), (1, 0)])  19.4 us
  transfers between devices with their start and end apart: 56, of which 25 were waited for; matrix products, arithmetic and copies ran while one was open for 0% of the time, Pallas kernels for 8%

commit v1 on v0

--- a/solution.py
+++ b/solution.py
@@ -32,9 +32,8 @@
 bf16 = jnp.bfloat16
 
 
-def shift(value, axis, by, sources=RING, targets=RING):
-    pairs = [(i, (i + by) % RING) for i in range(sources)]
-    return lax.ppermute(value, axis, [p for p in pairs if p[1] < targets])
+def shift(value, axis, by):
+    return lax.ppermute(value, axis, [(i, (i + by) % RING) for i in range(RING)])
 
 
 def swap(value):
@@ -44,7 +43,7 @@
 def turn_kernel(info, own, other, first, second, rows):
     width = COLS // 2
     here = info[2]
-    rows[pl.ds(pl.multiple_of(here * width, width), width), :] = own[here].astype(f32)
+    rows[pl.ds(pl.multiple_of(here * width, width), width), :] = own[...].astype(f32)
     rows[pl.ds(pl.multiple_of((1 - here) * width, width), width), :] = other[here].astype(f32)
     value = rows[...].T.astype(bf16)
     first[...] = value[: F // 2]
@@ -206,17 +205,30 @@
                 out[expert, matrix] = pieces[s][expert]
 
 
-def sweep_kernel(info, *rest):
-    parts, kept, sent, (whole, half_gram, half_poly, turned) = rest[:8], rest[8], rest[9], rest[10:]
-    for half in range(2):
-        for t in range(RING):
-            for s in range(RING):
-                near = (info[1 - half] - s) % RING
-                far = (info[half] - t) % RING
-                at = pl.multiple_of(far * CHUNK + near * PIECE, PIECE)
-                whole[pl.ds(at, PIECE), half * HALF : (half + 1) * HALF] = parts[half * RING + t][s]
-    both = (((1,), (1,)), ((), ()))
-    raw = lax.dot_general(whole[...], whole[...], both, preferred_element_type=f32)
+def put_half(half, info, parts, whole):
+    for t in range(RING):
+        for s in range(RING):
+            near = (info[1 - half] - s) % RING
+            far = (info[half] - t) % RING
+            at = pl.multiple_of(far * CHUNK + near * PIECE, PIECE)
+            whole[pl.ds(at, PIECE), :] = parts[t][s]
+
+
+def self_product(ref):
+    return lax.dot_general(ref[...], ref[...], (((1,), (1,)), ((), ())), preferred_element_type=f32)
+
+
+def gram_kernel(info, *rest):
+    parts, (raw, first_half) = rest[:RING], rest[RING:]
+    put_half(0, info, parts, first_half)
+    raw[...] = self_product(first_half)
+
+
+def sweep_kernel(info, raw_first, first_half, *rest):
+    parts, kept, sent = rest[:RING], rest[RING], rest[RING + 1]
+    second_half, half_gram, half_poly, turned, block = rest[RING + 2 :]
+    put_half(1, info, parts, second_half)
+    raw = raw_first[...] + self_product(second_half)
     diagonal = lax.broadcasted_iota(jnp.int32, (F, F), 0) == lax.broadcasted_iota(jnp.int32, (F, F), 1)
     norm = jnp.sqrt(jnp.sum(jnp.where(diagonal, raw, 0.0)))
     inverse = 1.0 / (norm + norm_eps)
@@ -230,8 +242,15 @@
     half_poly[...] = poly_of(gram)
     mixed = ns_first * gram + jnp.dot(half_poly[...], half_gram[...], preferred_element_type=f32)
     gram = ns_first * mixed + jnp.dot(mixed.astype(bf16), half_poly[...], preferred_element_type=f32)
-    column = pl.multiple_of((info[0] * RING + info[1]) * COLS, COLS)
-    mine = whole[:, pl.ds(column, COLS)]
+    place = info[0] * RING + info[1]
+    column = pl.multiple_of((place % (HALF // COLS)) * COLS, COLS)
+    for half, ref in ((0, first_half), (1, second_half)):
+
+        @pl.when(place // (HALF // COLS) == half)
+        def _(ref=ref):
+            block[...] = ref[:, pl.ds(column, COLS)]
+
+    mine = block[...]
     first = inverse * (
         ns_first * mine.astype(f32) + jnp.dot(half_poly[...], mine, preferred_element_type=f32)
     )
@@ -288,6 +307,7 @@
     rows = BLK * BLOCK
     turned = jnp.swapaxes(down_weight, 1, 2)
     other = swap(turned)
+    own = lax.dynamic_index_in_dim(turned, c, 0, False)
     info = jnp.stack([z, x, c, y]).astype(jnp.int32)
     columns = call(
         turn_kernel,
@@ -296,7 +316,7 @@
         [jax.ShapeDtypeStruct((F // 2, COLS), bf16)] * 2,
         [pltpu.VMEM((COLS, F), f32)],
         [info],
-        [turned, other],
+        [own, other],
     )
     count_b, expert_b = swap(block_count), swap(block_expert)
     columns, gate, up, cotangent, token_inputs, count_b, expert_b = lax.optimization_barrier(
@@ -379,7 +399,7 @@
         [info],
         [*final_terms[0], *final_terms[1]],
     )
-    arrived = [shift(parts[s], "rep", s, targets=3) for s in SHIFTS]
+    arrived = [shift(parts[s], "rep", s) for s in SHIFTS]
     block = call(
         settle_kernel,
         F * D,
@@ -389,27 +409,37 @@
         [info],
         [parts[0], *arrived],
     )
-    stage = gather_stage([block[0], block[1]], True)
+    stage = gather_stage(block, True)
     stage = gather_stage([jnp.stack(v) for v in stage], False)
+    raw, first_half = call(
+        gram_kernel,
+        F * F * D,
+        8,
+        [jax.ShapeDtypeStruct((F, F), f32), jax.ShapeDtypeStruct((F, HALF), bf16)],
+        [],
+        [info],
+        stage[0],
+    )
     kept, sent = call(
         sweep_kernel,
         8 * F * F * F,
         26,
         [jax.ShapeDtypeStruct((COLS // 2, F), bf16)] * 2,
         [
-            pltpu.VMEM((F, D), bf16),
+            pltpu.VMEM((F, HALF), bf16),
             pltpu.VMEM((F, F), bf16),
             pltpu.VMEM((F, F), bf16),
             pltpu.VMEM((COLS, F), f32),
+            pltpu.VMEM((F, COLS), bf16),
         ],
         [info],
-        [*stage[0], *stage[1]],
+        [raw, first_half, *stage[1]],
     )
     narrow = (2, COLS // 2, F)
     pair = call(
         pair_kernel, F * COLS, 2, jax.ShapeDtypeStruct(narrow, bf16), [], [info], [kept, swap(sent)]
     )
-    pieces = {0: pair, **{s: shift(pair, "rep", s, sources=3) for s in SHIFTS}}
+    pieces = {0: pair, **{s: shift(pair, "rep", s) for s in SHIFTS}}
     everyone = call(
         spread_kernel,
         F * COLS,

time: 284 us -> 275 us (0.968); the launches traced: 281 us -> 275 us
  starting transfers between devices: 97.8 us -> 89.5 us
  waiting for transfers between devices: 143 us -> 146 us
    ppermute x48, starting transfers between devices: 78.3 us -> 71.2 us  [shift(): lax.ppermute(value, axis, [(i, (i + by) % RING) for i in range(RING)])]
    ppermute x48, waiting for transfers between devices: 141 us -> 144 us  [shift(): lax.ppermute(value, axis, [(i, (i + by) % RING) for i in range(RING)])]
    pallas_call x10 -> x11, Pallas kernels: 37.2 us -> 38.4 us  [call(): pl.pallas_call(kernel, in_specs=[pl.BlockSpec(memory_space=pltpu.SMEM)] *...]
  transfers between devices with their start and end apart: 56 -> 56, of which waited for: 25 -> 26; matrix products, arithmetic and copies ran while one was open for 0% -> 0% of each run, Pallas kernels for 8% -> 9%
where the time goes in v1:
time: 275 us
  waiting for transfers between devices  146 us (53%)
  starting transfers between devices  89.5 us (33%)
  Pallas kernels  38.4 us (14%)
    ppermute x48, waiting for transfers between devices, shift(): lax.ppermute(value, axis, [(i, (i + by) % RING) for i in range(RING)])  144 us
    ppermute x48, starting transfers between devices, shift(): lax.ppermute(value, axis, [(i, (i + by) % RING) for i in range(RING)])  71.2 us
    pallas_call x11, Pallas kernels, call(): pl.pallas_call(kernel, in_specs=[pl.BlockSpec(memory_space=pltpu.SMEM)] *...  38.4 us
    ppermute x8, starting transfers between devices, swap(): return lax.ppermute(value, 'dp_2', [(0, 1), (1, 0)])  18.3 us
  transfers between devices with their start and end apart: 56, of which 26 were waited for; matrix products, arithmetic and copies ran while one was open for 0% of the time, Pallas kernels for 9%

profile of v1, /device:TPU:1, one launch (start us, length us, event | category | flops | bytes accessed | tf_op | source)
XLA Modules:
  0.0 274.9 jit_solution(10469421481969861262)
XLA Ops:
  0.0 1.4 collective-permute-start.2
  4.5 2.6 collective-permute-start.15
  8.7 3.8 %collective-permute-start.9 = (bf16[384,128]{1,0:T(8,128)(2,1)S(1)}, bf16[384,128]{1,0:T(8,128)(2,1)S(1)}, u32[]{:S(2)}, u32[]{:S(2)}) collective-permute-start(bf16[384,128]{1,0:T(8,128)(2,1)S(1)} %get-tuple-element.61), channel_id=1, source_target_pairs={{0,96},{32,0},{64,32},{96,64},{1,97},{33,1},{65,33},{97,65},{2,98}... | collective-permute-start | bytes 294920 | tf_op jit(solution)/shard_map/ppermute | solution.py:36
  12.5 2.7 collective-permute-done.13
  15.3 3.8 %collective-permute-start.18 = (bf16[4,384,128]{2,1,0:T(8,128)(2,1)S(1)}, bf16[4,384,128]{2,1,0:T(8,128)(2,1)S(1)}, u32[]{:S(2)}, u32[]{:S(2)}) collective-permute-start(bf16[4,384,128]{2,1,0:T(8,128)(2,1)S(1)} %pad_maximum_fusion.1.rest_4_), channel_id=1, source_target_pairs={{0,96},{32,0},{64,32},{96,64},{1,97},{33,1},{65,33},{97,65},{2,98}... | collective-permute-start | bytes 1179656 | tf_op jit(solution)/shard_map/ppermute | solution.py:36
  19.8 4.4 %collective-permute-done.8 = bf16[384,128]{1,0:T(8,128)(2,1)S(1)} collective-permute-done((bf16[384,128]{1,0:T(8,128)(2,1)S(1)}, bf16[384,128]{1,0:T(8,128)(2,1)S(1)}, u32[]{:S(2)}, u32[]{:S(2)}) %collective-permute-start.8) | collective-permute-done | bytes 98336 | tf_op jit(solution)/shard_map/ppermute | solution.py:36
  24.2 2.7 collective-permute-start.3
  28.9 10.4 %collective-permute-done.17.rest_6_ = bf16[4,384,128]{2,1,0:T(8,128)(2,1)S(1)} collective-permute-done((bf16[4,384,128]{2,1,0:T(8,128)(2,1)S(1)}, bf16[4,384,128]{2,1,0:T(8,128)(2,1)S(1)}, u32[]{:S(2)}, u32[]{:S(2)}) %collective-permute-start.17) | collective-permute-done | bytes 393248 | tf_op jit(solution)/shard_map/ppermute | solution.py:36
  39.3 4.5 %collective-permute-start.16 = (bf16[4,384,128]{2,1,0:T(8,128)(2,1)S(1)}, bf16[4,384,128]{2,1,0:T(8,128)(2,1)S(1)}, u32[]{:S(2)}, u32[]{:S(2)}) collective-permute-start(bf16[4,384,128]{2,1,0:T(8,128)(2,1)S(1)} %pad_maximum_fusion.1.rest_4_), channel_id=1, source_target_pairs={{0,32},{32,64},{64,96},{96,0},{1,33},{33,65},{65,97},{97,1},{2,34}... | collective-permute-start | bytes 1179656 | tf_op jit(solution)/shard_map/ppermute | solution.py:36
  45.8 7.4 %shard_map.74 = (bf16[1,192,1024]{2,1,0:T(8,128)(2,1)S(1)}, bf16[1,192,1024]{2,1,0:T(8,128)(2,1)S(1)}, bf16[1,192,1024]{2,1,0:T(8,128)(2,1)S(1)}, bf16[1,192,102...) custom-call(s32[4]{0:T(128)S(1)} %pad_add_fusion.info, ...), custom_call_target="tpu_custom_call" | custom-call | flops 3221225472 | bytes 6442450 | tf_op jit(solution)/shard_map/pallas_call | solution.py:279
  53.3 2.7 collective-permute-start.23
  56.0 9.6 %collective-permute-done.10.rest_1_ = bf16[4,384,128]{2,1,0:T(8,128)(2,1)S(1)} collective-permute-done((bf16[4,384,128]{2,1,0:T(8,128)(2,1)S(1)}, bf16[4,384,128]{2,1,0:T(8,128)(2,1)S(1)}, u32[]{:S(2)}, u32[]{:S(2)}) %collective-permute-start.10) | collective-permute-done | bytes 393248 | tf_op jit(solution)/shard_map/ppermute | solution.py:36
  65.6 13.5 %shard_map.75 = (bf16[2,192,1024]{2,1,0:T(8,128)(2,1)S(1)}, bf16[2,192,1024]{2,1,0:T(8,128)(2,1)S(1)}, bf16[2,192,1024]{2,1,0:T(8,128)(2,1)S(1)}, bf16[2,192,102...) custom-call(s32[4]{0:T(128)S(1)} %pad_add_fusion.info, ...), custom_call_target="tpu_custom_call" | custom-call | flops 9663676416 | bytes 19327352 | tf_op jit(solution)/shard_map/pallas_call | solution.py:279
  79.2 2.7 collective-permute-start.20
  83.0 1.9 collective-permute-start.24
  84.9 38.9 %collective-permute-done.24.rest_7_ = bf16[1,192,1024]{2,1,0:T(8,128)(2,1)S(1)} collective-permute-done((bf16[1,192,1024]{2,1,0:T(8,128)(2,1)S(1)}, bf16[1,192,1024]{2,1,0:T(8,128)(2,1)S(1)}, u32[]{:S(2)}, u32[]{:S(2)}) %collective-permute-start.24) | collective-permute-done | bytes 393248 | tf_op jit(solution)/shard_map/ppermute | solution.py:36
  123.8 2.7 collective-permute-start.29
  127.6 1.9 collective-permute-start.33
  130.6 36.8 %collective-permute-done.32.rest_6_ = bf16[1,192,1024]{2,1,0:T(8,128)(2,1)S(1)} collective-permute-done((bf16[1,192,1024]{2,1,0:T(8,128)(2,1)S(1)}, bf16[1,192,1024]{2,1,0:T(8,128)(2,1)S(1)}, u32[]{:S(2)}, u32[]{:S(2)}) %collective-permute-start.32) | collective-permute-done | bytes 393248 | tf_op jit(solution)/shard_map/ppermute | solution.py:36
  167.4 10.0 %collective-permute-start.26 = (bf16[3,48,1024]{2,1,0:T(8,128)(2,1)S(1)}, bf16[3,48,1024]{2,1,0:T(8,128)(2,1)S(1)}, u32[]{:S(2)}, u32[]{:S(2)}) collective-permute-start(bf16[3,48,1024]{2,1,0:T(8,128)(2,1)S(1)} %get-tuple-element.73), channel_id=1, source_target_pairs={{0,24},{8,0},{16,8},{24,16},{1,25},{9,1},{17,9},{25,17},{2,26},{10... | collective-permute-start | bytes 884744 | tf_op jit(solution)/shard_map/ppermute | solution.py:36
  180.4 2.1 collective-permute-start.35
  183.1 2.4 collective-permute-done.27.rest_3_
  185.4 1.5 collective-permute-done.34.rest_5_
  186.9 2.8 %collective-permute-done.35.rest_6_ = bf16[3,48,1024]{2,1,0:T(8,128)(2,1)S(1)} collective-permute-done((bf16[3,48,1024]{2,1,0:T(8,128)(2,1)S(1)}, bf16[3,48,1024]{2,1,0:T(8,128)(2,1)S(1)}, u32[]{:S(2)}, u32[]{:S(2)}) %collective-permute-start.35) | collective-permute-done | bytes 294944 | tf_op jit(solution)/shard_map/ppermute | solution.py:36
  189.7 1.9 collective-permute-done.36.rest_7_
  192.6 1.5 collective-permute-start.37
  194.1 1.5 collective-permute-start.38
  195.6 1.6 collective-permute-start.39
  197.2 1.4 collective-permute-done.37.rest_1_
  198.6 1.7 collective-permute-done.38.rest_2_
  200.4 1.5 collective-permute-done.39.rest_3_
  202.5 1.4 collective-permute-start.42
  206.1 2.9 %collective-permute-done.41 = bf16[48,1024]{1,0:T(8,128)(2,1)S(1)} collective-permute-done((bf16[48,1024]{1,0:T(8,128)(2,1)S(1)}, bf16[48,1024]{1,0:T(8,128)(2,1)S(1)}, u32[]{:S(2)}, u32[]{:S(2)}) %collective-permute-start.41) | collective-permute-done | bytes 98336 | tf_op jit(solution)/shard_map/ppermute | solution.py:36
  211.1 2.2 collective-permute-start.47
  213.3 2.7 collective-permute-start.44
  216.0 1.7 collective-permute-done.48
  217.7 6.2 %collective-permute-start.43 = (bf16[4,48,1024]{2,1,0:T(8,128)(2,1)S(1)}, bf16[4,48,1024]{2,1,0:T(8,128)(2,1)S(1)}, u32[]{:S(2)}, u32[]{:S(2)}) collective-permute-start(bf16[4,48,1024]{2,1,0:T(8,128)(2,1)S(1)} %pad_maximum_fusion.2.rest_0_), channel_id=1, source_target_pairs={{0,32},{32,64},{64,96},{96,0},{1,33},{33,65},{65,97},{97,1},{2,34}... | collective-permute-start | bytes 1179656 | tf_op jit(solution)/shard_map/ppermute | solution.py:36
  224.2 1.4 collective-permute-start.49
  225.6 5.1 %collective-permute-done.43.rest_1_ = bf16[4,48,1024]{2,1,0:T(8,128)(2,1)S(1)} collective-permute-done((bf16[4,48,1024]{2,1,0:T(8,128)(2,1)S(1)}, bf16[4,48,1024]{2,1,0:T(8,128)(2,1)S(1)}, u32[]{:S(2)}, u32[]{:S(2)}) %collective-permute-start.43) | collective-permute-done | bytes 393248 | tf_op jit(solution)/shard_map/ppermute | solution.py:36
  230.7 2.1 shard_map.80
  232.8 3.7 %collective-permute-done.49.rest_1_ = bf16[4,48,1024]{2,1,0:T(8,128)(2,1)S(1)} collective-permute-done((bf16[4,48,1024]{2,1,0:T(8,128)(2,1)S(1)}, bf16[4,48,1024]{2,1,0:T(8,128)(2,1)S(1)}, u32[]{:S(2)}, u32[]{:S(2)}) %collective-permute-start.49) | collective-permute-done | bytes 393248 | tf_op jit(solution)/shard_map/ppermute | solution.py:36
  236.6 8.8 %shard_map.81 = (bf16[64,768]{1,0:T(8,128)(2,1)S(1)}, bf16[64,768]{1,0:T(8,128)(2,1)S(1)}) custom-call(s32[4]{0:T(128)S(1)} %pad_add_fusion.info, f32[768,768]{1,0:T(8,128)S(1)} %get-tuple-element.92.raw_first, bf16[768,1024]{1,0:T(8,128)(2,1)S(1)} %get-tuple-element.93.first_half, bf16[4,48,1024]{2,1,0:T(8,128)(2,1)S(1)} %pad_maximum_fusion.3.rest_0_, ...), custom_call_target="tpu_custom_call" | custom-call | flops 3623878656 | bytes 7247757 | tf_op jit(solution)/shard_map/pallas_call | solution.py:279
  245.4 12.3 %collective-permute-start.52 = (bf16[64,768]{1,0:T(8,128)(2,1)S(1)}, bf16[64,768]{1,0:T(8,128)(2,1)S(1)}, u32[]{:S(2)}, u32[]{:S(2)}) collective-permute-start(bf16[64,768]{1,0:T(8,128)(2,1)S(1)} %get-tuple-element.96), channel_id=1, source_target_pairs={{0,4},{4,0},{1,5},{5,1},{2,6},{6,2},{3,7},{7,3},{8,12},{12,8},{9,1... | collective-permute-start | bytes 294920 | tf_op jit(solution)/shard_map/ppermute | solution.py:40
  259.2 1.6 collective-permute-start.55
  262.0 3.5 %collective-permute-done.55.rest_3_ = bf16[2,64,768]{2,1,0:T(8,128)(2,1)S(1)} collective-permute-done((bf16[2,64,768]{2,1,0:T(8,128)(2,1)S(1)}, bf16[2,64,768]{2,1,0:T(8,128)(2,1)S(1)}, u32[]{:S(2)}, u32[]{:S(2)}) %collective-permute-start.55) | collective-permute-done | bytes 196640 | tf_op jit(solution)/shard_map/ppermute | solution.py:36
  265.4 2.8 %collective-permute-done.54.rest_2_ = bf16[2,64,768]{2,1,0:T(8,128)(2,1)S(1)} collective-permute-done((bf16[2,64,768]{2,1,0:T(8,128)(2,1)S(1)}, bf16[2,64,768]{2,1,0:T(8,128)(2,1)S(1)}, u32[]{:S(2)}, u32[]{:S(2)}) %collective-permute-start.54) | collective-permute-done | bytes 196640 | tf_op jit(solution)/shard_map/ppermute | solution.py:36
  268.3 5.2 %collective-permute-done.53.rest_1_ = bf16[2,64,768]{2,1,0:T(8,128)(2,1)S(1)} collective-permute-done((bf16[2,64,768]{2,1,0:T(8,128)(2,1)S(1)}, bf16[2,64,768]{2,1,0:T(8,128)(2,1)S(1)}, u32[]{:S(2)}, u32[]{:S(2)}) %collective-permute-start.53) | collective-permute-done | bytes 196640 | tf_op jit(solution)/shard_map/ppermute | solution.py:36
  273.4 1.4 shard_map.83
  (85 shorter events, 25.3 us)
Async XLA Ops:
  3.9 41.2 %collective-permute-start.5 = (bf16[512,2048]{1,0:T(8,128)(2,1)}, bf16[512,2048]{1,0:T(8,128)(2,1)S(1)}, u32[]{:S(2)}, u32[]{:S(2)}) collective-permute-start(bf16[512,2048]{1,0:T(8,128)(2,1)} %cot_h.1), channel_id=1, source_target_pairs={{0,4},{4,0},{1,5},{5,1},{2,6},{6,2},{3,7},{7,3},{8,12},{12,8},{9,1... | collective-permute-start | bytes 6291464 | tf_op jit(solution)/shard_map/ppermute | solution.py:40
  4.4 61.3 %collective-permute-start.6 = (bf16[512,2048]{1,0:T(8,128)(2,1)}, bf16[512,2048]{1,0:T(8,128)(2,1)S(1)}, u32[]{:S(2)}, u32[]{:S(2)}) collective-permute-start(bf16[512,2048]{1,0:T(8,128)(2,1)} %tok_h), channel_id=1, source_target_pairs={{0,4},{4,0},{1,5},{5,1},{2,6},{6,2},{3,7},{7,3},{8,12},{12,8},{9,1... | collective-permute-start | bytes 6291464 | tf_op jit(solution)/shard_map/ppermute | solution.py:40
  7.1 5.4 %collective-permute-start.14 = (bf16[384,128]{1,0:T(8,128)(2,1)S(1)}, bf16[384,128]{1,0:T(8,128)(2,1)S(1)}, u32[]{:S(2)}, u32[]{:S(2)}) collective-permute-start(bf16[384,128]{1,0:T(8,128)(2,1)S(1)} %get-tuple-element.62), channel_id=1, source_target_pairs={{0,16},{8,24},{16,0},{24,8},{1,17},{9,25},{17,1},{25,9},{2,18},{10... | collective-permute-start | bytes 294920 | tf_op jit(solution)/shard_map/ppermute | solution.py:36
  7.6 7.6 %collective-permute-start.13 = (bf16[384,128]{1,0:T(8,128)(2,1)S(1)}, bf16[384,128]{1,0:T(8,128)(2,1)S(1)}, u32[]{:S(2)}, u32[]{:S(2)}) collective-permute-start(bf16[384,128]{1,0:T(8,128)(2,1)S(1)} %get-tuple-element.62), channel_id=1, source_target_pairs={{0,8},{8,16},{16,24},{24,0},{1,9},{9,17},{17,25},{25,1},{2,10},{10... | collective-permute-start | bytes 294920 | tf_op jit(solution)/shard_map/ppermute | solution.py:36
  8.7 10.4 %collective-permute-start.9 = (bf16[384,128]{1,0:T(8,128)(2,1)S(1)}, bf16[384,128]{1,0:T(8,128)(2,1)S(1)}, u32[]{:S(2)}, u32[]{:S(2)}) collective-permute-start(bf16[384,128]{1,0:T(8,128)(2,1)S(1)} %get-tuple-element.61), channel_id=1, source_target_pairs={{0,96},{32,0},{64,32},{96,64},{1,97},{33,1},{65,33},{97,65},{2,98}... | collective-permute-start | bytes 294920 | tf_op jit(solution)/shard_map/ppermute | solution.py:36
  15.3 13.6 %collective-permute-start.18 = (bf16[4,384,128]{2,1,0:T(8,128)(2,1)S(1)}, bf16[4,384,128]{2,1,0:T(8,128)(2,1)S(1)}, u32[]{:S(2)}, u32[]{:S(2)}) collective-permute-start(bf16[4,384,128]{2,1,0:T(8,128)(2,1)S(1)} %pad_maximum_fusion.1.rest_4_), channel_id=1, source_target_pairs={{0,96},{32,0},{64,32},{96,64},{1,97},{33,1},{65,33},{97,65},{2,98}... | collective-permute-start | bytes 1179656 | tf_op jit(solution)/shard_map/ppermute | solution.py:36
  19.1 7.8 %collective-permute-start.7 = (bf16[384,128]{1,0:T(8,128)(2,1)S(1)}, bf16[384,128]{1,0:T(8,128)(2,1)S(1)}, u32[]{:S(2)}, u32[]{:S(2)}) collective-permute-start(bf16[384,128]{1,0:T(8,128)(2,1)S(1)} %get-tuple-element.61), channel_id=1, source_target_pairs={{0,32},{32,64},{64,96},{96,0},{1,33},{33,65},{65,97},{97,1},{2,34}... | collective-permute-start | bytes 294920 | tf_op jit(solution)/shard_map/ppermute | solution.py:36
  24.2 19.7 %collective-permute-start.3 = (bf16[512,768]{1,0:T(8,128)(2,1)}, bf16[512,768]{1,0:T(8,128)(2,1)S(1)}, u32[]{:S(2)}, u32[]{:S(2)}) collective-permute-start(bf16[512,768]{1,0:T(8,128)(2,1)} %gate_h), channel_id=1, source_target_pairs={{0,4},{4,0},{1,5},{5,1},{2,6},{6,2},{3,7},{7,3},{8,12},{12,8},{9,1... | collective-permute-start | bytes 2359304 | tf_op jit(solution)/shard_map/ppermute | solution.py:40
  26.9 18.2 %collective-permute-start.4 = (bf16[512,768]{1,0:T(8,128)(2,1)}, bf16[512,768]{1,0:T(8,128)(2,1)S(1)}, u32[]{:S(2)}, u32[]{:S(2)}) collective-permute-start(bf16[512,768]{1,0:T(8,128)(2,1)} %up_h), channel_id=1, source_target_pairs={{0,4},{4,0},{1,5},{5,1},{2,6},{6,2},{3,7},{7,3},{8,12},{12,8},{9,1... | collective-permute-start | bytes 2359304 | tf_op jit(solution)/shard_map/ppermute | solution.py:40
  28.8 10.5 %collective-permute-start.17 = (bf16[4,384,128]{2,1,0:T(8,128)(2,1)S(1)}, bf16[4,384,128]{2,1,0:T(8,128)(2,1)S(1)}, u32[]{:S(2)}, u32[]{:S(2)}) collective-permute-start(bf16[4,384,128]{2,1,0:T(8,128)(2,1)S(1)} %pad_maximum_fusion.1.rest_4_), channel_id=1, source_target_pairs={{0,64},{32,96},{64,0},{96,32},{1,65},{33,97},{65,1},{97,33},{2,66}... | collective-permute-start | bytes 1179656 | tf_op jit(solution)/shard_map/ppermute | solution.py:36
  39.3 13.9 %collective-permute-start.16 = (bf16[4,384,128]{2,1,0:T(8,128)(2,1)S(1)}, bf16[4,384,128]{2,1,0:T(8,128)(2,1)S(1)}, u32[]{:S(2)}, u32[]{:S(2)}) collective-permute-start(bf16[4,384,128]{2,1,0:T(8,128)(2,1)S(1)} %pad_maximum_fusion.1.rest_4_), channel_id=1, source_target_pairs={{0,32},{32,64},{64,96},{96,0},{1,33},{33,65},{65,97},{97,1},{2,34}... | collective-permute-start | bytes 1179656 | tf_op jit(solution)/shard_map/ppermute | solution.py:36
  43.9 9.5 %collective-permute-start.12 = (bf16[4,384,128]{2,1,0:T(8,128)(2,1)S(1)}, bf16[4,384,128]{2,1,0:T(8,128)(2,1)S(1)}, u32[]{:S(2)}, u32[]{:S(2)}) collective-permute-start(bf16[4,384,128]{2,1,0:T(8,128)(2,1)S(1)} %pad_maximum_fusion.rest_0_), channel_id=1, source_target_pairs={{0,24},{8,0},{16,8},{24,16},{1,25},{9,1},{17,9},{25,17},{2,26},{10... | collective-permute-start | bytes 1179656 | tf_op jit(solution)/shard_map/ppermute | solution.py:36
  45.1 10.9 %collective-permute-start.11 = (bf16[4,384,128]{2,1,0:T(8,128)(2,1)S(1)}, bf16[4,384,128]{2,1,0:T(8,128)(2,1)S(1)}, u32[]{:S(2)}, u32[]{:S(2)}) collective-permute-start(bf16[4,384,128]{2,1,0:T(8,128)(2,1)S(1)} %pad_maximum_fusion.rest_0_), channel_id=1, source_target_pairs={{0,16},{8,24},{16,0},{24,8},{1,17},{9,25},{17,1},{25,9},{2,18},{10... | collective-permute-start | bytes 1179656 | tf_op jit(solution)/shard_map/ppermute | solution.py:36
  45.1 20.5 %collective-permute-start.10 = (bf16[4,384,128]{2,1,0:T(8,128)(2,1)S(1)}, bf16[4,384,128]{2,1,0:T(8,128)(2,1)S(1)}, u32[]{:S(2)}, u32[]{:S(2)}) collective-permute-start(bf16[4,384,128]{2,1,0:T(8,128)(2,1)S(1)} %pad_maximum_fusion.rest_0_), channel_id=1, source_target_pairs={{0,8},{8,16},{16,24},{24,0},{1,9},{9,17},{17,25},{25,1},{2,10},{10... | collective-permute-start | bytes 1179656 | tf_op jit(solution)/shard_map/ppermute | solution.py:36
  53.2 29.7 %collective-permute-start.22 = (bf16[1,192,1024]{2,1,0:T(8,128)(2,1)S(1)}, bf16[1,192,1024]{2,1,0:T(8,128)(2,1)S(1)}, u32[]{:S(2)}, u32[]{:S(2)}) collective-permute-start(bf16[1,192,1024]{2,1,0:T(8,128)(2,1)S(1)} %get-tuple-element.68), channel_id=1, source_target_pairs={{0,32},{32,64},{64,96},{96,0},{1,33},{33,65},{65,97},{97,1},{2,34}... | collective-permute-start | bytes 1179656 | tf_op jit(solution)/shard_map/ppermute | solution.py:36
  53.3 31.5 %collective-permute-start.23 = (bf16[1,192,1024]{2,1,0:T(8,128)(2,1)S(1)}, bf16[1,192,1024]{2,1,0:T(8,128)(2,1)S(1)}, u32[]{:S(2)}, u32[]{:S(2)}) collective-permute-start(bf16[1,192,1024]{2,1,0:T(8,128)(2,1)S(1)} %get-tuple-element.69), channel_id=1, source_target_pairs={{0,96},{32,0},{64,32},{96,64},{1,97},{33,1},{65,33},{97,65},{2,98}... | collective-permute-start | bytes 1179656 | tf_op jit(solution)/shard_map/ppermute | solution.py:36
  79.1 47.3 %collective-permute-start.19 = (bf16[2,192,1024]{2,1,0:T(8,128)(2,1)S(1)}, bf16[2,192,1024]{2,1,0:T(8,128)(2,1)S(1)}, u32[]{:S(2)}, u32[]{:S(2)}) collective-permute-start(bf16[2,192,1024]{2,1,0:T(8,128)(2,1)S(1)} %get-tuple-element.64), channel_id=1, source_target_pairs={{0,32},{32,64},{64,96},{96,0},{1,33},{33,65},{65,97},{97,1},{2,34}... | collective-permute-start | bytes 2359304 | tf_op jit(solution)/shard_map/ppermute | solution.py:36
  79.2 47.2 %collective-permute-start.20 = (bf16[2,192,1024]{2,1,0:T(8,128)(2,1)S(1)}, bf16[2,192,1024]{2,1,0:T(8,128)(2,1)S(1)}, u32[]{:S(2)}, u32[]{:S(2)}) collective-permute-start(bf16[2,192,1024]{2,1,0:T(8,128)(2,1)S(1)} %get-tuple-element.65), channel_id=1, source_target_pairs={{0,96},{32,0},{64,32},{96,64},{1,97},{33,1},{65,33},{97,65},{2,98}... | collective-permute-start | bytes 2359304 | tf_op jit(solution)/shard_map/ppermute | solution.py:36
  81.9 45.8 %collective-permute-start.21 = (bf16[2,192,1024]{2,1,0:T(8,128)(2,1)S(1)}, bf16[2,192,1024]{2,1,0:T(8,128)(2,1)S(1)}, u32[]{:S(2)}, u32[]{:S(2)}) collective-permute-start(bf16[2,192,1024]{2,1,0:T(8,128)(2,1)S(1)} %get-tuple-element.66), channel_id=1, source_target_pairs={{0,64},{32,96},{64,0},{96,32},{1,65},{33,97},{65,1},{97,33},{2,66}... | collective-permute-start | bytes 2359304 | tf_op jit(solution)/shard_map/ppermute | solution.py:36
  83.0 40.8 %collective-permute-start.24 = (bf16[1,192,1024]{2,1,0:T(8,128)(2,1)S(1)}, bf16[1,192,1024]{2,1,0:T(8,128)(2,1)S(1)}, u32[]{:S(2)}, u32[]{:S(2)}) collective-permute-start(bf16[1,192,1024]{2,1,0:T(8,128)(2,1)S(1)} %get-tuple-element.70), channel_id=1, source_target_pairs={{0,64},{32,96},{64,0},{96,32},{1,65},{33,97},{65,1},{97,33},{2,66}... | collective-permute-start | bytes 1179656 | tf_op jit(solution)/shard_map/ppermute | solution.py:36
  84.9 38.9 %collective-permute-start.31 = (bf16[1,192,1024]{2,1,0:T(8,128)(2,1)S(1)}, bf16[1,192,1024]{2,1,0:T(8,128)(2,1)S(1)}, u32[]{:S(2)}, u32[]{:S(2)}) collective-permute-start(bf16[1,192,1024]{2,1,0:T(8,128)(2,1)S(1)} %get-tuple-element.80), channel_id=1, source_target_pairs={{0,8},{8,16},{16,24},{24,0},{1,9},{9,17},{17,25},{25,1},{2,10},{10... | collective-permute-start | bytes 1179656 | tf_op jit(solution)/shard_map/ppermute | solution.py:36
  123.8 53.7 %collective-permute-start.28 = (bf16[2,192,1024]{2,1,0:T(8,128)(2,1)S(1)}, bf16[2,192,1024]{2,1,0:T(8,128)(2,1)S(1)}, u32[]{:S(2)}, u32[]{:S(2)}) collective-permute-start(bf16[2,192,1024]{2,1,0:T(8,128)(2,1)S(1)} %get-tuple-element.76), channel_id=1, source_target_pairs={{0,8},{8,16},{16,24},{24,0},{1,9},{9,17},{17,25},{25,1},{2,10},{10... | collective-permute-start | bytes 2359304 | tf_op jit(solution)/shard_map/ppermute | solution.py:36
  123.8 54.8 %collective-permute-start.29 = (bf16[2,192,1024]{2,1,0:T(8,128)(2,1)S(1)}, bf16[2,192,1024]{2,1,0:T(8,128)(2,1)S(1)}, u32[]{:S(2)}, u32[]{:S(2)}) collective-permute-start(bf16[2,192,1024]{2,1,0:T(8,128)(2,1)S(1)} %get-tuple-element.77), channel_id=1, source_target_pairs={{0,24},{8,0},{16,8},{24,16},{1,25},{9,1},{17,9},{25,17},{2,26},{10... | collective-permute-start | bytes 2359304 | tf_op jit(solution)/shard_map/ppermute | solution.py:36
  126.4 52.1 %collective-permute-start.30 = (bf16[2,192,1024]{2,1,0:T(8,128)(2,1)S(1)}, bf16[2,192,1024]{2,1,0:T(8,128)(2,1)S(1)}, u32[]{:S(2)}, u32[]{:S(2)}) collective-permute-start(bf16[2,192,1024]{2,1,0:T(8,128)(2,1)S(1)} %get-tuple-element.78), channel_id=1, source_target_pairs={{0,16},{8,24},{16,0},{24,8},{1,17},{9,25},{17,1},{25,9},{2,18},{10... | collective-permute-start | bytes 2359304 | tf_op jit(solution)/shard_map/ppermute | solution.py:36
  126.5 40.9 %collective-permute-start.32 = (bf16[1,192,1024]{2,1,0:T(8,128)(2,1)S(1)}, bf16[1,192,1024]{2,1,0:T(8,128)(2,1)S(1)}, u32[]{:S(2)}, u32[]{:S(2)}) collective-permute-start(bf16[1,192,1024]{2,1,0:T(8,128)(2,1)S(1)} %get-tuple-element.81), channel_id=1, source_target_pairs={{0,24},{8,0},{16,8},{24,16},{1,25},{9,1},{17,9},{25,17},{2,26},{10... | collective-permute-start | bytes 1179656 | tf_op jit(solution)/shard_map/ppermute | solution.py:36
  127.6 39.8 %collective-permute-start.33 = (bf16[1,192,1024]{2,1,0:T(8,128)(2,1)S(1)}, bf16[1,192,1024]{2,1,0:T(8,128)(2,1)S(1)}, u32[]{:S(2)}, u32[]{:S(2)}) collective-permute-start(bf16[1,192,1024]{2,1,0:T(8,128)(2,1)S(1)} %get-tuple-element.82), channel_id=1, source_target_pairs={{0,16},{8,24},{16,0},{24,8},{1,17},{9,25},{17,1},{25,9},{2,18},{10... | collective-permute-start | bytes 1179656 | tf_op jit(solution)/shard_map/ppermute | solution.py:36
  167.4 15.1 %collective-permute-start.25 = (bf16[3,48,1024]{2,1,0:T(8,128)(2,1)S(1)}, bf16[3,48,1024]{2,1,0:T(8,128)(2,1)S(1)}, u32[]{:S(2)}, u32[]{:S(2)}) collective-permute-start(bf16[3,48,1024]{2,1,0:T(8,128)(2,1)S(1)} %get-tuple-element.72), channel_id=1, source_target_pairs={{0,8},{8,16},{16,24},{24,0},{1,9},{9,17},{17,25},{25,1},{2,10},{10... | collective-permute-start | bytes 884744 | tf_op jit(solution)/shard_map/ppermute | solution.py:36
  167.4 15.7 %collective-permute-start.26 = (bf16[3,48,1024]{2,1,0:T(8,128)(2,1)S(1)}, bf16[3,48,1024]{2,1,0:T(8,128)(2,1)S(1)}, u32[]{:S(2)}, u32[]{:S(2)}) collective-permute-start(bf16[3,48,1024]{2,1,0:T(8,128)(2,1)S(1)} %get-tuple-element.73), channel_id=1, source_target_pairs={{0,24},{8,0},{16,8},{24,16},{1,25},{9,1},{17,9},{25,17},{2,26},{10... | collective-permute-start | bytes 884744 | tf_op jit(solution)/shard_map/ppermute | solution.py:36
  177.4 8.0 %collective-permute-start.27 = (bf16[3,48,1024]{2,1,0:T(8,128)(2,1)S(1)}, bf16[3,48,1024]{2,1,0:T(8,128)(2,1)S(1)}, u32[]{:S(2)}, u32[]{:S(2)}) collective-permute-start(bf16[3,48,1024]{2,1,0:T(8,128)(2,1)S(1)} %get-tuple-element.74), channel_id=1, source_target_pairs={{0,16},{8,24},{16,0},{24,8},{1,17},{9,25},{17,1},{25,9},{2,18},{10... | collective-permute-start | bytes 884744 | tf_op jit(solution)/shard_map/ppermute | solution.py:36
  179.7 7.1 %collective-permute-start.34 = (bf16[3,48,1024]{2,1,0:T(8,128)(2,1)S(1)}, bf16[3,48,1024]{2,1,0:T(8,128)(2,1)S(1)}, u32[]{:S(2)}, u32[]{:S(2)}) collective-permute-start(bf16[3,48,1024]{2,1,0:T(8,128)(2,1)S(1)} %get-tuple-element.84), channel_id=1, source_target_pairs={{0,32},{32,64},{64,96},{96,0},{1,33},{33,65},{65,97},{97,1},{2,34}... | collective-permute-start | bytes 884744 | tf_op jit(solution)/shard_map/ppermute | solution.py:36
  180.4 9.3 %collective-permute-start.35 = (bf16[3,48,1024]{2,1,0:T(8,128)(2,1)S(1)}, bf16[3,48,1024]{2,1,0:T(8,128)(2,1)S(1)}, u32[]{:S(2)}, u32[]{:S(2)}) collective-permute-start(bf16[3,48,1024]{2,1,0:T(8,128)(2,1)S(1)} %get-tuple-element.85), channel_id=1, source_target_pairs={{0,96},{32,0},{64,32},{96,64},{1,97},{33,1},{65,33},{97,65},{2,98}... | collective-permute-start | bytes 884744 | tf_op jit(solution)/shard_map/ppermute | solution.py:36
  182.5 9.1 %collective-permute-start.36 = (bf16[3,48,1024]{2,1,0:T(8,128)(2,1)S(1)}, bf16[3,48,1024]{2,1,0:T(8,128)(2,1)S(1)}, u32[]{:S(2)}, u32[]{:S(2)}) collective-permute-start(bf16[3,48,1024]{2,1,0:T(8,128)(2,1)S(1)} %get-tuple-element.86), channel_id=1, source_target_pairs={{0,64},{32,96},{64,0},{96,32},{1,65},{33,97},{65,1},{97,33},{2,66}... | collective-permute-start | bytes 884744 | tf_op jit(solution)/shard_map/ppermute | solution.py:36
  192.6 6.0 %collective-permute-start.37 = (bf16[2,48,1024]{2,1,0:T(8,128)(2,1)S(1)}, bf16[2,48,1024]{2,1,0:T(8,128)(2,1)S(1)}, u32[]{:S(2)}, u32[]{:S(2)}) collective-permute-start(bf16[2,48,1024]{2,1,0:T(8,128)(2,1)S(1)} %get-tuple-element.88), channel_id=1, source_target_pairs={{0,1},{1,2},{2,3},{3,0},{4,5},{5,6},{6,7},{7,4},{8,9},{9,10},{10,1... | collective-permute-start | bytes 589832 | tf_op jit(solution)/shard_map/ppermute | solution.py:36
  194.1 6.2 %collective-permute-start.38 = (bf16[2,48,1024]{2,1,0:T(8,128)(2,1)S(1)}, bf16[2,48,1024]{2,1,0:T(8,128)(2,1)S(1)}, u32[]{:S(2)}, u32[]{:S(2)}) collective-permute-start(bf16[2,48,1024]{2,1,0:T(8,128)(2,1)S(1)} %get-tuple-element.89), channel_id=1, source_target_pairs={{0,3},{1,0},{2,1},{3,2},{4,7},{5,4},{6,5},{7,6},{8,11},{9,8},{10,9... | collective-permute-start | bytes 589832 | tf_op jit(solution)/shard_map/ppermute | solution.py:36
  195.6 6.3 %collective-permute-start.39 = (bf16[2,48,1024]{2,1,0:T(8,128)(2,1)S(1)}, bf16[2,48,1024]{2,1,0:T(8,128)(2,1)S(1)}, u32[]{:S(2)}, u32[]{:S(2)}) collective-permute-start(bf16[2,48,1024]{2,1,0:T(8,128)(2,1)S(1)} %get-tuple-element.90), channel_id=1, source_target_pairs={{0,2},{1,3},{2,0},{3,1},{4,6},{5,7},{6,4},{7,5},{8,10},{9,11},{10,... | collective-permute-start | bytes 589832 | tf_op jit(solution)/shard_map/ppermute | solution.py:36
  210.0 14.2 %collective-permute-start.45 = (bf16[4,48,1024]{2,1,0:T(8,128)(2,1)S(1)}, bf16[4,48,1024]{2,1,0:T(8,128)(2,1)S(1)}, u32[]{:S(2)}, u32[]{:S(2)}) collective-permute-start(bf16[4,48,1024]{2,1,0:T(8,128)(2,1)S(1)} %pad_maximum_fusion.2.rest_0_), channel_id=1, source_target_pairs={{0,96},{32,0},{64,32},{96,64},{1,97},{33,1},{65,33},{97,65},{2,98}... | collective-permute-start | bytes 1179656 | tf_op jit(solution)/shard_map/ppermute | solution.py:36
  211.0 6.7 %collective-permute-start.48 = (bf16[48,1024]{1,0:T(8,128)(2,1)S(1)}, bf16[48,1024]{1,0:T(8,128)(2,1)S(1)}, u32[]{:S(2)}, u32[]{:S(2)}) collective-permute-start(bf16[48,1024]{1,0:T(8,128)(2,1)S(1)} %get-tuple-element.94), channel_id=1, source_target_pairs={{0,96},{32,0},{64,32},{96,64},{1,97},{33,1},{65,33},{97,65},{2,98}... | collective-permute-start | bytes 294920 | tf_op jit(solution)/shard_map/ppermute | solution.py:36
  211.1 12.9 %collective-permute-start.47 = (bf16[48,1024]{1,0:T(8,128)(2,1)S(1)}, bf16[48,1024]{1,0:T(8,128)(2,1)S(1)}, u32[]{:S(2)}, u32[]{:S(2)}) collective-permute-start(bf16[48,1024]{1,0:T(8,128)(2,1)S(1)} %get-tuple-element.94), channel_id=1, source_target_pairs={{0,64},{32,96},{64,0},{96,32},{1,65},{33,97},{65,1},{97,33},{2,66}... | collective-permute-start | bytes 294920 | tf_op jit(solution)/shard_map/ppermute | solution.py:36
  213.3 10.7 %collective-permute-start.46 = (bf16[48,1024]{1,0:T(8,128)(2,1)S(1)}, bf16[48,1024]{1,0:T(8,128)(2,1)S(1)}, u32[]{:S(2)}, u32[]{:S(2)}) collective-permute-start(bf16[48,1024]{1,0:T(8,128)(2,1)S(1)} %get-tuple-element.94), channel_id=1, source_target_pairs={{0,32},{32,64},{64,96},{96,0},{1,33},{33,65},{65,97},{97,1},{2,34}... | collective-permute-start | bytes 294920 | tf_op jit(solution)/shard_map/ppermute | solution.py:36
  213.3 12.3 %collective-permute-start.44 = (bf16[4,48,1024]{2,1,0:T(8,128)(2,1)S(1)}, bf16[4,48,1024]{2,1,0:T(8,128)(2,1)S(1)}, u32[]{:S(2)}, u32[]{:S(2)}) collective-permute-start(bf16[4,48,1024]{2,1,0:T(8,128)(2,1)S(1)} %pad_maximum_fusion.2.rest_0_), channel_id=1, source_target_pairs={{0,64},{32,96},{64,0},{96,32},{1,65},{33,97},{65,1},{97,33},{2,66}... | collective-permute-start | bytes 1179656 | tf_op jit(solution)/shard_map/ppermute | solution.py:36
  217.7 13.0 %collective-permute-start.43 = (bf16[4,48,1024]{2,1,0:T(8,128)(2,1)S(1)}, bf16[4,48,1024]{2,1,0:T(8,128)(2,1)S(1)}, u32[]{:S(2)}, u32[]{:S(2)}) collective-permute-start(bf16[4,48,1024]{2,1,0:T(8,128)(2,1)S(1)} %pad_maximum_fusion.2.rest_0_), channel_id=1, source_target_pairs={{0,32},{32,64},{64,96},{96,0},{1,33},{33,65},{65,97},{97,1},{2,34}... | collective-permute-start | bytes 1179656 | tf_op jit(solution)/shard_map/ppermute | solution.py:36
  224.0 8.8 %collective-permute-start.51 = (bf16[4,48,1024]{2,1,0:T(8,128)(2,1)S(1)}, bf16[4,48,1024]{2,1,0:T(8,128)(2,1)S(1)}, u32[]{:S(2)}, u32[]{:S(2)}) collective-permute-start(bf16[4,48,1024]{2,1,0:T(8,128)(2,1)S(1)} %pad_maximum_fusion.3.rest_0_), channel_id=1, source_target_pairs={{0,24},{8,0},{16,8},{24,16},{1,25},{9,1},{17,9},{25,17},{2,26},{10... | collective-permute-start | bytes 1179656 | tf_op jit(solution)/shard_map/ppermute | solution.py:36
  224.1 8.7 %collective-permute-start.50 = (bf16[4,48,1024]{2,1,0:T(8,128)(2,1)S(1)}, bf16[4,48,1024]{2,1,0:T(8,128)(2,1)S(1)}, u32[]{:S(2)}, u32[]{:S(2)}) collective-permute-start(bf16[4,48,1024]{2,1,0:T(8,128)(2,1)S(1)} %pad_maximum_fusion.3.rest_0_), channel_id=1, source_target_pairs={{0,16},{8,24},{16,0},{24,8},{1,17},{9,25},{17,1},{25,9},{2,18},{10... | collective-permute-start | bytes 1179656 | tf_op jit(solution)/shard_map/ppermute | solution.py:36
  224.2 12.3 %collective-permute-start.49 = (bf16[4,48,1024]{2,1,0:T(8,128)(2,1)S(1)}, bf16[4,48,1024]{2,1,0:T(8,128)(2,1)S(1)}, u32[]{:S(2)}, u32[]{:S(2)}) collective-permute-start(bf16[4,48,1024]{2,1,0:T(8,128)(2,1)S(1)} %pad_maximum_fusion.3.rest_0_), channel_id=1, source_target_pairs={{0,8},{8,16},{16,24},{24,0},{1,9},{9,17},{17,25},{25,1},{2,10},{10... | collective-permute-start | bytes 1179656 | tf_op jit(solution)/shard_map/ppermute | solution.py:36
  245.4 13.3 %collective-permute-start.52 = (bf16[64,768]{1,0:T(8,128)(2,1)S(1)}, bf16[64,768]{1,0:T(8,128)(2,1)S(1)}, u32[]{:S(2)}, u32[]{:S(2)}) collective-permute-start(bf16[64,768]{1,0:T(8,128)(2,1)S(1)} %get-tuple-element.96), channel_id=1, source_target_pairs={{0,4},{4,0},{1,5},{5,1},{2,6},{6,2},{3,7},{7,3},{8,12},{12,8},{9,1... | collective-permute-start | bytes 294920 | tf_op jit(solution)/shard_map/ppermute | solution.py:40
  259.2 6.2 %collective-permute-start.55 = (bf16[2,64,768]{2,1,0:T(8,128)(2,1)S(1)}, bf16[2,64,768]{2,1,0:T(8,128)(2,1)S(1)}, u32[]{:S(2)}, u32[]{:S(2)}) collective-permute-start(bf16[2,64,768]{2,1,0:T(8,128)(2,1)S(1)} %shard_map.82.rest_0_), channel_id=1, source_target_pairs={{0,3},{1,0},{2,1},{3,2},{4,7},{5,4},{6,5},{7,6},{8,11},{9,8},{10,9... | collective-permute-start | bytes 589832 | tf_op jit(solution)/shard_map/ppermute | solution.py:36
  260.9 7.4 %collective-permute-start.54 = (bf16[2,64,768]{2,1,0:T(8,128)(2,1)S(1)}, bf16[2,64,768]{2,1,0:T(8,128)(2,1)S(1)}, u32[]{:S(2)}, u32[]{:S(2)}) collective-permute-start(bf16[2,64,768]{2,1,0:T(8,128)(2,1)S(1)} %shard_map.82.rest_0_), channel_id=1, source_target_pairs={{0,2},{1,3},{2,0},{3,1},{4,6},{5,7},{6,4},{7,5},{8,10},{9,11},{10,... | collective-permute-start | bytes 589832 | tf_op jit(solution)/shard_map/ppermute | solution.py:36
  262.0 11.5 %collective-permute-start.53 = (bf16[2,64,768]{2,1,0:T(8,128)(2,1)S(1)}, bf16[2,64,768]{2,1,0:T(8,128)(2,1)S(1)}, u32[]{:S(2)}, u32[]{:S(2)}) collective-permute-start(bf16[2,64,768]{2,1,0:T(8,128)(2,1)S(1)} %shard_map.82.rest_0_), channel_id=1, source_target_pairs={{0,1},{1,2},{2,3},{3,0},{4,5},{5,6},{6,7},{7,4},{8,9},{9,10},{10,1... | collective-permute-start | bytes 589832 | tf_op jit(solution)/shard_map/ppermute | solution.py:36
  (10 other events, 122.9 us)

commit v2 on v1

--- a/solution.py
+++ b/solution.py
@@ -195,14 +195,22 @@
 
 
 def spread_kernel(info, *rest):
-    pieces, out = rest[:RING], rest[RING]
-    for s in range(RING):
-        matrix = (info[3] - s) % RING
-
-        @pl.when(matrix < 3)
-        def _(s=s, matrix=matrix):
-            for expert in range(2):
-                out[expert, matrix] = pieces[s][expert]
+    pieces, out, sems = rest[:RING], rest[RING], rest[RING + 1]
+
+    def copies(s):
+        matrix = jnp.minimum((info[3] - s) % RING, 2)
+        return [
+            pltpu.make_async_copy(pieces[s].at[e], out.at[e, matrix], sems.at[s, e])
+            for e in range(2)
+        ]
+
+    for finish in (False, True):
+        for s in range(RING):
+
+            @pl.when((info[3] - s) % RING < 3)
+            def _(s=s, finish=finish):
+                for copy in copies(s):
+                    copy.wait() if finish else copy.start()
 
 
 def put_half(half, info, parts, whole):
@@ -214,34 +222,66 @@
             whole[pl.ds(at, PIECE), :] = parts[t][s]
 
 
-def self_product(ref):
-    return lax.dot_general(ref[...], ref[...], (((1,), (1,)), ((), ())), preferred_element_type=f32)
+SIDE = F // 3
+
+
+def upper_blocks(left, right, out, turned=False):
+    for j in range(3):
+        rows, cols = slice(0, (j + 1) * SIDE), slice(j * SIDE, (j + 1) * SIDE)
+        if turned:
+            out[rows, cols] = lax.dot_general(
+                left[rows, :], right[cols, :], (((1,), (1,)), ((), ())), preferred_element_type=f32
+            )
+        else:
+            out[rows, cols] = jnp.dot(left[rows, :], right[:, cols], preferred_element_type=f32)
+
+
+def mirror(out):
+    for j in range(3):
+        for i in range(j):
+            low, high = slice(i * SIDE, (i + 1) * SIDE), slice(j * SIDE, (j + 1) * SIDE)
+            out[high, low] = out[low, high].T
 
 
 def gram_kernel(info, *rest):
     parts, (raw, first_half) = rest[:RING], rest[RING:]
     put_half(0, info, parts, first_half)
-    raw[...] = self_product(first_half)
+    upper_blocks(first_half, first_half, raw, True)
 
 
 def sweep_kernel(info, raw_first, first_half, *rest):
     parts, kept, sent = rest[:RING], rest[RING], rest[RING + 1]
-    second_half, half_gram, half_poly, turned, block = rest[RING + 2 :]
+    second_half, half_gram, half_poly, turned, block, gram, other = rest[RING + 2 :]
     put_half(1, info, parts, second_half)
-    raw = raw_first[...] + self_product(second_half)
-    diagonal = lax.broadcasted_iota(jnp.int32, (F, F), 0) == lax.broadcasted_iota(jnp.int32, (F, F), 1)
-    norm = jnp.sqrt(jnp.sum(jnp.where(diagonal, raw, 0.0)))
-    inverse = 1.0 / (norm + norm_eps)
-    gram = raw * inverse * inverse
-
-    def poly_of(gram):
-        half_gram[...] = gram.astype(bf16)
-        squared = jnp.dot(half_gram[...], half_gram[...], preferred_element_type=f32)
-        return (ns_second * gram + ns_third * squared).astype(bf16)
-
-    half_poly[...] = poly_of(gram)
-    mixed = ns_first * gram + jnp.dot(half_poly[...], half_gram[...], preferred_element_type=f32)
-    gram = ns_first * mixed + jnp.dot(mixed.astype(bf16), half_poly[...], preferred_element_type=f32)
+    upper_blocks(second_half, second_half, other, True)
+    for j in range(3):
+        rows, cols = slice(0, (j + 1) * SIDE), slice(j * SIDE, (j + 1) * SIDE)
+        gram[rows, cols] = other[rows, cols] + raw_first[rows, cols]
+    mirror(gram)
+    diagonal = lax.broadcasted_iota(jnp.int32, (SIDE, SIDE), 0) == lax.broadcasted_iota(
+        jnp.int32, (SIDE, SIDE), 1
+    )
+    trace = 0.0
+    for j in range(3):
+        one = slice(j * SIDE, (j + 1) * SIDE)
+        trace = trace + jnp.sum(jnp.where(diagonal, gram[one, one], 0.0))
+    inverse = 1.0 / (jnp.sqrt(trace) + norm_eps)
+    gram[...] = gram[...] * inverse * inverse
+
+    def poly_of():
+        half_gram[...] = gram[...].astype(bf16)
+        upper_blocks(half_gram, half_gram, other)
+        mirror(other)
+        return (ns_second * gram[...] + ns_third * other[...]).astype(bf16)
+
+    half_poly[...] = poly_of()
+    upper_blocks(half_poly, half_gram, other)
+    mirror(other)
+    gram[...] = ns_first * gram[...] + other[...]
+    half_gram[...] = gram[...].astype(bf16)
+    upper_blocks(half_gram, half_poly, other)
+    mirror(other)
+    gram[...] = ns_first * gram[...] + other[...]
     place = info[0] * RING + info[1]
     column = pl.multiple_of((place % (HALF // COLS)) * COLS, COLS)
     for half, ref in ((0, first_half), (1, second_half)):
@@ -255,7 +295,7 @@
         ns_first * mine.astype(f32) + jnp.dot(half_poly[...], mine, preferred_element_type=f32)
     )
     first = first.astype(bf16)
-    last = poly_of(gram)
+    last = poly_of()
     newer = ns_first * first.astype(f32) + jnp.dot(last, first, preferred_element_type=f32)
     turned[...] = (jnp.sqrt(jnp.float32(D)) * newer).T
     width = COLS // 2
@@ -267,7 +307,7 @@
     return [jax.ShapeDtypeStruct((count, CHUNK, HALF), bf16)] * 8
 
 
-def call(kernel, flops, room, out_shape, scratch, scalars, operands, far=0):
+def call(kernel, flops, room, out_shape, scratch, scalars, operands, far=0, out_far=False):
     several = isinstance(out_shape, list)
     operands = [
         pltpu.with_memory_space_constraint(v, pltpu.HBM) if i < far else v
@@ -275,7 +315,7 @@
     ]
     specs = [pl.BlockSpec(memory_space=pltpu.HBM)] * far
     specs += [pl.BlockSpec(memory_space=pltpu.VMEM)] * (len(operands) - far)
-    out_spec = pl.BlockSpec(memory_space=pltpu.VMEM)
+    out_spec = pl.BlockSpec(memory_space=pltpu.HBM if out_far else pltpu.VMEM)
     return pl.pallas_call(
         kernel,
         in_specs=[pl.BlockSpec(memory_space=pltpu.SMEM)] * len(scalars) + specs,
@@ -431,6 +471,8 @@
             pltpu.VMEM((F, F), bf16),
             pltpu.VMEM((COLS, F), f32),
             pltpu.VMEM((F, COLS), bf16),
+            pltpu.VMEM((F, F), f32),
+            pltpu.VMEM((F, F), f32),
         ],
         [info],
         [raw, first_half, *stage[1]],
@@ -445,9 +487,10 @@
         F * COLS,
         4,
         jax.ShapeDtypeStruct((2, 3, COLS // 2, F), bf16),
-        [],
+        [pltpu.SemaphoreType.DMA((RING, 2))],
         [info],
         [pieces[s] for s in range(RING)],
+        out_far=True,
     )
     return jnp.swapaxes(everyone, 2, 3)
 

time: 275 us -> 273 us (level)
  transfers between devices with their start and end apart: 56 -> 56, of which waited for: 26 -> 27; matrix products, arithmetic and copies ran while one was open for 0% -> 0% of each run, Pallas kernels for 9% -> 9%
where the time goes in v2:
time: 273 us
  waiting for transfers between devices  146 us (53%)
  starting transfers between devices  89.5 us (33%)
  Pallas kernels  35.7 us (13%)
    ppermute x48, waiting for transfers between devices, shift(): lax.ppermute(value, axis, [(i, (i + by) % RING) for i in range(RING)])  145 us
    ppermute x48, starting transfers between devices, shift(): lax.ppermute(value, axis, [(i, (i + by) % RING) for i in range(RING)])  71.2 us
    pallas_call x11, Pallas kernels, call(): pl.pallas_call(kernel, in_specs=[pl.BlockSpec(memory_space=pltpu.SMEM)] *...  35.7 us
    ppermute x8, starting transfers between devices, swap(): return lax.ppermute(value, 'dp_2', [(0, 1), (1, 0)])  18.3 us
  transfers between devices with their start and end apart: 56, of which 27 were waited for; matrix products, arithmetic and copies ran while one was open for 0% of the time, Pallas kernels for 9%

profile of v2, /device:TPU:1, one launch (start us, length us, event | category | flops | bytes accessed | tf_op | source)
XLA Modules:
  0.0 272.7 jit_solution(9559905613877343211)
XLA Ops:
  0.0 1.4 collective-permute-start.2
  4.5 2.6 collective-permute-start.15
  8.7 3.8 %collective-permute-start.9 = (bf16[384,128]{1,0:T(8,128)(2,1)S(1)}, bf16[384,128]{1,0:T(8,128)(2,1)S(1)}, u32[]{:S(2)}, u32[]{:S(2)}) collective-permute-start(bf16[384,128]{1,0:T(8,128)(2,1)S(1)} %get-tuple-element.61), channel_id=1, source_target_pairs={{0,96},{32,0},{64,32},{96,64},{1,97},{33,1},{65,33},{97,65},{2,98}... | collective-permute-start | bytes 294920 | tf_op jit(solution)/shard_map/ppermute | solution.py:36
  12.5 2.7 collective-permute-done.13
  15.3 3.8 %collective-permute-start.18 = (bf16[4,384,128]{2,1,0:T(8,128)(2,1)S(1)}, bf16[4,384,128]{2,1,0:T(8,128)(2,1)S(1)}, u32[]{:S(2)}, u32[]{:S(2)}) collective-permute-start(bf16[4,384,128]{2,1,0:T(8,128)(2,1)S(1)} %pad_maximum_fusion.1.rest_4_), channel_id=1, source_target_pairs={{0,96},{32,0},{64,32},{96,64},{1,97},{33,1},{65,33},{97,65},{2,98}... | collective-permute-start | bytes 1179656 | tf_op jit(solution)/shard_map/ppermute | solution.py:36
  19.8 4.4 %collective-permute-done.8 = bf16[384,128]{1,0:T(8,128)(2,1)S(1)} collective-permute-done((bf16[384,128]{1,0:T(8,128)(2,1)S(1)}, bf16[384,128]{1,0:T(8,128)(2,1)S(1)}, u32[]{:S(2)}, u32[]{:S(2)}) %collective-permute-start.8) | collective-permute-done | bytes 98336 | tf_op jit(solution)/shard_map/ppermute | solution.py:36
  24.2 2.7 %collective-permute-start.3 = (bf16[512,768]{1,0:T(8,128)(2,1)}, bf16[512,768]{1,0:T(8,128)(2,1)S(1)}, u32[]{:S(2)}, u32[]{:S(2)}) collective-permute-start(bf16[512,768]{1,0:T(8,128)(2,1)} %gate_h), channel_id=1, source_target_pairs={{0,4},{4,0},{1,5},{5,1},{2,6},{6,2},{3,7},{7,3},{8,12},{12,8},{9,1... | collective-permute-start | bytes 2359304 | tf_op jit(solution)/shard_map/ppermute | solution.py:40
  28.9 10.4 %collective-permute-done.17.rest_6_ = bf16[4,384,128]{2,1,0:T(8,128)(2,1)S(1)} collective-permute-done((bf16[4,384,128]{2,1,0:T(8,128)(2,1)S(1)}, bf16[4,384,128]{2,1,0:T(8,128)(2,1)S(1)}, u32[]{:S(2)}, u32[]{:S(2)}) %collective-permute-start.17) | collective-permute-done | bytes 393248 | tf_op jit(solution)/shard_map/ppermute | solution.py:36
  39.3 4.5 %collective-permute-start.16 = (bf16[4,384,128]{2,1,0:T(8,128)(2,1)S(1)}, bf16[4,384,128]{2,1,0:T(8,128)(2,1)S(1)}, u32[]{:S(2)}, u32[]{:S(2)}) collective-permute-start(bf16[4,384,128]{2,1,0:T(8,128)(2,1)S(1)} %pad_maximum_fusion.1.rest_4_), channel_id=1, source_target_pairs={{0,32},{32,64},{64,96},{96,0},{1,33},{33,65},{65,97},{97,1},{2,34}... | collective-permute-start | bytes 1179656 | tf_op jit(solution)/shard_map/ppermute | solution.py:36
  45.8 7.4 %shard_map.74 = (bf16[1,192,1024]{2,1,0:T(8,128)(2,1)S(1)}, bf16[1,192,1024]{2,1,0:T(8,128)(2,1)S(1)}, bf16[1,192,1024]{2,1,0:T(8,128)(2,1)S(1)}, bf16[1,192,102...) custom-call(s32[4]{0:T(128)S(1)} %pad_add_fusion.info, ...), custom_call_target="tpu_custom_call" | custom-call | flops 3221225472 | bytes 6442450 | tf_op jit(solution)/shard_map/pallas_call | solution.py:319
  53.3 2.7 collective-permute-start.23
  56.0 9.6 %collective-permute-done.10.rest_1_ = bf16[4,384,128]{2,1,0:T(8,128)(2,1)S(1)} collective-permute-done((bf16[4,384,128]{2,1,0:T(8,128)(2,1)S(1)}, bf16[4,384,128]{2,1,0:T(8,128)(2,1)S(1)}, u32[]{:S(2)}, u32[]{:S(2)}) %collective-permute-start.10) | collective-permute-done | bytes 393248 | tf_op jit(solution)/shard_map/ppermute | solution.py:36
  65.6 13.5 %shard_map.75 = (bf16[2,192,1024]{2,1,0:T(8,128)(2,1)S(1)}, bf16[2,192,1024]{2,1,0:T(8,128)(2,1)S(1)}, bf16[2,192,1024]{2,1,0:T(8,128)(2,1)S(1)}, bf16[2,192,102...) custom-call(s32[4]{0:T(128)S(1)} %pad_add_fusion.info, ...), custom_call_target="tpu_custom_call" | custom-call | flops 9663676416 | bytes 19327352 | tf_op jit(solution)/shard_map/pallas_call | solution.py:319
  79.2 2.7 collective-permute-start.20
  83.0 1.9 collective-permute-start.24
  84.9 38.9 %collective-permute-done.24.rest_7_ = bf16[1,192,1024]{2,1,0:T(8,128)(2,1)S(1)} collective-permute-done((bf16[1,192,1024]{2,1,0:T(8,128)(2,1)S(1)}, bf16[1,192,1024]{2,1,0:T(8,128)(2,1)S(1)}, u32[]{:S(2)}, u32[]{:S(2)}) %collective-permute-start.24) | collective-permute-done | bytes 393248 | tf_op jit(solution)/shard_map/ppermute | solution.py:36
  123.8 2.7 collective-permute-start.29
  127.6 1.9 collective-permute-start.33
  130.6 36.8 %collective-permute-done.32.rest_6_ = bf16[1,192,1024]{2,1,0:T(8,128)(2,1)S(1)} collective-permute-done((bf16[1,192,1024]{2,1,0:T(8,128)(2,1)S(1)}, bf16[1,192,1024]{2,1,0:T(8,128)(2,1)S(1)}, u32[]{:S(2)}, u32[]{:S(2)}) %collective-permute-start.32) | collective-permute-done | bytes 393248 | tf_op jit(solution)/shard_map/ppermute | solution.py:36
  167.4 10.0 %collective-permute-start.26 = (bf16[3,48,1024]{2,1,0:T(8,128)(2,1)S(1)}, bf16[3,48,1024]{2,1,0:T(8,128)(2,1)S(1)}, u32[]{:S(2)}, u32[]{:S(2)}) collective-permute-start(bf16[3,48,1024]{2,1,0:T(8,128)(2,1)S(1)} %get-tuple-element.73), channel_id=1, source_target_pairs={{0,24},{8,0},{16,8},{24,16},{1,25},{9,1},{17,9},{25,17},{2,26},{10... | collective-permute-start | bytes 884744 | tf_op jit(solution)/shard_map/ppermute | solution.py:36
  180.4 2.1 collective-permute-start.35
  183.1 2.4 collective-permute-done.27.rest_3_
  185.4 1.5 collective-permute-done.34.rest_5_
  186.9 2.8 %collective-permute-done.35.rest_6_ = bf16[3,48,1024]{2,1,0:T(8,128)(2,1)S(1)} collective-permute-done((bf16[3,48,1024]{2,1,0:T(8,128)(2,1)S(1)}, bf16[3,48,1024]{2,1,0:T(8,128)(2,1)S(1)}, u32[]{:S(2)}, u32[]{:S(2)}) %collective-permute-start.35) | collective-permute-done | bytes 294944 | tf_op jit(solution)/shard_map/ppermute | solution.py:36
  189.7 1.9 collective-permute-done.36.rest_7_
  192.6 1.5 collective-permute-start.37
  194.1 1.5 collective-permute-start.38
  195.6 1.6 collective-permute-start.39
  197.2 1.4 collective-permute-done.37.rest_1_
  198.6 1.7 collective-permute-done.38.rest_2_
  200.4 1.5 collective-permute-done.39.rest_3_
  202.5 1.4 collective-permute-start.42
  206.1 2.9 %collective-permute-done.41 = bf16[48,1024]{1,0:T(8,128)(2,1)S(1)} collective-permute-done((bf16[48,1024]{1,0:T(8,128)(2,1)S(1)}, bf16[48,1024]{1,0:T(8,128)(2,1)S(1)}, u32[]{:S(2)}, u32[]{:S(2)}) %collective-permute-start.41) | collective-permute-done | bytes 98336 | tf_op jit(solution)/shard_map/ppermute | solution.py:36
  211.1 2.2 collective-permute-start.47
  213.3 2.7 collective-permute-start.44
  216.0 1.7 collective-permute-done.48
  217.7 6.2 %collective-permute-start.43 = (bf16[4,48,1024]{2,1,0:T(8,128)(2,1)S(1)}, bf16[4,48,1024]{2,1,0:T(8,128)(2,1)S(1)}, u32[]{:S(2)}, u32[]{:S(2)}) collective-permute-start(bf16[4,48,1024]{2,1,0:T(8,128)(2,1)S(1)} %pad_maximum_fusion.2.rest_0_), channel_id=1, source_target_pairs={{0,32},{32,64},{64,96},{96,0},{1,33},{33,65},{65,97},{97,1},{2,34}... | collective-permute-start | bytes 1179656 | tf_op jit(solution)/shard_map/ppermute | solution.py:36
  224.2 1.4 collective-permute-start.49
  225.6 5.1 %collective-permute-done.43.rest_1_ = bf16[4,48,1024]{2,1,0:T(8,128)(2,1)S(1)} collective-permute-done((bf16[4,48,1024]{2,1,0:T(8,128)(2,1)S(1)}, bf16[4,48,1024]{2,1,0:T(8,128)(2,1)S(1)}, u32[]{:S(2)}, u32[]{:S(2)}) %collective-permute-start.43) | collective-permute-done | bytes 393248 | tf_op jit(solution)/shard_map/ppermute | solution.py:36
  230.7 1.7 shard_map.80
  232.7 3.9 %collective-permute-done.49.rest_1_ = bf16[4,48,1024]{2,1,0:T(8,128)(2,1)S(1)} collective-permute-done((bf16[4,48,1024]{2,1,0:T(8,128)(2,1)S(1)}, bf16[4,48,1024]{2,1,0:T(8,128)(2,1)S(1)}, u32[]{:S(2)}, u32[]{:S(2)}) %collective-permute-start.49) | collective-permute-done | bytes 393248 | tf_op jit(solution)/shard_map/ppermute | solution.py:36
  236.6 6.5 %shard_map.81 = (bf16[64,768]{1,0:T(8,128)(2,1)S(1)}, bf16[64,768]{1,0:T(8,128)(2,1)S(1)}) custom-call(s32[4]{0:T(128)S(1)} %pad_add_fusion.info, f32[768,768]{1,0:T(8,128)S(1)} %get-tuple-element.92.raw_first, bf16[768,1024]{1,0:T(8,128)(2,1)S(1)} %get-tuple-element.93.first_half, bf16[4,48,1024]{2,1,0:T(8,128)(2,1)S(1)} %pad_maximum_fusion.3.rest_0_, ...), custom_call_target="tpu_custom_call" | custom-call | flops 3623878656 | bytes 7247757 | tf_op jit(solution)/shard_map/pallas_call | solution.py:319
  243.1 12.3 %collective-permute-start.52 = (bf16[64,768]{1,0:T(8,128)(2,1)S(1)}, bf16[64,768]{1,0:T(8,128)(2,1)S(1)}, u32[]{:S(2)}, u32[]{:S(2)}) collective-permute-start(bf16[64,768]{1,0:T(8,128)(2,1)S(1)} %get-tuple-element.96), channel_id=1, source_target_pairs={{0,4},{4,0},{1,5},{5,1},{2,6},{6,2},{3,7},{7,3},{8,12},{12,8},{9,1... | collective-permute-start | bytes 294920 | tf_op jit(solution)/shard_map/ppermute | solution.py:40
  257.0 1.6 collective-permute-start.55
  259.7 3.5 %collective-permute-done.55.rest_3_ = bf16[2,64,768]{2,1,0:T(8,128)(2,1)S(1)} collective-permute-done((bf16[2,64,768]{2,1,0:T(8,128)(2,1)S(1)}, bf16[2,64,768]{2,1,0:T(8,128)(2,1)S(1)}, u32[]{:S(2)}, u32[]{:S(2)}) %collective-permute-start.55) | collective-permute-done | bytes 196640 | tf_op jit(solution)/shard_map/ppermute | solution.py:36
  263.1 2.8 %collective-permute-done.54.rest_2_ = bf16[2,64,768]{2,1,0:T(8,128)(2,1)S(1)} collective-permute-done((bf16[2,64,768]{2,1,0:T(8,128)(2,1)S(1)}, bf16[2,64,768]{2,1,0:T(8,128)(2,1)S(1)}, u32[]{:S(2)}, u32[]{:S(2)}) %collective-permute-start.54) | collective-permute-done | bytes 196640 | tf_op jit(solution)/shard_map/ppermute | solution.py:36
  266.0 5.2 %collective-permute-done.53.rest_1_ = bf16[2,64,768]{2,1,0:T(8,128)(2,1)S(1)} collective-permute-done((bf16[2,64,768]{2,1,0:T(8,128)(2,1)S(1)}, bf16[2,64,768]{2,1,0:T(8,128)(2,1)S(1)}, u32[]{:S(2)}, u32[]{:S(2)}) %collective-permute-start.53) | collective-permute-done | bytes 196640 | tf_op jit(solution)/shard_map/ppermute | solution.py:36
  271.1 1.4 shard_map.83
  (85 shorter events, 25.5 us)
Async XLA Ops:
  3.9 41.2 %collective-permute-start.5 = (bf16[512,2048]{1,0:T(8,128)(2,1)}, bf16[512,2048]{1,0:T(8,128)(2,1)S(1)}, u32[]{:S(2)}, u32[]{:S(2)}) collective-permute-start(bf16[512,2048]{1,0:T(8,128)(2,1)} %cot_h.1), channel_id=1, source_target_pairs={{0,4},{4,0},{1,5},{5,1},{2,6},{6,2},{3,7},{7,3},{8,12},{12,8},{9,1... | collective-permute-start | bytes 6291464 | tf_op jit(solution)/shard_map/ppermute | solution.py:40
  4.4 61.3 %collective-permute-start.6 = (bf16[512,2048]{1,0:T(8,128)(2,1)}, bf16[512,2048]{1,0:T(8,128)(2,1)S(1)}, u32[]{:S(2)}, u32[]{:S(2)}) collective-permute-start(bf16[512,2048]{1,0:T(8,128)(2,1)} %tok_h), channel_id=1, source_target_pairs={{0,4},{4,0},{1,5},{5,1},{2,6},{6,2},{3,7},{7,3},{8,12},{12,8},{9,1... | collective-permute-start | bytes 6291464 | tf_op jit(solution)/shard_map/ppermute | solution.py:40
  7.1 5.4 %collective-permute-start.14 = (bf16[384,128]{1,0:T(8,128)(2,1)S(1)}, bf16[384,128]{1,0:T(8,128)(2,1)S(1)}, u32[]{:S(2)}, u32[]{:S(2)}) collective-permute-start(bf16[384,128]{1,0:T(8,128)(2,1)S(1)} %get-tuple-element.62), channel_id=1, source_target_pairs={{0,16},{8,24},{16,0},{24,8},{1,17},{9,25},{17,1},{25,9},{2,18},{10... | collective-permute-start | bytes 294920 | tf_op jit(solution)/shard_map/ppermute | solution.py:36
  7.6 7.6 %collective-permute-start.13 = (bf16[384,128]{1,0:T(8,128)(2,1)S(1)}, bf16[384,128]{1,0:T(8,128)(2,1)S(1)}, u32[]{:S(2)}, u32[]{:S(2)}) collective-permute-start(bf16[384,128]{1,0:T(8,128)(2,1)S(1)} %get-tuple-element.62), channel_id=1, source_target_pairs={{0,8},{8,16},{16,24},{24,0},{1,9},{9,17},{17,25},{25,1},{2,10},{10... | collective-permute-start | bytes 294920 | tf_op jit(solution)/shard_map/ppermute | solution.py:36
  8.7 10.4 %collective-permute-start.9 = (bf16[384,128]{1,0:T(8,128)(2,1)S(1)}, bf16[384,128]{1,0:T(8,128)(2,1)S(1)}, u32[]{:S(2)}, u32[]{:S(2)}) collective-permute-start(bf16[384,128]{1,0:T(8,128)(2,1)S(1)} %get-tuple-element.61), channel_id=1, source_target_pairs={{0,96},{32,0},{64,32},{96,64},{1,97},{33,1},{65,33},{97,65},{2,98}... | collective-permute-start | bytes 294920 | tf_op jit(solution)/shard_map/ppermute | solution.py:36
  15.3 13.6 %collective-permute-start.18 = (bf16[4,384,128]{2,1,0:T(8,128)(2,1)S(1)}, bf16[4,384,128]{2,1,0:T(8,128)(2,1)S(1)}, u32[]{:S(2)}, u32[]{:S(2)}) collective-permute-start(bf16[4,384,128]{2,1,0:T(8,128)(2,1)S(1)} %pad_maximum_fusion.1.rest_4_), channel_id=1, source_target_pairs={{0,96},{32,0},{64,32},{96,64},{1,97},{33,1},{65,33},{97,65},{2,98}... | collective-permute-start | bytes 1179656 | tf_op jit(solution)/shard_map/ppermute | solution.py:36
  19.1 7.8 %collective-permute-start.7 = (bf16[384,128]{1,0:T(8,128)(2,1)S(1)}, bf16[384,128]{1,0:T(8,128)(2,1)S(1)}, u32[]{:S(2)}, u32[]{:S(2)}) collective-permute-start(bf16[384,128]{1,0:T(8,128)(2,1)S(1)} %get-tuple-element.61), channel_id=1, source_target_pairs={{0,32},{32,64},{64,96},{96,0},{1,33},{33,65},{65,97},{97,1},{2,34}... | collective-permute-start | bytes 294920 | tf_op jit(solution)/shard_map/ppermute | solution.py:36
  24.2 19.7 %collective-permute-start.3 = (bf16[512,768]{1,0:T(8,128)(2,1)}, bf16[512,768]{1,0:T(8,128)(2,1)S(1)}, u32[]{:S(2)}, u32[]{:S(2)}) collective-permute-start(bf16[512,768]{1,0:T(8,128)(2,1)} %gate_h), channel_id=1, source_target_pairs={{0,4},{4,0},{1,5},{5,1},{2,6},{6,2},{3,7},{7,3},{8,12},{12,8},{9,1... | collective-permute-start | bytes 2359304 | tf_op jit(solution)/shard_map/ppermute | solution.py:40
  26.9 18.2 %collective-permute-start.4 = (bf16[512,768]{1,0:T(8,128)(2,1)}, bf16[512,768]{1,0:T(8,128)(2,1)S(1)}, u32[]{:S(2)}, u32[]{:S(2)}) collective-permute-start(bf16[512,768]{1,0:T(8,128)(2,1)} %up_h), channel_id=1, source_target_pairs={{0,4},{4,0},{1,5},{5,1},{2,6},{6,2},{3,7},{7,3},{8,12},{12,8},{9,1... | collective-permute-start | bytes 2359304 | tf_op jit(solution)/shard_map/ppermute | solution.py:40
  28.8 10.5 %collective-permute-start.17 = (bf16[4,384,128]{2,1,0:T(8,128)(2,1)S(1)}, bf16[4,384,128]{2,1,0:T(8,128)(2,1)S(1)}, u32[]{:S(2)}, u32[]{:S(2)}) collective-permute-start(bf16[4,384,128]{2,1,0:T(8,128)(2,1)S(1)} %pad_maximum_fusion.1.rest_4_), channel_id=1, source_target_pairs={{0,64},{32,96},{64,0},{96,32},{1,65},{33,97},{65,1},{97,33},{2,66}... | collective-permute-start | bytes 1179656 | tf_op jit(solution)/shard_map/ppermute | solution.py:36
  39.3 13.9 %collective-permute-start.16 = (bf16[4,384,128]{2,1,0:T(8,128)(2,1)S(1)}, bf16[4,384,128]{2,1,0:T(8,128)(2,1)S(1)}, u32[]{:S(2)}, u32[]{:S(2)}) collective-permute-start(bf16[4,384,128]{2,1,0:T(8,128)(2,1)S(1)} %pad_maximum_fusion.1.rest_4_), channel_id=1, source_target_pairs={{0,32},{32,64},{64,96},{96,0},{1,33},{33,65},{65,97},{97,1},{2,34}... | collective-permute-start | bytes 1179656 | tf_op jit(solution)/shard_map/ppermute | solution.py:36
  43.9 9.5 %collective-permute-start.12 = (bf16[4,384,128]{2,1,0:T(8,128)(2,1)S(1)}, bf16[4,384,128]{2,1,0:T(8,128)(2,1)S(1)}, u32[]{:S(2)}, u32[]{:S(2)}) collective-permute-start(bf16[4,384,128]{2,1,0:T(8,128)(2,1)S(1)} %pad_maximum_fusion.rest_0_), channel_id=1, source_target_pairs={{0,24},{8,0},{16,8},{24,16},{1,25},{9,1},{17,9},{25,17},{2,26},{10... | collective-permute-start | bytes 1179656 | tf_op jit(solution)/shard_map/ppermute | solution.py:36
  45.1 10.9 %collective-permute-start.11 = (bf16[4,384,128]{2,1,0:T(8,128)(2,1)S(1)}, bf16[4,384,128]{2,1,0:T(8,128)(2,1)S(1)}, u32[]{:S(2)}, u32[]{:S(2)}) collective-permute-start(bf16[4,384,128]{2,1,0:T(8,128)(2,1)S(1)} %pad_maximum_fusion.rest_0_), channel_id=1, source_target_pairs={{0,16},{8,24},{16,0},{24,8},{1,17},{9,25},{17,1},{25,9},{2,18},{10... | collective-permute-start | bytes 1179656 | tf_op jit(solution)/shard_map/ppermute | solution.py:36
  45.1 20.5 %collective-permute-start.10 = (bf16[4,384,128]{2,1,0:T(8,128)(2,1)S(1)}, bf16[4,384,128]{2,1,0:T(8,128)(2,1)S(1)}, u32[]{:S(2)}, u32[]{:S(2)}) collective-permute-start(bf16[4,384,128]{2,1,0:T(8,128)(2,1)S(1)} %pad_maximum_fusion.rest_0_), channel_id=1, source_target_pairs={{0,8},{8,16},{16,24},{24,0},{1,9},{9,17},{17,25},{25,1},{2,10},{10... | collective-permute-start | bytes 1179656 | tf_op jit(solution)/shard_map/ppermute | solution.py:36
  53.2 29.7 %collective-permute-start.22 = (bf16[1,192,1024]{2,1,0:T(8,128)(2,1)S(1)}, bf16[1,192,1024]{2,1,0:T(8,128)(2,1)S(1)}, u32[]{:S(2)}, u32[]{:S(2)}) collective-permute-start(bf16[1,192,1024]{2,1,0:T(8,128)(2,1)S(1)} %get-tuple-element.68), channel_id=1, source_target_pairs={{0,32},{32,64},{64,96},{96,0},{1,33},{33,65},{65,97},{97,1},{2,34}... | collective-permute-start | bytes 1179656 | tf_op jit(solution)/shard_map/ppermute | solution.py:36
  53.3 31.5 %collective-permute-start.23 = (bf16[1,192,1024]{2,1,0:T(8,128)(2,1)S(1)}, bf16[1,192,1024]{2,1,0:T(8,128)(2,1)S(1)}, u32[]{:S(2)}, u32[]{:S(2)}) collective-permute-start(bf16[1,192,1024]{2,1,0:T(8,128)(2,1)S(1)} %get-tuple-element.69), channel_id=1, source_target_pairs={{0,96},{32,0},{64,32},{96,64},{1,97},{33,1},{65,33},{97,65},{2,98}... | collective-permute-start | bytes 1179656 | tf_op jit(solution)/shard_map/ppermute | solution.py:36
  79.1 47.3 %collective-permute-start.19 = (bf16[2,192,1024]{2,1,0:T(8,128)(2,1)S(1)}, bf16[2,192,1024]{2,1,0:T(8,128)(2,1)S(1)}, u32[]{:S(2)}, u32[]{:S(2)}) collective-permute-start(bf16[2,192,1024]{2,1,0:T(8,128)(2,1)S(1)} %get-tuple-element.64), channel_id=1, source_target_pairs={{0,32},{32,64},{64,96},{96,0},{1,33},{33,65},{65,97},{97,1},{2,34}... | collective-permute-start | bytes 2359304 | tf_op jit(solution)/shard_map/ppermute | solution.py:36
  79.2 47.2 %collective-permute-start.20 = (bf16[2,192,1024]{2,1,0:T(8,128)(2,1)S(1)}, bf16[2,192,1024]{2,1,0:T(8,128)(2,1)S(1)}, u32[]{:S(2)}, u32[]{:S(2)}) collective-permute-start(bf16[2,192,1024]{2,1,0:T(8,128)(2,1)S(1)} %get-tuple-element.65), channel_id=1, source_target_pairs={{0,96},{32,0},{64,32},{96,64},{1,97},{33,1},{65,33},{97,65},{2,98}... | collective-permute-start | bytes 2359304 | tf_op jit(solution)/shard_map/ppermute | solution.py:36
  81.9 45.8 %collective-permute-start.21 = (bf16[2,192,1024]{2,1,0:T(8,128)(2,1)S(1)}, bf16[2,192,1024]{2,1,0:T(8,128)(2,1)S(1)}, u32[]{:S(2)}, u32[]{:S(2)}) collective-permute-start(bf16[2,192,1024]{2,1,0:T(8,128)(2,1)S(1)} %get-tuple-element.66), channel_id=1, source_target_pairs={{0,64},{32,96},{64,0},{96,32},{1,65},{33,97},{65,1},{97,33},{2,66}... | collective-permute-start | bytes 2359304 | tf_op jit(solution)/shard_map/ppermute | solution.py:36
  83.0 40.8 %collective-permute-start.24 = (bf16[1,192,1024]{2,1,0:T(8,128)(2,1)S(1)}, bf16[1,192,1024]{2,1,0:T(8,128)(2,1)S(1)}, u32[]{:S(2)}, u32[]{:S(2)}) collective-permute-start(bf16[1,192,1024]{2,1,0:T(8,128)(2,1)S(1)} %get-tuple-element.70), channel_id=1, source_target_pairs={{0,64},{32,96},{64,0},{96,32},{1,65},{33,97},{65,1},{97,33},{2,66}... | collective-permute-start | bytes 1179656 | tf_op jit(solution)/shard_map/ppermute | solution.py:36
  84.9 38.9 %collective-permute-start.31 = (bf16[1,192,1024]{2,1,0:T(8,128)(2,1)S(1)}, bf16[1,192,1024]{2,1,0:T(8,128)(2,1)S(1)}, u32[]{:S(2)}, u32[]{:S(2)}) collective-permute-start(bf16[1,192,1024]{2,1,0:T(8,128)(2,1)S(1)} %get-tuple-element.80), channel_id=1, source_target_pairs={{0,8},{8,16},{16,24},{24,0},{1,9},{9,17},{17,25},{25,1},{2,10},{10... | collective-permute-start | bytes 1179656 | tf_op jit(solution)/shard_map/ppermute | solution.py:36
  123.8 53.7 %collective-permute-start.28 = (bf16[2,192,1024]{2,1,0:T(8,128)(2,1)S(1)}, bf16[2,192,1024]{2,1,0:T(8,128)(2,1)S(1)}, u32[]{:S(2)}, u32[]{:S(2)}) collective-permute-start(bf16[2,192,1024]{2,1,0:T(8,128)(2,1)S(1)} %get-tuple-element.76), channel_id=1, source_target_pairs={{0,8},{8,16},{16,24},{24,0},{1,9},{9,17},{17,25},{25,1},{2,10},{10... | collective-permute-start | bytes 2359304 | tf_op jit(solution)/shard_map/ppermute | solution.py:36
  123.8 54.8 %collective-permute-start.29 = (bf16[2,192,1024]{2,1,0:T(8,128)(2,1)S(1)}, bf16[2,192,1024]{2,1,0:T(8,128)(2,1)S(1)}, u32[]{:S(2)}, u32[]{:S(2)}) collective-permute-start(bf16[2,192,1024]{2,1,0:T(8,128)(2,1)S(1)} %get-tuple-element.77), channel_id=1, source_target_pairs={{0,24},{8,0},{16,8},{24,16},{1,25},{9,1},{17,9},{25,17},{2,26},{10... | collective-permute-start | bytes 2359304 | tf_op jit(solution)/shard_map/ppermute | solution.py:36
  126.4 52.1 %collective-permute-start.30 = (bf16[2,192,1024]{2,1,0:T(8,128)(2,1)S(1)}, bf16[2,192,1024]{2,1,0:T(8,128)(2,1)S(1)}, u32[]{:S(2)}, u32[]{:S(2)}) collective-permute-start(bf16[2,192,1024]{2,1,0:T(8,128)(2,1)S(1)} %get-tuple-element.78), channel_id=1, source_target_pairs={{0,16},{8,24},{16,0},{24,8},{1,17},{9,25},{17,1},{25,9},{2,18},{10... | collective-permute-start | bytes 2359304 | tf_op jit(solution)/shard_map/ppermute | solution.py:36
  126.5 40.9 %collective-permute-start.32 = (bf16[1,192,1024]{2,1,0:T(8,128)(2,1)S(1)}, bf16[1,192,1024]{2,1,0:T(8,128)(2,1)S(1)}, u32[]{:S(2)}, u32[]{:S(2)}) collective-permute-start(bf16[1,192,1024]{2,1,0:T(8,128)(2,1)S(1)} %get-tuple-element.81), channel_id=1, source_target_pairs={{0,24},{8,0},{16,8},{24,16},{1,25},{9,1},{17,9},{25,17},{2,26},{10... | collective-permute-start | bytes 1179656 | tf_op jit(solution)/shard_map/ppermute | solution.py:36
  127.6 39.8 %collective-permute-start.33 = (bf16[1,192,1024]{2,1,0:T(8,128)(2,1)S(1)}, bf16[1,192,1024]{2,1,0:T(8,128)(2,1)S(1)}, u32[]{:S(2)}, u32[]{:S(2)}) collective-permute-start(bf16[1,192,1024]{2,1,0:T(8,128)(2,1)S(1)} %get-tuple-element.82), channel_id=1, source_target_pairs={{0,16},{8,24},{16,0},{24,8},{1,17},{9,25},{17,1},{25,9},{2,18},{10... | collective-permute-start | bytes 1179656 | tf_op jit(solution)/shard_map/ppermute | solution.py:36
  167.4 15.1 %collective-permute-start.25 = (bf16[3,48,1024]{2,1,0:T(8,128)(2,1)S(1)}, bf16[3,48,1024]{2,1,0:T(8,128)(2,1)S(1)}, u32[]{:S(2)}, u32[]{:S(2)}) collective-permute-start(bf16[3,48,1024]{2,1,0:T(8,128)(2,1)S(1)} %get-tuple-element.72), channel_id=1, source_target_pairs={{0,8},{8,16},{16,24},{24,0},{1,9},{9,17},{17,25},{25,1},{2,10},{10... | collective-permute-start | bytes 884744 | tf_op jit(solution)/shard_map/ppermute | solution.py:36
  167.4 15.7 %collective-permute-start.26 = (bf16[3,48,1024]{2,1,0:T(8,128)(2,1)S(1)}, bf16[3,48,1024]{2,1,0:T(8,128)(2,1)S(1)}, u32[]{:S(2)}, u32[]{:S(2)}) collective-permute-start(bf16[3,48,1024]{2,1,0:T(8,128)(2,1)S(1)} %get-tuple-element.73), channel_id=1, source_target_pairs={{0,24},{8,0},{16,8},{24,16},{1,25},{9,1},{17,9},{25,17},{2,26},{10... | collective-permute-start | bytes 884744 | tf_op jit(solution)/shard_map/ppermute | solution.py:36
  177.4 8.0 %collective-permute-start.27 = (bf16[3,48,1024]{2,1,0:T(8,128)(2,1)S(1)}, bf16[3,48,1024]{2,1,0:T(8,128)(2,1)S(1)}, u32[]{:S(2)}, u32[]{:S(2)}) collective-permute-start(bf16[3,48,1024]{2,1,0:T(8,128)(2,1)S(1)} %get-tuple-element.74), channel_id=1, source_target_pairs={{0,16},{8,24},{16,0},{24,8},{1,17},{9,25},{17,1},{25,9},{2,18},{10... | collective-permute-start | bytes 884744 | tf_op jit(solution)/shard_map/ppermute | solution.py:36
  179.7 7.1 %collective-permute-start.34 = (bf16[3,48,1024]{2,1,0:T(8,128)(2,1)S(1)}, bf16[3,48,1024]{2,1,0:T(8,128)(2,1)S(1)}, u32[]{:S(2)}, u32[]{:S(2)}) collective-permute-start(bf16[3,48,1024]{2,1,0:T(8,128)(2,1)S(1)} %get-tuple-element.84), channel_id=1, source_target_pairs={{0,32},{32,64},{64,96},{96,0},{1,33},{33,65},{65,97},{97,1},{2,34}... | collective-permute-start | bytes 884744 | tf_op jit(solution)/shard_map/ppermute | solution.py:36
  180.4 9.3 %collective-permute-start.35 = (bf16[3,48,1024]{2,1,0:T(8,128)(2,1)S(1)}, bf16[3,48,1024]{2,1,0:T(8,128)(2,1)S(1)}, u32[]{:S(2)}, u32[]{:S(2)}) collective-permute-start(bf16[3,48,1024]{2,1,0:T(8,128)(2,1)S(1)} %get-tuple-element.85), channel_id=1, source_target_pairs={{0,96},{32,0},{64,32},{96,64},{1,97},{33,1},{65,33},{97,65},{2,98}... | collective-permute-start | bytes 884744 | tf_op jit(solution)/shard_map/ppermute | solution.py:36
  182.5 9.1 %collective-permute-start.36 = (bf16[3,48,1024]{2,1,0:T(8,128)(2,1)S(1)}, bf16[3,48,1024]{2,1,0:T(8,128)(2,1)S(1)}, u32[]{:S(2)}, u32[]{:S(2)}) collective-permute-start(bf16[3,48,1024]{2,1,0:T(8,128)(2,1)S(1)} %get-tuple-element.86), channel_id=1, source_target_pairs={{0,64},{32,96},{64,0},{96,32},{1,65},{33,97},{65,1},{97,33},{2,66}... | collective-permute-start | bytes 884744 | tf_op jit(solution)/shard_map/ppermute | solution.py:36
  192.6 6.0 %collective-permute-start.37 = (bf16[2,48,1024]{2,1,0:T(8,128)(2,1)S(1)}, bf16[2,48,1024]{2,1,0:T(8,128)(2,1)S(1)}, u32[]{:S(2)}, u32[]{:S(2)}) collective-permute-start(bf16[2,48,1024]{2,1,0:T(8,128)(2,1)S(1)} %get-tuple-element.88), channel_id=1, source_target_pairs={{0,1},{1,2},{2,3},{3,0},{4,5},{5,6},{6,7},{7,4},{8,9},{9,10},{10,1... | collective-permute-start | bytes 589832 | tf_op jit(solution)/shard_map/ppermute | solution.py:36
  194.1 6.2 %collective-permute-start.38 = (bf16[2,48,1024]{2,1,0:T(8,128)(2,1)S(1)}, bf16[2,48,1024]{2,1,0:T(8,128)(2,1)S(1)}, u32[]{:S(2)}, u32[]{:S(2)}) collective-permute-start(bf16[2,48,1024]{2,1,0:T(8,128)(2,1)S(1)} %get-tuple-element.89), channel_id=1, source_target_pairs={{0,3},{1,0},{2,1},{3,2},{4,7},{5,4},{6,5},{7,6},{8,11},{9,8},{10,9... | collective-permute-start | bytes 589832 | tf_op jit(solution)/shard_map/ppermute | solution.py:36
  195.6 6.3 %collective-permute-start.39 = (bf16[2,48,1024]{2,1,0:T(8,128)(2,1)S(1)}, bf16[2,48,1024]{2,1,0:T(8,128)(2,1)S(1)}, u32[]{:S(2)}, u32[]{:S(2)}) collective-permute-start(bf16[2,48,1024]{2,1,0:T(8,128)(2,1)S(1)} %get-tuple-element.90), channel_id=1, source_target_pairs={{0,2},{1,3},{2,0},{3,1},{4,6},{5,7},{6,4},{7,5},{8,10},{9,11},{10,... | collective-permute-start | bytes 589832 | tf_op jit(solution)/shard_map/ppermute | solution.py:36
  210.0 14.2 %collective-permute-start.45 = (bf16[4,48,1024]{2,1,0:T(8,128)(2,1)S(1)}, bf16[4,48,1024]{2,1,0:T(8,128)(2,1)S(1)}, u32[]{:S(2)}, u32[]{:S(2)}) collective-permute-start(bf16[4,48,1024]{2,1,0:T(8,128)(2,1)S(1)} %pad_maximum_fusion.2.rest_0_), channel_id=1, source_target_pairs={{0,96},{32,0},{64,32},{96,64},{1,97},{33,1},{65,33},{97,65},{2,98}... | collective-permute-start | bytes 1179656 | tf_op jit(solution)/shard_map/ppermute | solution.py:36
  211.0 6.7 %collective-permute-start.48 = (bf16[48,1024]{1,0:T(8,128)(2,1)S(1)}, bf16[48,1024]{1,0:T(8,128)(2,1)S(1)}, u32[]{:S(2)}, u32[]{:S(2)}) collective-permute-start(bf16[48,1024]{1,0:T(8,128)(2,1)S(1)} %get-tuple-element.94), channel_id=1, source_target_pairs={{0,96},{32,0},{64,32},{96,64},{1,97},{33,1},{65,33},{97,65},{2,98}... | collective-permute-start | bytes 294920 | tf_op jit(solution)/shard_map/ppermute | solution.py:36
  211.1 12.9 %collective-permute-start.47 = (bf16[48,1024]{1,0:T(8,128)(2,1)S(1)}, bf16[48,1024]{1,0:T(8,128)(2,1)S(1)}, u32[]{:S(2)}, u32[]{:S(2)}) collective-permute-start(bf16[48,1024]{1,0:T(8,128)(2,1)S(1)} %get-tuple-element.94), channel_id=1, source_target_pairs={{0,64},{32,96},{64,0},{96,32},{1,65},{33,97},{65,1},{97,33},{2,66}... | collective-permute-start | bytes 294920 | tf_op jit(solution)/shard_map/ppermute | solution.py:36
  213.3 10.7 %collective-permute-start.46 = (bf16[48,1024]{1,0:T(8,128)(2,1)S(1)}, bf16[48,1024]{1,0:T(8,128)(2,1)S(1)}, u32[]{:S(2)}, u32[]{:S(2)}) collective-permute-start(bf16[48,1024]{1,0:T(8,128)(2,1)S(1)} %get-tuple-element.94), channel_id=1, source_target_pairs={{0,32},{32,64},{64,96},{96,0},{1,33},{33,65},{65,97},{97,1},{2,34}... | collective-permute-start | bytes 294920 | tf_op jit(solution)/shard_map/ppermute | solution.py:36
  213.3 12.3 %collective-permute-start.44 = (bf16[4,48,1024]{2,1,0:T(8,128)(2,1)S(1)}, bf16[4,48,1024]{2,1,0:T(8,128)(2,1)S(1)}, u32[]{:S(2)}, u32[]{:S(2)}) collective-permute-start(bf16[4,48,1024]{2,1,0:T(8,128)(2,1)S(1)} %pad_maximum_fusion.2.rest_0_), channel_id=1, source_target_pairs={{0,64},{32,96},{64,0},{96,32},{1,65},{33,97},{65,1},{97,33},{2,66}... | collective-permute-start | bytes 1179656 | tf_op jit(solution)/shard_map/ppermute | solution.py:36
  217.7 13.0 %collective-permute-start.43 = (bf16[4,48,1024]{2,1,0:T(8,128)(2,1)S(1)}, bf16[4,48,1024]{2,1,0:T(8,128)(2,1)S(1)}, u32[]{:S(2)}, u32[]{:S(2)}) collective-permute-start(bf16[4,48,1024]{2,1,0:T(8,128)(2,1)S(1)} %pad_maximum_fusion.2.rest_0_), channel_id=1, source_target_pairs={{0,32},{32,64},{64,96},{96,0},{1,33},{33,65},{65,97},{97,1},{2,34}... | collective-permute-start | bytes 1179656 | tf_op jit(solution)/shard_map/ppermute | solution.py:36
  224.0 8.4 %collective-permute-start.51 = (bf16[4,48,1024]{2,1,0:T(8,128)(2,1)S(1)}, bf16[4,48,1024]{2,1,0:T(8,128)(2,1)S(1)}, u32[]{:S(2)}, u32[]{:S(2)}) collective-permute-start(bf16[4,48,1024]{2,1,0:T(8,128)(2,1)S(1)} %pad_maximum_fusion.3.rest_0_), channel_id=1, source_target_pairs={{0,24},{8,0},{16,8},{24,16},{1,25},{9,1},{17,9},{25,17},{2,26},{10... | collective-permute-start | bytes 1179656 | tf_op jit(solution)/shard_map/ppermute | solution.py:36
  224.1 8.5 %collective-permute-start.50 = (bf16[4,48,1024]{2,1,0:T(8,128)(2,1)S(1)}, bf16[4,48,1024]{2,1,0:T(8,128)(2,1)S(1)}, u32[]{:S(2)}, u32[]{:S(2)}) collective-permute-start(bf16[4,48,1024]{2,1,0:T(8,128)(2,1)S(1)} %pad_maximum_fusion.3.rest_0_), channel_id=1, source_target_pairs={{0,16},{8,24},{16,0},{24,8},{1,17},{9,25},{17,1},{25,9},{2,18},{10... | collective-permute-start | bytes 1179656 | tf_op jit(solution)/shard_map/ppermute | solution.py:36
  224.2 12.3 %collective-permute-start.49 = (bf16[4,48,1024]{2,1,0:T(8,128)(2,1)S(1)}, bf16[4,48,1024]{2,1,0:T(8,128)(2,1)S(1)}, u32[]{:S(2)}, u32[]{:S(2)}) collective-permute-start(bf16[4,48,1024]{2,1,0:T(8,128)(2,1)S(1)} %pad_maximum_fusion.3.rest_0_), channel_id=1, source_target_pairs={{0,8},{8,16},{16,24},{24,0},{1,9},{9,17},{17,25},{25,1},{2,10},{10... | collective-permute-start | bytes 1179656 | tf_op jit(solution)/shard_map/ppermute | solution.py:36
  243.1 13.3 %collective-permute-start.52 = (bf16[64,768]{1,0:T(8,128)(2,1)S(1)}, bf16[64,768]{1,0:T(8,128)(2,1)S(1)}, u32[]{:S(2)}, u32[]{:S(2)}) collective-permute-start(bf16[64,768]{1,0:T(8,128)(2,1)S(1)} %get-tuple-element.96), channel_id=1, source_target_pairs={{0,4},{4,0},{1,5},{5,1},{2,6},{6,2},{3,7},{7,3},{8,12},{12,8},{9,1... | collective-permute-start | bytes 294920 | tf_op jit(solution)/shard_map/ppermute | solution.py:40
  257.0 6.2 %collective-permute-start.55 = (bf16[2,64,768]{2,1,0:T(8,128)(2,1)S(1)}, bf16[2,64,768]{2,1,0:T(8,128)(2,1)S(1)}, u32[]{:S(2)}, u32[]{:S(2)}) collective-permute-start(bf16[2,64,768]{2,1,0:T(8,128)(2,1)S(1)} %shard_map.82.rest_0_), channel_id=1, source_target_pairs={{0,3},{1,0},{2,1},{3,2},{4,7},{5,4},{6,5},{7,6},{8,11},{9,8},{10,9... | collective-permute-start | bytes 589832 | tf_op jit(solution)/shard_map/ppermute | solution.py:36
  258.6 7.4 %collective-permute-start.54 = (bf16[2,64,768]{2,1,0:T(8,128)(2,1)S(1)}, bf16[2,64,768]{2,1,0:T(8,128)(2,1)S(1)}, u32[]{:S(2)}, u32[]{:S(2)}) collective-permute-start(bf16[2,64,768]{2,1,0:T(8,128)(2,1)S(1)} %shard_map.82.rest_0_), channel_id=1, source_target_pairs={{0,2},{1,3},{2,0},{3,1},{4,6},{5,7},{6,4},{7,5},{8,10},{9,11},{10,... | collective-permute-start | bytes 589832 | tf_op jit(solution)/shard_map/ppermute | solution.py:36
  259.7 11.5 %collective-permute-start.53 = (bf16[2,64,768]{2,1,0:T(8,128)(2,1)S(1)}, bf16[2,64,768]{2,1,0:T(8,128)(2,1)S(1)}, u32[]{:S(2)}, u32[]{:S(2)}) collective-permute-start(bf16[2,64,768]{2,1,0:T(8,128)(2,1)S(1)} %shard_map.82.rest_0_), channel_id=1, source_target_pairs={{0,1},{1,2},{2,3},{3,0},{4,5},{5,6},{6,7},{7,4},{8,9},{9,10},{10,1... | collective-permute-start | bytes 589832 | tf_op jit(solution)/shard_map/ppermute | solution.py:36
  (10 other events, 122.9 us)

commit v3 on v2

--- a/solution.py
+++ b/solution.py
@@ -97,8 +97,8 @@
     def factors(gate_ref, up_ref, count, expert, base):
         def block(i, carry):
             rows = pl.ds(pl.multiple_of(i * BLOCK, BLOCK), BLOCK)
-            gate = gate_ref[rows, :].astype(f32).T
-            up = up_ref[rows, :].astype(f32).T
+            gate = gate_ref[rows, :].T.astype(f32)
+            up = up_ref[rows, :].T.astype(f32)
             limit = jnp.where(expert[i] == info[2], count[i], 0)
             live = lax.broadcasted_iota(jnp.int32, (F, BLOCK), 1) < limit
             sig = jax.nn.sigmoid(gate)
@@ -124,7 +124,7 @@
 def grads_kernel(info, cot_h, tok_h, for_gate, for_up, cot_b, tok_b, *rest):
     weights, outs, (cot_a, tok_a, whole, left, acc, sems) = rest[:8], rest[8:16], rest[16:]
     rows = BLK * BLOCK
-    part = rows // 2
+    part = rows
     halves = F // 2
     copies = [
         pltpu.make_async_copy(source, target, sems.at[i])

time: 273 us -> 273 us (level)
  no operation moved by 1% of the time
where the time goes in v3:
time: 273 us
  waiting for transfers between devices  146 us (53%)
  starting transfers between devices  89.4 us (33%)
  Pallas kernels  35.5 us (13%)
    ppermute x48, waiting for transfers between devices, shift(): lax.ppermute(value, axis, [(i, (i + by) % RING) for i in range(RING)])  145 us
    ppermute x48, starting transfers between devices, shift(): lax.ppermute(value, axis, [(i, (i + by) % RING) for i in range(RING)])  71.1 us
    pallas_call x11, Pallas kernels, call(): pl.pallas_call(kernel, in_specs=[pl.BlockSpec(memory_space=pltpu.SMEM)] *...  35.5 us
    ppermute x8, starting transfers between devices, swap(): return lax.ppermute(value, 'dp_2', [(0, 1), (1, 0)])  18.3 us
  transfers between devices with their start and end apart: 56, of which 27 were waited for; matrix products, arithmetic and copies ran while one was open for 0% of the time, Pallas kernels for 9%

profile of v3, /device:TPU:1, one launch (start us, length us, event | category | flops | bytes accessed | tf_op | source)
XLA Modules:
  0.0 272.5 jit_solution(4183376151260231011)
XLA Ops:
  0.0 1.4 collective-permute-start.2
  4.5 2.6 collective-permute-start.15
  8.7 3.8 %collective-permute-start.9 = (bf16[384,128]{1,0:T(8,128)(2,1)S(1)}, bf16[384,128]{1,0:T(8,128)(2,1)S(1)}, u32[]{:S(2)}, u32[]{:S(2)}) collective-permute-start(bf16[384,128]{1,0:T(8,128)(2,1)S(1)} %get-tuple-element.61), channel_id=1, source_target_pairs={{0,96},{32,0},{64,32},{96,64},{1,97},{33,1},{65,33},{97,65},{2,98}... | collective-permute-start | bytes 294920 | tf_op jit(solution)/shard_map/ppermute | solution.py:36
  12.5 2.7 collective-permute-done.13
  15.3 3.8 %collective-permute-start.18 = (bf16[4,384,128]{2,1,0:T(8,128)(2,1)S(1)}, bf16[4,384,128]{2,1,0:T(8,128)(2,1)S(1)}, u32[]{:S(2)}, u32[]{:S(2)}) collective-permute-start(bf16[4,384,128]{2,1,0:T(8,128)(2,1)S(1)} %pad_maximum_fusion.1.rest_4_), channel_id=1, source_target_pairs={{0,96},{32,0},{64,32},{96,64},{1,97},{33,1},{65,33},{97,65},{2,98}... | collective-permute-start | bytes 1179656 | tf_op jit(solution)/shard_map/ppermute | solution.py:36
  19.8 4.4 %collective-permute-done.8 = bf16[384,128]{1,0:T(8,128)(2,1)S(1)} collective-permute-done((bf16[384,128]{1,0:T(8,128)(2,1)S(1)}, bf16[384,128]{1,0:T(8,128)(2,1)S(1)}, u32[]{:S(2)}, u32[]{:S(2)}) %collective-permute-start.8) | collective-permute-done | bytes 98336 | tf_op jit(solution)/shard_map/ppermute | solution.py:36
  24.2 2.7 %collective-permute-start.3 = (bf16[512,768]{1,0:T(8,128)(2,1)}, bf16[512,768]{1,0:T(8,128)(2,1)S(1)}, u32[]{:S(2)}, u32[]{:S(2)}) collective-permute-start(bf16[512,768]{1,0:T(8,128)(2,1)} %gate_h), channel_id=1, source_target_pairs={{0,4},{4,0},{1,5},{5,1},{2,6},{6,2},{3,7},{7,3},{8,12},{12,8},{9,1... | collective-permute-start | bytes 2359304 | tf_op jit(solution)/shard_map/ppermute | solution.py:40
  28.9 10.4 %collective-permute-done.17.rest_6_ = bf16[4,384,128]{2,1,0:T(8,128)(2,1)S(1)} collective-permute-done((bf16[4,384,128]{2,1,0:T(8,128)(2,1)S(1)}, bf16[4,384,128]{2,1,0:T(8,128)(2,1)S(1)}, u32[]{:S(2)}, u32[]{:S(2)}) %collective-permute-start.17) | collective-permute-done | bytes 393248 | tf_op jit(solution)/shard_map/ppermute | solution.py:36
  39.3 4.5 %collective-permute-start.16 = (bf16[4,384,128]{2,1,0:T(8,128)(2,1)S(1)}, bf16[4,384,128]{2,1,0:T(8,128)(2,1)S(1)}, u32[]{:S(2)}, u32[]{:S(2)}) collective-permute-start(bf16[4,384,128]{2,1,0:T(8,128)(2,1)S(1)} %pad_maximum_fusion.1.rest_4_), channel_id=1, source_target_pairs={{0,32},{32,64},{64,96},{96,0},{1,33},{33,65},{65,97},{97,1},{2,34}... | collective-permute-start | bytes 1179656 | tf_op jit(solution)/shard_map/ppermute | solution.py:36
  45.8 7.3 %shard_map.74 = (bf16[1,192,1024]{2,1,0:T(8,128)(2,1)S(1)}, bf16[1,192,1024]{2,1,0:T(8,128)(2,1)S(1)}, bf16[1,192,1024]{2,1,0:T(8,128)(2,1)S(1)}, bf16[1,192,102...) custom-call(s32[4]{0:T(128)S(1)} %pad_add_fusion.info, ...), custom_call_target="tpu_custom_call" | custom-call | flops 3221225472 | bytes 6442450 | tf_op jit(solution)/shard_map/pallas_call | solution.py:319
  53.2 2.7 collective-permute-start.23
  55.9 9.8 %collective-permute-done.10.rest_1_ = bf16[4,384,128]{2,1,0:T(8,128)(2,1)S(1)} collective-permute-done((bf16[4,384,128]{2,1,0:T(8,128)(2,1)S(1)}, bf16[4,384,128]{2,1,0:T(8,128)(2,1)S(1)}, u32[]{:S(2)}, u32[]{:S(2)}) %collective-permute-start.10) | collective-permute-done | bytes 393248 | tf_op jit(solution)/shard_map/ppermute | solution.py:36
  65.6 13.1 %shard_map.75 = (bf16[2,192,1024]{2,1,0:T(8,128)(2,1)S(1)}, bf16[2,192,1024]{2,1,0:T(8,128)(2,1)S(1)}, bf16[2,192,1024]{2,1,0:T(8,128)(2,1)S(1)}, bf16[2,192,102...) custom-call(s32[4]{0:T(128)S(1)} %pad_add_fusion.info, ...), custom_call_target="tpu_custom_call" | custom-call | flops 9663676416 | bytes 19327352 | tf_op jit(solution)/shard_map/pallas_call | solution.py:319
  78.9 2.7 collective-permute-start.20
  82.6 1.9 collective-permute-start.24
  84.5 38.9 %collective-permute-done.24.rest_7_ = bf16[1,192,1024]{2,1,0:T(8,128)(2,1)S(1)} collective-permute-done((bf16[1,192,1024]{2,1,0:T(8,128)(2,1)S(1)}, bf16[1,192,1024]{2,1,0:T(8,128)(2,1)S(1)}, u32[]{:S(2)}, u32[]{:S(2)}) %collective-permute-start.24) | collective-permute-done | bytes 393248 | tf_op jit(solution)/shard_map/ppermute | solution.py:36
  123.4 2.7 collective-permute-start.29
  127.3 1.9 collective-permute-start.33
  130.3 36.7 %collective-permute-done.32.rest_6_ = bf16[1,192,1024]{2,1,0:T(8,128)(2,1)S(1)} collective-permute-done((bf16[1,192,1024]{2,1,0:T(8,128)(2,1)S(1)}, bf16[1,192,1024]{2,1,0:T(8,128)(2,1)S(1)}, u32[]{:S(2)}, u32[]{:S(2)}) %collective-permute-start.32) | collective-permute-done | bytes 393248 | tf_op jit(solution)/shard_map/ppermute | solution.py:36
  167.0 10.0 %collective-permute-start.26 = (bf16[3,48,1024]{2,1,0:T(8,128)(2,1)S(1)}, bf16[3,48,1024]{2,1,0:T(8,128)(2,1)S(1)}, u32[]{:S(2)}, u32[]{:S(2)}) collective-permute-start(bf16[3,48,1024]{2,1,0:T(8,128)(2,1)S(1)} %get-tuple-element.73), channel_id=1, source_target_pairs={{0,24},{8,0},{16,8},{24,16},{1,25},{9,1},{17,9},{25,17},{2,26},{10... | collective-permute-start | bytes 884744 | tf_op jit(solution)/shard_map/ppermute | solution.py:36
  180.0 2.1 collective-permute-start.35
  182.6 2.4 collective-permute-done.27.rest_3_
  185.0 1.5 collective-permute-done.34.rest_5_
  186.5 2.8 %collective-permute-done.35.rest_6_ = bf16[3,48,1024]{2,1,0:T(8,128)(2,1)S(1)} collective-permute-done((bf16[3,48,1024]{2,1,0:T(8,128)(2,1)S(1)}, bf16[3,48,1024]{2,1,0:T(8,128)(2,1)S(1)}, u32[]{:S(2)}, u32[]{:S(2)}) %collective-permute-start.35) | collective-permute-done | bytes 294944 | tf_op jit(solution)/shard_map/ppermute | solution.py:36
  189.2 1.9 collective-permute-done.36.rest_7_
  192.1 1.4 collective-permute-start.37
  193.5 1.6 collective-permute-start.38
  195.1 1.6 collective-permute-start.39
  196.7 1.4 collective-permute-done.37.rest_1_
  198.1 1.7 collective-permute-done.38.rest_2_
  199.8 1.5 collective-permute-done.39.rest_3_
  202.0 1.4 collective-permute-start.42
  205.6 2.9 %collective-permute-done.41 = bf16[48,1024]{1,0:T(8,128)(2,1)S(1)} collective-permute-done((bf16[48,1024]{1,0:T(8,128)(2,1)S(1)}, bf16[48,1024]{1,0:T(8,128)(2,1)S(1)}, u32[]{:S(2)}, u32[]{:S(2)}) %collective-permute-start.41) | collective-permute-done | bytes 98336 | tf_op jit(solution)/shard_map/ppermute | solution.py:36
  210.6 2.2 collective-permute-start.47
  212.8 2.7 collective-permute-start.44
  215.5 1.7 collective-permute-done.48
  217.2 6.2 %collective-permute-start.43 = (bf16[4,48,1024]{2,1,0:T(8,128)(2,1)S(1)}, bf16[4,48,1024]{2,1,0:T(8,128)(2,1)S(1)}, u32[]{:S(2)}, u32[]{:S(2)}) collective-permute-start(bf16[4,48,1024]{2,1,0:T(8,128)(2,1)S(1)} %pad_maximum_fusion.2.rest_0_), channel_id=1, source_target_pairs={{0,32},{32,64},{64,96},{96,0},{1,33},{33,65},{65,97},{97,1},{2,34}... | collective-permute-start | bytes 1179656 | tf_op jit(solution)/shard_map/ppermute | solution.py:36
  223.7 1.4 collective-permute-start.49
  225.0 5.0 %collective-permute-done.43.rest_1_ = bf16[4,48,1024]{2,1,0:T(8,128)(2,1)S(1)} collective-permute-done((bf16[4,48,1024]{2,1,0:T(8,128)(2,1)S(1)}, bf16[4,48,1024]{2,1,0:T(8,128)(2,1)S(1)}, u32[]{:S(2)}, u32[]{:S(2)}) %collective-permute-start.43) | collective-permute-done | bytes 393248 | tf_op jit(solution)/shard_map/ppermute | solution.py:36
  230.0 1.7 shard_map.80
  232.1 3.9 %collective-permute-done.49.rest_1_ = bf16[4,48,1024]{2,1,0:T(8,128)(2,1)S(1)} collective-permute-done((bf16[4,48,1024]{2,1,0:T(8,128)(2,1)S(1)}, bf16[4,48,1024]{2,1,0:T(8,128)(2,1)S(1)}, u32[]{:S(2)}, u32[]{:S(2)}) %collective-permute-start.49) | collective-permute-done | bytes 393248 | tf_op jit(solution)/shard_map/ppermute | solution.py:36
  236.0 6.8 %shard_map.81 = (bf16[64,768]{1,0:T(8,128)(2,1)S(1)}, bf16[64,768]{1,0:T(8,128)(2,1)S(1)}) custom-call(s32[4]{0:T(128)S(1)} %pad_add_fusion.info, f32[768,768]{1,0:T(8,128)S(1)} %get-tuple-element.92.raw_first, bf16[768,1024]{1,0:T(8,128)(2,1)S(1)} %get-tuple-element.93.first_half, bf16[4,48,1024]{2,1,0:T(8,128)(2,1)S(1)} %pad_maximum_fusion.3.rest_0_, ...), custom_call_target="tpu_custom_call" | custom-call | flops 3623878656 | bytes 7247757 | tf_op jit(solution)/shard_map/pallas_call | solution.py:319
  242.8 12.4 %collective-permute-start.52 = (bf16[64,768]{1,0:T(8,128)(2,1)S(1)}, bf16[64,768]{1,0:T(8,128)(2,1)S(1)}, u32[]{:S(2)}, u32[]{:S(2)}) collective-permute-start(bf16[64,768]{1,0:T(8,128)(2,1)S(1)} %get-tuple-element.96), channel_id=1, source_target_pairs={{0,4},{4,0},{1,5},{5,1},{2,6},{6,2},{3,7},{7,3},{8,12},{12,8},{9,1... | collective-permute-start | bytes 294920 | tf_op jit(solution)/shard_map/ppermute | solution.py:40
  256.7 1.6 collective-permute-start.55
  259.4 3.4 %collective-permute-done.55.rest_3_ = bf16[2,64,768]{2,1,0:T(8,128)(2,1)S(1)} collective-permute-done((bf16[2,64,768]{2,1,0:T(8,128)(2,1)S(1)}, bf16[2,64,768]{2,1,0:T(8,128)(2,1)S(1)}, u32[]{:S(2)}, u32[]{:S(2)}) %collective-permute-start.55) | collective-permute-done | bytes 196640 | tf_op jit(solution)/shard_map/ppermute | solution.py:36
  262.9 2.8 %collective-permute-done.54.rest_2_ = bf16[2,64,768]{2,1,0:T(8,128)(2,1)S(1)} collective-permute-done((bf16[2,64,768]{2,1,0:T(8,128)(2,1)S(1)}, bf16[2,64,768]{2,1,0:T(8,128)(2,1)S(1)}, u32[]{:S(2)}, u32[]{:S(2)}) %collective-permute-start.54) | collective-permute-done | bytes 196640 | tf_op jit(solution)/shard_map/ppermute | solution.py:36
  265.7 5.2 %collective-permute-done.53.rest_1_ = bf16[2,64,768]{2,1,0:T(8,128)(2,1)S(1)} collective-permute-done((bf16[2,64,768]{2,1,0:T(8,128)(2,1)S(1)}, bf16[2,64,768]{2,1,0:T(8,128)(2,1)S(1)}, u32[]{:S(2)}, u32[]{:S(2)}) %collective-permute-start.53) | collective-permute-done | bytes 196640 | tf_op jit(solution)/shard_map/ppermute | solution.py:36
  270.9 1.4 shard_map.83
  (85 shorter events, 25.6 us)
Async XLA Ops:
  3.9 41.2 %collective-permute-start.5 = (bf16[512,2048]{1,0:T(8,128)(2,1)}, bf16[512,2048]{1,0:T(8,128)(2,1)S(1)}, u32[]{:S(2)}, u32[]{:S(2)}) collective-permute-start(bf16[512,2048]{1,0:T(8,128)(2,1)} %cot_h.1), channel_id=1, source_target_pairs={{0,4},{4,0},{1,5},{5,1},{2,6},{6,2},{3,7},{7,3},{8,12},{12,8},{9,1... | collective-permute-start | bytes 6291464 | tf_op jit(solution)/shard_map/ppermute | solution.py:40
  4.4 61.3 %collective-permute-start.6 = (bf16[512,2048]{1,0:T(8,128)(2,1)}, bf16[512,2048]{1,0:T(8,128)(2,1)S(1)}, u32[]{:S(2)}, u32[]{:S(2)}) collective-permute-start(bf16[512,2048]{1,0:T(8,128)(2,1)} %tok_h), channel_id=1, source_target_pairs={{0,4},{4,0},{1,5},{5,1},{2,6},{6,2},{3,7},{7,3},{8,12},{12,8},{9,1... | collective-permute-start | bytes 6291464 | tf_op jit(solution)/shard_map/ppermute | solution.py:40
  7.1 5.4 %collective-permute-start.14 = (bf16[384,128]{1,0:T(8,128)(2,1)S(1)}, bf16[384,128]{1,0:T(8,128)(2,1)S(1)}, u32[]{:S(2)}, u32[]{:S(2)}) collective-permute-start(bf16[384,128]{1,0:T(8,128)(2,1)S(1)} %get-tuple-element.62), channel_id=1, source_target_pairs={{0,16},{8,24},{16,0},{24,8},{1,17},{9,25},{17,1},{25,9},{2,18},{10... | collective-permute-start | bytes 294920 | tf_op jit(solution)/shard_map/ppermute | solution.py:36
  7.6 7.6 %collective-permute-start.13 = (bf16[384,128]{1,0:T(8,128)(2,1)S(1)}, bf16[384,128]{1,0:T(8,128)(2,1)S(1)}, u32[]{:S(2)}, u32[]{:S(2)}) collective-permute-start(bf16[384,128]{1,0:T(8,128)(2,1)S(1)} %get-tuple-element.62), channel_id=1, source_target_pairs={{0,8},{8,16},{16,24},{24,0},{1,9},{9,17},{17,25},{25,1},{2,10},{10... | collective-permute-start | bytes 294920 | tf_op jit(solution)/shard_map/ppermute | solution.py:36
  8.7 10.4 %collective-permute-start.9 = (bf16[384,128]{1,0:T(8,128)(2,1)S(1)}, bf16[384,128]{1,0:T(8,128)(2,1)S(1)}, u32[]{:S(2)}, u32[]{:S(2)}) collective-permute-start(bf16[384,128]{1,0:T(8,128)(2,1)S(1)} %get-tuple-element.61), channel_id=1, source_target_pairs={{0,96},{32,0},{64,32},{96,64},{1,97},{33,1},{65,33},{97,65},{2,98}... | collective-permute-start | bytes 294920 | tf_op jit(solution)/shard_map/ppermute | solution.py:36
  15.3 13.6 %collective-permute-start.18 = (bf16[4,384,128]{2,1,0:T(8,128)(2,1)S(1)}, bf16[4,384,128]{2,1,0:T(8,128)(2,1)S(1)}, u32[]{:S(2)}, u32[]{:S(2)}) collective-permute-start(bf16[4,384,128]{2,1,0:T(8,128)(2,1)S(1)} %pad_maximum_fusion.1.rest_4_), channel_id=1, source_target_pairs={{0,96},{32,0},{64,32},{96,64},{1,97},{33,1},{65,33},{97,65},{2,98}... | collective-permute-start | bytes 1179656 | tf_op jit(solution)/shard_map/ppermute | solution.py:36
  19.1 7.8 %collective-permute-start.7 = (bf16[384,128]{1,0:T(8,128)(2,1)S(1)}, bf16[384,128]{1,0:T(8,128)(2,1)S(1)}, u32[]{:S(2)}, u32[]{:S(2)}) collective-permute-start(bf16[384,128]{1,0:T(8,128)(2,1)S(1)} %get-tuple-element.61), channel_id=1, source_target_pairs={{0,32},{32,64},{64,96},{96,0},{1,33},{33,65},{65,97},{97,1},{2,34}... | collective-permute-start | bytes 294920 | tf_op jit(solution)/shard_map/ppermute | solution.py:36
  24.2 19.7 %collective-permute-start.3 = (bf16[512,768]{1,0:T(8,128)(2,1)}, bf16[512,768]{1,0:T(8,128)(2,1)S(1)}, u32[]{:S(2)}, u32[]{:S(2)}) collective-permute-start(bf16[512,768]{1,0:T(8,128)(2,1)} %gate_h), channel_id=1, source_target_pairs={{0,4},{4,0},{1,5},{5,1},{2,6},{6,2},{3,7},{7,3},{8,12},{12,8},{9,1... | collective-permute-start | bytes 2359304 | tf_op jit(solution)/shard_map/ppermute | solution.py:40
  26.9 18.2 %collective-permute-start.4 = (bf16[512,768]{1,0:T(8,128)(2,1)}, bf16[512,768]{1,0:T(8,128)(2,1)S(1)}, u32[]{:S(2)}, u32[]{:S(2)}) collective-permute-start(bf16[512,768]{1,0:T(8,128)(2,1)} %up_h), channel_id=1, source_target_pairs={{0,4},{4,0},{1,5},{5,1},{2,6},{6,2},{3,7},{7,3},{8,12},{12,8},{9,1... | collective-permute-start | bytes 2359304 | tf_op jit(solution)/shard_map/ppermute | solution.py:40
  28.8 10.5 %collective-permute-start.17 = (bf16[4,384,128]{2,1,0:T(8,128)(2,1)S(1)}, bf16[4,384,128]{2,1,0:T(8,128)(2,1)S(1)}, u32[]{:S(2)}, u32[]{:S(2)}) collective-permute-start(bf16[4,384,128]{2,1,0:T(8,128)(2,1)S(1)} %pad_maximum_fusion.1.rest_4_), channel_id=1, source_target_pairs={{0,64},{32,96},{64,0},{96,32},{1,65},{33,97},{65,1},{97,33},{2,66}... | collective-permute-start | bytes 1179656 | tf_op jit(solution)/shard_map/ppermute | solution.py:36
  39.3 13.8 %collective-permute-start.16 = (bf16[4,384,128]{2,1,0:T(8,128)(2,1)S(1)}, bf16[4,384,128]{2,1,0:T(8,128)(2,1)S(1)}, u32[]{:S(2)}, u32[]{:S(2)}) collective-permute-start(bf16[4,384,128]{2,1,0:T(8,128)(2,1)S(1)} %pad_maximum_fusion.1.rest_4_), channel_id=1, source_target_pairs={{0,32},{32,64},{64,96},{96,0},{1,33},{33,65},{65,97},{97,1},{2,34}... | collective-permute-start | bytes 1179656 | tf_op jit(solution)/shard_map/ppermute | solution.py:36
  43.9 9.3 %collective-permute-start.12 = (bf16[4,384,128]{2,1,0:T(8,128)(2,1)S(1)}, bf16[4,384,128]{2,1,0:T(8,128)(2,1)S(1)}, u32[]{:S(2)}, u32[]{:S(2)}) collective-permute-start(bf16[4,384,128]{2,1,0:T(8,128)(2,1)S(1)} %pad_maximum_fusion.rest_0_), channel_id=1, source_target_pairs={{0,24},{8,0},{16,8},{24,16},{1,25},{9,1},{17,9},{25,17},{2,26},{10... | collective-permute-start | bytes 1179656 | tf_op jit(solution)/shard_map/ppermute | solution.py:36
  45.1 10.8 %collective-permute-start.11 = (bf16[4,384,128]{2,1,0:T(8,128)(2,1)S(1)}, bf16[4,384,128]{2,1,0:T(8,128)(2,1)S(1)}, u32[]{:S(2)}, u32[]{:S(2)}) collective-permute-start(bf16[4,384,128]{2,1,0:T(8,128)(2,1)S(1)} %pad_maximum_fusion.rest_0_), channel_id=1, source_target_pairs={{0,16},{8,24},{16,0},{24,8},{1,17},{9,25},{17,1},{25,9},{2,18},{10... | collective-permute-start | bytes 1179656 | tf_op jit(solution)/shard_map/ppermute | solution.py:36
  45.1 20.5 %collective-permute-start.10 = (bf16[4,384,128]{2,1,0:T(8,128)(2,1)S(1)}, bf16[4,384,128]{2,1,0:T(8,128)(2,1)S(1)}, u32[]{:S(2)}, u32[]{:S(2)}) collective-permute-start(bf16[4,384,128]{2,1,0:T(8,128)(2,1)S(1)} %pad_maximum_fusion.rest_0_), channel_id=1, source_target_pairs={{0,8},{8,16},{16,24},{24,0},{1,9},{9,17},{17,25},{25,1},{2,10},{10... | collective-permute-start | bytes 1179656 | tf_op jit(solution)/shard_map/ppermute | solution.py:36
  53.1 29.5 %collective-permute-start.22 = (bf16[1,192,1024]{2,1,0:T(8,128)(2,1)S(1)}, bf16[1,192,1024]{2,1,0:T(8,128)(2,1)S(1)}, u32[]{:S(2)}, u32[]{:S(2)}) collective-permute-start(bf16[1,192,1024]{2,1,0:T(8,128)(2,1)S(1)} %get-tuple-element.68), channel_id=1, source_target_pairs={{0,32},{32,64},{64,96},{96,0},{1,33},{33,65},{65,97},{97,1},{2,34}... | collective-permute-start | bytes 1179656 | tf_op jit(solution)/shard_map/ppermute | solution.py:36
  53.2 31.3 %collective-permute-start.23 = (bf16[1,192,1024]{2,1,0:T(8,128)(2,1)S(1)}, bf16[1,192,1024]{2,1,0:T(8,128)(2,1)S(1)}, u32[]{:S(2)}, u32[]{:S(2)}) collective-permute-start(bf16[1,192,1024]{2,1,0:T(8,128)(2,1)S(1)} %get-tuple-element.69), channel_id=1, source_target_pairs={{0,96},{32,0},{64,32},{96,64},{1,97},{33,1},{65,33},{97,65},{2,98}... | collective-permute-start | bytes 1179656 | tf_op jit(solution)/shard_map/ppermute | solution.py:36
  78.8 47.3 %collective-permute-start.19 = (bf16[2,192,1024]{2,1,0:T(8,128)(2,1)S(1)}, bf16[2,192,1024]{2,1,0:T(8,128)(2,1)S(1)}, u32[]{:S(2)}, u32[]{:S(2)}) collective-permute-start(bf16[2,192,1024]{2,1,0:T(8,128)(2,1)S(1)} %get-tuple-element.64), channel_id=1, source_target_pairs={{0,32},{32,64},{64,96},{96,0},{1,33},{33,65},{65,97},{97,1},{2,34}... | collective-permute-start | bytes 2359304 | tf_op jit(solution)/shard_map/ppermute | solution.py:36
  78.9 47.2 %collective-permute-start.20 = (bf16[2,192,1024]{2,1,0:T(8,128)(2,1)S(1)}, bf16[2,192,1024]{2,1,0:T(8,128)(2,1)S(1)}, u32[]{:S(2)}, u32[]{:S(2)}) collective-permute-start(bf16[2,192,1024]{2,1,0:T(8,128)(2,1)S(1)} %get-tuple-element.65), channel_id=1, source_target_pairs={{0,96},{32,0},{64,32},{96,64},{1,97},{33,1},{65,33},{97,65},{2,98}... | collective-permute-start | bytes 2359304 | tf_op jit(solution)/shard_map/ppermute | solution.py:36
  81.5 45.7 %collective-permute-start.21 = (bf16[2,192,1024]{2,1,0:T(8,128)(2,1)S(1)}, bf16[2,192,1024]{2,1,0:T(8,128)(2,1)S(1)}, u32[]{:S(2)}, u32[]{:S(2)}) collective-permute-start(bf16[2,192,1024]{2,1,0:T(8,128)(2,1)S(1)} %get-tuple-element.66), channel_id=1, source_target_pairs={{0,64},{32,96},{64,0},{96,32},{1,65},{33,97},{65,1},{97,33},{2,66}... | collective-permute-start | bytes 2359304 | tf_op jit(solution)/shard_map/ppermute | solution.py:36
  82.6 40.8 %collective-permute-start.24 = (bf16[1,192,1024]{2,1,0:T(8,128)(2,1)S(1)}, bf16[1,192,1024]{2,1,0:T(8,128)(2,1)S(1)}, u32[]{:S(2)}, u32[]{:S(2)}) collective-permute-start(bf16[1,192,1024]{2,1,0:T(8,128)(2,1)S(1)} %get-tuple-element.70), channel_id=1, source_target_pairs={{0,64},{32,96},{64,0},{96,32},{1,65},{33,97},{65,1},{97,33},{2,66}... | collective-permute-start | bytes 1179656 | tf_op jit(solution)/shard_map/ppermute | solution.py:36
  84.5 38.9 %collective-permute-start.31 = (bf16[1,192,1024]{2,1,0:T(8,128)(2,1)S(1)}, bf16[1,192,1024]{2,1,0:T(8,128)(2,1)S(1)}, u32[]{:S(2)}, u32[]{:S(2)}) collective-permute-start(bf16[1,192,1024]{2,1,0:T(8,128)(2,1)S(1)} %get-tuple-element.80), channel_id=1, source_target_pairs={{0,8},{8,16},{16,24},{24,0},{1,9},{9,17},{17,25},{25,1},{2,10},{10... | collective-permute-start | bytes 1179656 | tf_op jit(solution)/shard_map/ppermute | solution.py:36
  123.4 53.7 %collective-permute-start.28 = (bf16[2,192,1024]{2,1,0:T(8,128)(2,1)S(1)}, bf16[2,192,1024]{2,1,0:T(8,128)(2,1)S(1)}, u32[]{:S(2)}, u32[]{:S(2)}) collective-permute-start(bf16[2,192,1024]{2,1,0:T(8,128)(2,1)S(1)} %get-tuple-element.76), channel_id=1, source_target_pairs={{0,8},{8,16},{16,24},{24,0},{1,9},{9,17},{17,25},{25,1},{2,10},{10... | collective-permute-start | bytes 2359304 | tf_op jit(solution)/shard_map/ppermute | solution.py:36
  123.4 54.8 %collective-permute-start.29 = (bf16[2,192,1024]{2,1,0:T(8,128)(2,1)S(1)}, bf16[2,192,1024]{2,1,0:T(8,128)(2,1)S(1)}, u32[]{:S(2)}, u32[]{:S(2)}) collective-permute-start(bf16[2,192,1024]{2,1,0:T(8,128)(2,1)S(1)} %get-tuple-element.77), channel_id=1, source_target_pairs={{0,24},{8,0},{16,8},{24,16},{1,25},{9,1},{17,9},{25,17},{2,26},{10... | collective-permute-start | bytes 2359304 | tf_op jit(solution)/shard_map/ppermute | solution.py:36
  126.1 52.1 %collective-permute-start.30 = (bf16[2,192,1024]{2,1,0:T(8,128)(2,1)S(1)}, bf16[2,192,1024]{2,1,0:T(8,128)(2,1)S(1)}, u32[]{:S(2)}, u32[]{:S(2)}) collective-permute-start(bf16[2,192,1024]{2,1,0:T(8,128)(2,1)S(1)} %get-tuple-element.78), channel_id=1, source_target_pairs={{0,16},{8,24},{16,0},{24,8},{1,17},{9,25},{17,1},{25,9},{2,18},{10... | collective-permute-start | bytes 2359304 | tf_op jit(solution)/shard_map/ppermute | solution.py:36
  126.1 40.9 %collective-permute-start.32 = (bf16[1,192,1024]{2,1,0:T(8,128)(2,1)S(1)}, bf16[1,192,1024]{2,1,0:T(8,128)(2,1)S(1)}, u32[]{:S(2)}, u32[]{:S(2)}) collective-permute-start(bf16[1,192,1024]{2,1,0:T(8,128)(2,1)S(1)} %get-tuple-element.81), channel_id=1, source_target_pairs={{0,24},{8,0},{16,8},{24,16},{1,25},{9,1},{17,9},{25,17},{2,26},{10... | collective-permute-start | bytes 1179656 | tf_op jit(solution)/shard_map/ppermute | solution.py:36
  127.3 39.7 %collective-permute-start.33 = (bf16[1,192,1024]{2,1,0:T(8,128)(2,1)S(1)}, bf16[1,192,1024]{2,1,0:T(8,128)(2,1)S(1)}, u32[]{:S(2)}, u32[]{:S(2)}) collective-permute-start(bf16[1,192,1024]{2,1,0:T(8,128)(2,1)S(1)} %get-tuple-element.82), channel_id=1, source_target_pairs={{0,16},{8,24},{16,0},{24,8},{1,17},{9,25},{17,1},{25,9},{2,18},{10... | collective-permute-start | bytes 1179656 | tf_op jit(solution)/shard_map/ppermute | solution.py:36
  167.0 15.1 %collective-permute-start.25 = (bf16[3,48,1024]{2,1,0:T(8,128)(2,1)S(1)}, bf16[3,48,1024]{2,1,0:T(8,128)(2,1)S(1)}, u32[]{:S(2)}, u32[]{:S(2)}) collective-permute-start(bf16[3,48,1024]{2,1,0:T(8,128)(2,1)S(1)} %get-tuple-element.72), channel_id=1, source_target_pairs={{0,8},{8,16},{16,24},{24,0},{1,9},{9,17},{17,25},{25,1},{2,10},{10... | collective-permute-start | bytes 884744 | tf_op jit(solution)/shard_map/ppermute | solution.py:36
  167.0 15.6 %collective-permute-start.26 = (bf16[3,48,1024]{2,1,0:T(8,128)(2,1)S(1)}, bf16[3,48,1024]{2,1,0:T(8,128)(2,1)S(1)}, u32[]{:S(2)}, u32[]{:S(2)}) collective-permute-start(bf16[3,48,1024]{2,1,0:T(8,128)(2,1)S(1)} %get-tuple-element.73), channel_id=1, source_target_pairs={{0,24},{8,0},{16,8},{24,16},{1,25},{9,1},{17,9},{25,17},{2,26},{10... | collective-permute-start | bytes 884744 | tf_op jit(solution)/shard_map/ppermute | solution.py:36
  177.0 8.0 %collective-permute-start.27 = (bf16[3,48,1024]{2,1,0:T(8,128)(2,1)S(1)}, bf16[3,48,1024]{2,1,0:T(8,128)(2,1)S(1)}, u32[]{:S(2)}, u32[]{:S(2)}) collective-permute-start(bf16[3,48,1024]{2,1,0:T(8,128)(2,1)S(1)} %get-tuple-element.74), channel_id=1, source_target_pairs={{0,16},{8,24},{16,0},{24,8},{1,17},{9,25},{17,1},{25,9},{2,18},{10... | collective-permute-start | bytes 884744 | tf_op jit(solution)/shard_map/ppermute | solution.py:36
  179.3 7.1 %collective-permute-start.34 = (bf16[3,48,1024]{2,1,0:T(8,128)(2,1)S(1)}, bf16[3,48,1024]{2,1,0:T(8,128)(2,1)S(1)}, u32[]{:S(2)}, u32[]{:S(2)}) collective-permute-start(bf16[3,48,1024]{2,1,0:T(8,128)(2,1)S(1)} %get-tuple-element.84), channel_id=1, source_target_pairs={{0,32},{32,64},{64,96},{96,0},{1,33},{33,65},{65,97},{97,1},{2,34}... | collective-permute-start | bytes 884744 | tf_op jit(solution)/shard_map/ppermute | solution.py:36
  180.0 9.2 %collective-permute-start.35 = (bf16[3,48,1024]{2,1,0:T(8,128)(2,1)S(1)}, bf16[3,48,1024]{2,1,0:T(8,128)(2,1)S(1)}, u32[]{:S(2)}, u32[]{:S(2)}) collective-permute-start(bf16[3,48,1024]{2,1,0:T(8,128)(2,1)S(1)} %get-tuple-element.85), channel_id=1, source_target_pairs={{0,96},{32,0},{64,32},{96,64},{1,97},{33,1},{65,33},{97,65},{2,98}... | collective-permute-start | bytes 884744 | tf_op jit(solution)/shard_map/ppermute | solution.py:36
  182.1 9.1 %collective-permute-start.36 = (bf16[3,48,1024]{2,1,0:T(8,128)(2,1)S(1)}, bf16[3,48,1024]{2,1,0:T(8,128)(2,1)S(1)}, u32[]{:S(2)}, u32[]{:S(2)}) collective-permute-start(bf16[3,48,1024]{2,1,0:T(8,128)(2,1)S(1)} %get-tuple-element.86), channel_id=1, source_target_pairs={{0,64},{32,96},{64,0},{96,32},{1,65},{33,97},{65,1},{97,33},{2,66}... | collective-permute-start | bytes 884744 | tf_op jit(solution)/shard_map/ppermute | solution.py:36
  192.1 6.0 %collective-permute-start.37 = (bf16[2,48,1024]{2,1,0:T(8,128)(2,1)S(1)}, bf16[2,48,1024]{2,1,0:T(8,128)(2,1)S(1)}, u32[]{:S(2)}, u32[]{:S(2)}) collective-permute-start(bf16[2,48,1024]{2,1,0:T(8,128)(2,1)S(1)} %get-tuple-element.88), channel_id=1, source_target_pairs={{0,1},{1,2},{2,3},{3,0},{4,5},{5,6},{6,7},{7,4},{8,9},{9,10},{10,1... | collective-permute-start | bytes 589832 | tf_op jit(solution)/shard_map/ppermute | solution.py:36
  193.5 6.3 %collective-permute-start.38 = (bf16[2,48,1024]{2,1,0:T(8,128)(2,1)S(1)}, bf16[2,48,1024]{2,1,0:T(8,128)(2,1)S(1)}, u32[]{:S(2)}, u32[]{:S(2)}) collective-permute-start(bf16[2,48,1024]{2,1,0:T(8,128)(2,1)S(1)} %get-tuple-element.89), channel_id=1, source_target_pairs={{0,3},{1,0},{2,1},{3,2},{4,7},{5,4},{6,5},{7,6},{8,11},{9,8},{10,9... | collective-permute-start | bytes 589832 | tf_op jit(solution)/shard_map/ppermute | solution.py:36
  195.1 6.3 %collective-permute-start.39 = (bf16[2,48,1024]{2,1,0:T(8,128)(2,1)S(1)}, bf16[2,48,1024]{2,1,0:T(8,128)(2,1)S(1)}, u32[]{:S(2)}, u32[]{:S(2)}) collective-permute-start(bf16[2,48,1024]{2,1,0:T(8,128)(2,1)S(1)} %get-tuple-element.90), channel_id=1, source_target_pairs={{0,2},{1,3},{2,0},{3,1},{4,6},{5,7},{6,4},{7,5},{8,10},{9,11},{10,... | collective-permute-start | bytes 589832 | tf_op jit(solution)/shard_map/ppermute | solution.py:36
  209.5 14.2 %collective-permute-start.45 = (bf16[4,48,1024]{2,1,0:T(8,128)(2,1)S(1)}, bf16[4,48,1024]{2,1,0:T(8,128)(2,1)S(1)}, u32[]{:S(2)}, u32[]{:S(2)}) collective-permute-start(bf16[4,48,1024]{2,1,0:T(8,128)(2,1)S(1)} %pad_maximum_fusion.2.rest_0_), channel_id=1, source_target_pairs={{0,96},{32,0},{64,32},{96,64},{1,97},{33,1},{65,33},{97,65},{2,98}... | collective-permute-start | bytes 1179656 | tf_op jit(solution)/shard_map/ppermute | solution.py:36
  210.5 6.8 %collective-permute-start.48 = (bf16[48,1024]{1,0:T(8,128)(2,1)S(1)}, bf16[48,1024]{1,0:T(8,128)(2,1)S(1)}, u32[]{:S(2)}, u32[]{:S(2)}) collective-permute-start(bf16[48,1024]{1,0:T(8,128)(2,1)S(1)} %get-tuple-element.94), channel_id=1, source_target_pairs={{0,96},{32,0},{64,32},{96,64},{1,97},{33,1},{65,33},{97,65},{2,98}... | collective-permute-start | bytes 294920 | tf_op jit(solution)/shard_map/ppermute | solution.py:36
  210.6 12.9 %collective-permute-start.47 = (bf16[48,1024]{1,0:T(8,128)(2,1)S(1)}, bf16[48,1024]{1,0:T(8,128)(2,1)S(1)}, u32[]{:S(2)}, u32[]{:S(2)}) collective-permute-start(bf16[48,1024]{1,0:T(8,128)(2,1)S(1)} %get-tuple-element.94), channel_id=1, source_target_pairs={{0,64},{32,96},{64,0},{96,32},{1,65},{33,97},{65,1},{97,33},{2,66}... | collective-permute-start | bytes 294920 | tf_op jit(solution)/shard_map/ppermute | solution.py:36
  212.8 10.6 %collective-permute-start.46 = (bf16[48,1024]{1,0:T(8,128)(2,1)S(1)}, bf16[48,1024]{1,0:T(8,128)(2,1)S(1)}, u32[]{:S(2)}, u32[]{:S(2)}) collective-permute-start(bf16[48,1024]{1,0:T(8,128)(2,1)S(1)} %get-tuple-element.94), channel_id=1, source_target_pairs={{0,32},{32,64},{64,96},{96,0},{1,33},{33,65},{65,97},{97,1},{2,34}... | collective-permute-start | bytes 294920 | tf_op jit(solution)/shard_map/ppermute | solution.py:36
  212.8 12.2 %collective-permute-start.44 = (bf16[4,48,1024]{2,1,0:T(8,128)(2,1)S(1)}, bf16[4,48,1024]{2,1,0:T(8,128)(2,1)S(1)}, u32[]{:S(2)}, u32[]{:S(2)}) collective-permute-start(bf16[4,48,1024]{2,1,0:T(8,128)(2,1)S(1)} %pad_maximum_fusion.2.rest_0_), channel_id=1, source_target_pairs={{0,64},{32,96},{64,0},{96,32},{1,65},{33,97},{65,1},{97,33},{2,66}... | collective-permute-start | bytes 1179656 | tf_op jit(solution)/shard_map/ppermute | solution.py:36
  217.2 12.8 %collective-permute-start.43 = (bf16[4,48,1024]{2,1,0:T(8,128)(2,1)S(1)}, bf16[4,48,1024]{2,1,0:T(8,128)(2,1)S(1)}, u32[]{:S(2)}, u32[]{:S(2)}) collective-permute-start(bf16[4,48,1024]{2,1,0:T(8,128)(2,1)S(1)} %pad_maximum_fusion.2.rest_0_), channel_id=1, source_target_pairs={{0,32},{32,64},{64,96},{96,0},{1,33},{33,65},{65,97},{97,1},{2,34}... | collective-permute-start | bytes 1179656 | tf_op jit(solution)/shard_map/ppermute | solution.py:36
  223.5 8.2 %collective-permute-start.51 = (bf16[4,48,1024]{2,1,0:T(8,128)(2,1)S(1)}, bf16[4,48,1024]{2,1,0:T(8,128)(2,1)S(1)}, u32[]{:S(2)}, u32[]{:S(2)}) collective-permute-start(bf16[4,48,1024]{2,1,0:T(8,128)(2,1)S(1)} %pad_maximum_fusion.3.rest_0_), channel_id=1, source_target_pairs={{0,24},{8,0},{16,8},{24,16},{1,25},{9,1},{17,9},{25,17},{2,26},{10... | collective-permute-start | bytes 1179656 | tf_op jit(solution)/shard_map/ppermute | solution.py:36
  223.6 8.5 %collective-permute-start.50 = (bf16[4,48,1024]{2,1,0:T(8,128)(2,1)S(1)}, bf16[4,48,1024]{2,1,0:T(8,128)(2,1)S(1)}, u32[]{:S(2)}, u32[]{:S(2)}) collective-permute-start(bf16[4,48,1024]{2,1,0:T(8,128)(2,1)S(1)} %pad_maximum_fusion.3.rest_0_), channel_id=1, source_target_pairs={{0,16},{8,24},{16,0},{24,8},{1,17},{9,25},{17,1},{25,9},{2,18},{10... | collective-permute-start | bytes 1179656 | tf_op jit(solution)/shard_map/ppermute | solution.py:36
  223.7 12.3 %collective-permute-start.49 = (bf16[4,48,1024]{2,1,0:T(8,128)(2,1)S(1)}, bf16[4,48,1024]{2,1,0:T(8,128)(2,1)S(1)}, u32[]{:S(2)}, u32[]{:S(2)}) collective-permute-start(bf16[4,48,1024]{2,1,0:T(8,128)(2,1)S(1)} %pad_maximum_fusion.3.rest_0_), channel_id=1, source_target_pairs={{0,8},{8,16},{16,24},{24,0},{1,9},{9,17},{17,25},{25,1},{2,10},{10... | collective-permute-start | bytes 1179656 | tf_op jit(solution)/shard_map/ppermute | solution.py:36
  242.8 13.3 %collective-permute-start.52 = (bf16[64,768]{1,0:T(8,128)(2,1)S(1)}, bf16[64,768]{1,0:T(8,128)(2,1)S(1)}, u32[]{:S(2)}, u32[]{:S(2)}) collective-permute-start(bf16[64,768]{1,0:T(8,128)(2,1)S(1)} %get-tuple-element.96), channel_id=1, source_target_pairs={{0,4},{4,0},{1,5},{5,1},{2,6},{6,2},{3,7},{7,3},{8,12},{12,8},{9,1... | collective-permute-start | bytes 294920 | tf_op jit(solution)/shard_map/ppermute | solution.py:40
  256.7 6.2 %collective-permute-start.55 = (bf16[2,64,768]{2,1,0:T(8,128)(2,1)S(1)}, bf16[2,64,768]{2,1,0:T(8,128)(2,1)S(1)}, u32[]{:S(2)}, u32[]{:S(2)}) collective-permute-start(bf16[2,64,768]{2,1,0:T(8,128)(2,1)S(1)} %shard_map.82.rest_0_), channel_id=1, source_target_pairs={{0,3},{1,0},{2,1},{3,2},{4,7},{5,4},{6,5},{7,6},{8,11},{9,8},{10,9... | collective-permute-start | bytes 589832 | tf_op jit(solution)/shard_map/ppermute | solution.py:36
  258.3 7.4 %collective-permute-start.54 = (bf16[2,64,768]{2,1,0:T(8,128)(2,1)S(1)}, bf16[2,64,768]{2,1,0:T(8,128)(2,1)S(1)}, u32[]{:S(2)}, u32[]{:S(2)}) collective-permute-start(bf16[2,64,768]{2,1,0:T(8,128)(2,1)S(1)} %shard_map.82.rest_0_), channel_id=1, source_target_pairs={{0,2},{1,3},{2,0},{3,1},{4,6},{5,7},{6,4},{7,5},{8,10},{9,11},{10,... | collective-permute-start | bytes 589832 | tf_op jit(solution)/shard_map/ppermute | solution.py:36
  259.4 11.5 %collective-permute-start.53 = (bf16[2,64,768]{2,1,0:T(8,128)(2,1)S(1)}, bf16[2,64,768]{2,1,0:T(8,128)(2,1)S(1)}, u32[]{:S(2)}, u32[]{:S(2)}) collective-permute-start(bf16[2,64,768]{2,1,0:T(8,128)(2,1)S(1)} %shard_map.82.rest_0_), channel_id=1, source_target_pairs={{0,1},{1,2},{2,3},{3,0},{4,5},{5,6},{6,7},{7,4},{8,9},{9,10},{10,1... | collective-permute-start | bytes 589832 | tf_op jit(solution)/shard_map/ppermute | solution.py:36
  (10 other events, 122.9 us)
